TPU v7x, 32 devices: a whole 2x2x4 slice. The times are simulated.
32 devices in a mesh: tile: 8 (over z, x), sub: 4 (over y, core).
Axes of the slice: x: 2, y: 2, z: 4, core: 2. Of those that a mesh axis runs over, the one named last changes fastest.
Arguments:
- grid_feats: bfloat16 [4096, 512], P(('tile', 'sub')), may hold values from -6 to 6
- mesh_feats: bfloat16 [4096, 512], P(('tile', 'sub')), may hold values from -6 to 6
- encode_edges: bfloat16 [32768, 512], P(('tile', 'sub')), may hold values from -6 to 6
- decode_edges: bfloat16 [16384, 512], P(('tile', 'sub')), may hold values from -6 to 6
- encode_source: int32 [32768], P(('tile', 'sub')), may hold values from 0 to 4095, as said below
- encode_target: int32 [32768], P(('tile', 'sub')), may hold values from -1 to 4095, as said below
- decode_source: int32 [16384], P(('tile', 'sub')), may hold values from 0 to 4095, as said below
- decode_target: int32 [16384], P(('tile', 'sub')), may hold values from -1 to 4095, as said below
- owner_fine: int32 [4096], P(('tile', 'sub')), may hold values from 0 to 1023, as said below
- owner_coarse: int32 [1024], P('tile'), may hold values from 0 to 511
- encode_weight: bfloat16 [512, 512], replicated, may hold values from -0.25 to 0.25
- decode_weight: bfloat16 [512, 512], replicated, may hold values from -0.25 to 0.25
- middle_weight: bfloat16 [512, 512], replicated, may hold values from -0.25 to 0.25
- summit_weight: bfloat16 [512, 512], replicated, may hold values from -0.25 to 0.25
- cotangent: bfloat16 [4096, 512], P(('tile', 'sub')), may hold values from -6 to 6
Outputs:
- grid_update: bfloat16 [4096, 512], P(('tile', 'sub'))
- encode_grad: float32 [512, 512], replicated
- decode_grad: float32 [512, 512], replicated
- middle_grad: float32 [512, 512], replicated
- summit_grad: float32 [512, 512], replicated
Inputs may be any that keep to these rules, and one draw needn't show every extreme that they name: `encode_source`: edge slot e is listed on device d = e // 1024; its source grid node lies on device d - 1, d or d + 1. `encode_target`: -1 marks padding; every other value is a mesh node of the device that lists the slot. On each device padding fills whole blocks of 128 slots after all live ones; every device has a live block, and some device has no padding. `decode_source`: edge slot e is listed on device d = e // 512; its source mesh node lies on device d - 1, d or d + 1. `decode_target`: -1 marks padding; every other value is a grid node of the device that lists the slot. On each device padding fills whole blocks of 128 slots after all live ones; every device has a live block, and some device has no padding. `owner_fine`: the middle node of fine mesh node m lies on the tile of the device that holds m.
All inputs are finite; a program needn't handle non-finite values.
Results may differ from a plain program's by a relative error of at most 0.012.
Values may be sent and summed in bfloat16 or wider, within the bound.
No kernel may reach another device: no remote copies, remote signals or barrier semaphores. Data moves between devices by JAX's collectives and lax.ppermute only.
A program may use at most 64 MiB of HBM per device.

v0:
```python
import jax
import jax.numpy as jnp
from jax import lax
from jax.sharding import PartitionSpec as P

TOP_NODES = 512
BLOCK = 128


def extended(x, sides, width):
    for axis, dim in sides:
        peers, length = (lax.axis_size(axis), x.shape[dim])
        up = [(i, (i + 1) % peers) for i in range(peers - 1)]
        down = [(j, i) for i, j in up]
        last = lax.slice_in_dim(x, length - width, length, axis=dim)
        initial = lax.slice_in_dim(x, 0, width, axis=dim)
        before = lax.ppermute(last, axis, up)
        after = lax.ppermute(initial, axis, down)
        x = jnp.concatenate([before, x, after], axis=dim)
    return x


def from_behind(x, axis, by):
    peers = lax.axis_size(axis)
    pairs = [(i, i + by) for i in range(peers) if 0 <= i + by < peers]
    return lax.ppermute(x, axis, pairs)


def silu_slope(values):
    sigmoid = jax.nn.sigmoid(values)
    return sigmoid * (1.0 + values * (1.0 - sigmoid))


def live_count(targets):
    heads = targets.reshape(-1, BLOCK)[:, 0]
    return jnp.sum((heads >= 0).astype(jnp.int32))


def local_targets(targets, first, limit):
    return jnp.where(targets >= 0, targets - first, limit)


def outer_sum(left, right):
    return lax.dot_general(
        left, right, (((0,), (0,)), ((), ())), preferred_element_type=jnp.float32
    )


def times_transposed(left, right):
    return lax.dot_general(
        left, right, (((1,), (1,)), ((), ())), preferred_element_type=jnp.float32
    )


def membership(indices, rows, dtype):
    return (jnp.arange(rows, dtype=jnp.int32)[:, None] == indices[None, :]).astype(dtype)


def exact_sum(members, values):
    return jnp.dot(
        members, values, precision=lax.Precision.HIGHEST, preferred_element_type=jnp.float32
    )


def edge_forward(sources, senders, targets, edge_feats, weight, segments, blocks):
    features = weight.shape[1]

    def block_step(block_id, carried):
        summed, stored = carried
        offset = block_id * BLOCK
        picked = lax.dynamic_slice_in_dim(senders, offset, BLOCK)
        receivers = lax.dynamic_slice_in_dim(targets, offset, BLOCK)
        edge_part = lax.dynamic_slice_in_dim(edge_feats, offset, BLOCK, 0)
        fetched = jnp.take(sources, picked, axis=0)
        preact = jnp.dot(fetched, weight, preferred_element_type=jnp.float32) + edge_part.astype(
            jnp.float32
        )
        summed = summed + exact_sum(
            membership(receivers, segments, jnp.float32), jax.nn.silu(preact)
        )
        stored = lax.dynamic_update_slice_in_dim(stored, preact, offset, 0)
        return (summed, stored)

    start_sum = jnp.zeros((segments, features), jnp.float32)
    start_store = jnp.zeros((senders.shape[0], features), jnp.float32)
    return lax.fori_loop(0, blocks, block_step, (start_sum, start_store))


def edge_backward(
    sources, senders, targets, stored, weight, upstream, factor, blocks, returned_rows
):
    features = weight.shape[1]

    def block_step(block_id, carried):
        gradient, returned = carried
        offset = block_id * BLOCK
        picked = lax.dynamic_slice_in_dim(senders, offset, BLOCK)
        receivers = lax.dynamic_slice_in_dim(targets, offset, BLOCK)
        preact = lax.dynamic_slice_in_dim(stored, offset, BLOCK, 0)
        fetched = jnp.take(sources, picked, axis=0)
        incoming = jnp.take(upstream, receivers, axis=0).astype(jnp.float32) * factor
        slope = (incoming * silu_slope(preact)).astype(jnp.bfloat16)
        gradient = gradient + outer_sum(fetched, slope)
        if returned_rows:
            passed = times_transposed(slope, weight)
            returned = returned + exact_sum(membership(picked, returned_rows, jnp.float32), passed)
        return (gradient, returned)

    start_grad = jnp.zeros((features, features), jnp.float32)
    start_back = jnp.zeros((max(returned_rows, 1), features), jnp.float32)
    return lax.fori_loop(0, blocks, block_step, (start_grad, start_back))


def shards(
    grid_feats,
    mesh_feats,
    encode_edges,
    decode_edges,
    encode_source,
    encode_target,
    decode_source,
    decode_target,
    owner_fine,
    owner_coarse,
    encode_weight,
    decode_weight,
    middle_weight,
    summit_weight,
    cotangent,
):
    grid_rows = grid_feats.shape[0]
    mesh_rows = mesh_feats.shape[0]
    level_rows = owner_coarse.shape[0]
    tiles = lax.axis_size("tile")
    subs = lax.axis_size("sub")
    device = lax.axis_index(("tile", "sub"))
    tile_id = lax.axis_index("tile")
    encode_factor = mesh_rows / encode_source.shape[0]
    decode_factor = grid_rows / decode_source.shape[0]
    middle_factor = level_rows / (mesh_rows * subs)
    summit_factor = TOP_NODES / (level_rows * tiles)
    grid_wide = extended(grid_feats, ((("tile", "sub"), 0),), grid_rows)
    encode_senders = encode_source - (device - 1) * grid_rows
    encode_targets = local_targets(encode_target, device * mesh_rows, mesh_rows)
    encode_blocks = live_count(encode_target)
    encode_summed, encode_stored = edge_forward(
        grid_wide,
        encode_senders,
        encode_targets,
        encode_edges,
        encode_weight,
        mesh_rows,
        encode_blocks,
    )
    mesh_mid = (mesh_feats.astype(jnp.float32) + encode_factor * encode_summed).astype(jnp.bfloat16)
    fine_local = owner_fine - tile_id * level_rows
    fine_members = membership(fine_local, level_rows, jnp.bfloat16)
    middle_part = jnp.dot(fine_members, mesh_mid, preferred_element_type=jnp.float32)
    middle_sum = lax.psum(middle_part, "sub")
    middle_in = (middle_factor * middle_sum).astype(jnp.bfloat16)
    middle_act = jnp.dot(middle_in, middle_weight, preferred_element_type=jnp.float32)
    middle_out = (middle_in.astype(jnp.float32) + jax.nn.silu(middle_act)).astype(jnp.bfloat16)
    top_members = membership(owner_coarse, TOP_NODES, jnp.bfloat16)
    summit_part = jnp.dot(top_members, middle_out, preferred_element_type=jnp.float32)
    summit_whole = lax.psum(summit_part, "tile")
    summit_in = (summit_factor * summit_whole).astype(jnp.bfloat16)
    summit_act = jnp.dot(summit_in, summit_weight, preferred_element_type=jnp.float32)
    summit_out = jax.nn.silu(summit_act).astype(jnp.bfloat16)
    coarse_of = jnp.take(owner_coarse, fine_local)
    lifted = jnp.take(middle_out, fine_local, axis=0).astype(jnp.float32) + jnp.take(
        summit_out, coarse_of, axis=0
    ).astype(jnp.float32)
    mesh_out = (mesh_mid.astype(jnp.float32) + lifted).astype(jnp.bfloat16)
    mesh_wide = extended(mesh_out, ((("tile", "sub"), 0),), mesh_rows)
    decode_senders = decode_source - (device - 1) * mesh_rows
    decode_targets = local_targets(decode_target, device * grid_rows, grid_rows)
    decode_blocks = live_count(decode_target)
    decode_summed, decode_stored = edge_forward(
        mesh_wide,
        decode_senders,
        decode_targets,
        decode_edges,
        decode_weight,
        grid_rows,
        decode_blocks,
    )
    grid_update = (grid_feats.astype(jnp.float32) + decode_factor * decode_summed).astype(
        jnp.bfloat16
    )
    decode_local, decode_returned = edge_backward(
        mesh_wide,
        decode_senders,
        decode_targets,
        decode_stored,
        decode_weight,
        cotangent,
        decode_factor,
        decode_blocks,
        3 * mesh_rows,
    )
    from_next = from_behind(decode_returned[:mesh_rows], ("tile", "sub"), -1)
    from_prev = from_behind(decode_returned[2 * mesh_rows :], ("tile", "sub"), 1)
    mesh_grad = decode_returned[mesh_rows : 2 * mesh_rows] + from_next + from_prev
    level_part = exact_sum(fine_members.astype(jnp.float32), mesh_grad)
    level_grad = lax.psum(level_part, "sub")
    summit_grad_part = exact_sum(top_members.astype(jnp.float32), level_grad)
    summit_grad_whole = lax.psum(summit_grad_part, "tile")
    summit_slope = (summit_grad_whole * silu_slope(summit_act)).astype(jnp.bfloat16)
    summit_local = outer_sum(summit_in, summit_slope)
    summit_back = times_transposed(summit_slope, summit_weight).astype(jnp.bfloat16)
    level_total = level_grad + summit_factor * jnp.take(summit_back, owner_coarse, axis=0).astype(
        jnp.float32
    )
    middle_slope = (level_total * silu_slope(middle_act)).astype(jnp.bfloat16)
    middle_local = outer_sum(middle_in, middle_slope)
    middle_back = level_total + times_transposed(middle_slope, middle_weight)
    mesh_total = mesh_grad + middle_factor * jnp.take(middle_back, fine_local, axis=0)
    encode_local, unused_rows = edge_backward(
        grid_wide,
        encode_senders,
        encode_targets,
        encode_stored,
        encode_weight,
        mesh_total,
        encode_factor,
        encode_blocks,
        0,
    )
    sub_share = 1.0 / subs
    encode_grad, decode_grad, middle_grad = lax.psum(
        (encode_local, decode_local, sub_share * middle_local), ("tile", "sub")
    )
    return (grid_update, encode_grad, decode_grad, middle_grad, summit_local)


def solution(mesh):
    placed = (
        P(("tile", "sub"), None),
        P(("tile", "sub"), None),
        P(("tile", "sub"), None),
        P(("tile", "sub"), None),
        P(("tile", "sub")),
        P(("tile", "sub")),
        P(("tile", "sub")),
        P(("tile", "sub")),
        P(("tile", "sub")),
        P("tile"),
        P(),
        P(),
        P(),
        P(),
        P(("tile", "sub"), None),
    )
    return jax.shard_map(
        shards,
        mesh=mesh,
        in_specs=placed,
        out_specs=(P(("tile", "sub"), None), P(), P(), P(), P()),
        check_vma=False,
    )
```

profile of v0, /device:TPU:0, one launch (start us, length us, event | category | flops | bytes accessed | tf_op | source)
XLA Modules:
  0.0 562.8 jit_solution(5614955575473783883)
XLA Ops:
  7.2 2.5 collective-permute-start
  9.8 1.3 collective-permute-start.1
  12.5 1.3 convert_reduce_fusion
  15.4 1.6 broadcast_in_dim.93
  17.0 24.1 %while.46 = (s32[]{:T(128)}, f32[128,512]{1,0:T(8,128)S(1)}, f32[1024,512]{1,0:T(8,128)}, s32[]{:T(128)}, s32[1024]{0:T(1024)S(1)}, /*index=5*/s32[1024]{0:T(102...) while((s32[]{:T(128)}, f32[128,512]{1,0:T(8,128)S(1)}, ...), condition=%wide.region_3.5_spmd, body=%wide.region_2.0_spmd.sunk | while | flops 168314624 | bytes 2367415 | solution.py:86
  18.6 1.9 constant_dynamic-update-slice_fusion.7
  22.5 1.9 constant_dynamic-update-slice_fusion.7
  26.5 1.9 constant_dynamic-update-slice_fusion.7
  30.4 1.9 constant_dynamic-update-slice_fusion.7
  34.3 1.9 constant_dynamic-update-slice_fusion.7
  38.2 1.9 constant_dynamic-update-slice_fusion.7
  42.2 43.7 %all-reduce.7.cloned.1.call-done = f32[128,512]{1,0:T(8,128)} async-done(((f32[128,512]{1,0:T(8,128)}), f32[128,512]{1,0:T(8,128)}) %all-reduce.7.cloned.1.call-update) | async-done | bytes 262160 | tf_op jit(solution)/shard_map/psum | solution.py:159
  85.9 2.0 add_convert_fusion.2
  87.9 1.3 fusion.43
  91.4 76.8 %all-reduce.9.cloned.1.call-done = f32[512,512]{1,0:T(8,128)} async-done(((f32[512,512]{1,0:T(8,128)}), f32[512,512]{1,0:T(8,128)}) %all-reduce.9.cloned.1.call-update) | async-done | bytes 1048592 | tf_op jit(solution)/shard_map/psum | solution.py:165
  168.2 2.7 multiply_convert_fusion.6
  171.9 1.7 collective-permute-start.2
  173.6 1.3 collective-permute-start.3
  176.2 2.0 collective-permute-done.3
  179.1 13.2 %while.47 = (s32[]{:T(128)}, f32[128,512]{1,0:T(8,128)}, f32[512,512]{1,0:T(8,128)S(1)}, s32[]{:T(128)}, s32[512]{0:T(512)}, /*index=5*/s32[512]{0:T(512)}, bf16...) while((s32[]{:T(128)}, f32[128,512]{1,0:T(8,128)}, ...), condition=%wide.region_7.10_spmd, body=%wide.region_6.9_spmd.sunk | while | flops 168314624 | bytes 2367799 | solution.py:86
  183.4 2.0 convolution_add_fusion.14
  189.6 2.0 convolution_add_fusion.14
  193.5 15.0 %while.48 = (s32[]{:T(128)}, f32[512,512]{1,0:T(8,128)S(1)}, f32[384,512]{1,0:T(8,128)S(1)}, s32[]{:T(128)}, s32[512]{0:T(512)}, /*index=5*/bf16[384,512]{1,0:T(...) while((s32[]{:T(128)}, f32[512,512]{1,0:T(8,128)S(1)}, ...), condition=%wide.region_9.12_spmd, body=%wide.region_8.11_spmd.sunk | while | flops 438357888 | bytes 8272603 | solution.py:111
  194.2 1.4 compare_and_fusion.16
  197.3 1.5 convolution_add_fusion.15
  198.8 1.3 fusion.84
  201.4 1.4 compare_and_fusion.16
  204.5 1.5 convolution_add_fusion.15
  206.0 1.3 fusion.84
  208.6 1.3 collective-permute-start.4
  209.9 19.5 %collective-permute-start.5 = (f32[128,512]{1,0:T(8,128)S(1)}, f32[128,512]{1,0:T(8,128)S(1)}, u32[]{:S(2)}, u32[]{:S(2)}) collective-permute-start(f32[128,512]{1,0:T(8,128)S(1)} %get-tuple-element.310), channel_id=1, source_target_pairs={{0,1},{1,2},{2,3},{3,4},{4,5},{5,6},{6,7},{7,8},{8,9},{9,10},{10,1... | collective-permute-start | bytes 786440 | tf_op jit(solution)/shard_map/ppermute | solution.py:26
  230.6 1.6 fusion.48
  232.3 53.1 %all-reduce.11.cloned.1.call-done = f32[128,512]{1,0:T(8,128)} async-done(((f32[128,512]{1,0:T(8,128)}), f32[128,512]{1,0:T(8,128)}) %all-reduce.11.cloned.1.call-update) | async-done | bytes 262160 | tf_op jit(solution)/shard_map/psum | solution.py:205
  285.4 2.5 fusion.42
  288.0 79.6 %all-reduce.13.cloned.1.call-done = f32[512,512]{1,0:T(8,128)} async-done(((f32[512,512]{1,0:T(8,128)}), f32[512,512]{1,0:T(8,128)}) %all-reduce.13.cloned.1.call-update) | async-done | bytes 1048592 | tf_op jit(solution)/shard_map/psum | solution.py:207
  367.6 1.9 multiply_convert_fusion.5
  370.9 1.6 convolution_add_fusion.7
  374.6 27.5 %while.49 = (s32[]{:T(128)}, f32[512,512]{1,0:T(8,128)S(1)}, s32[]{:T(128)}, s32[1024]{0:T(1024)}, bf16[384,512]{1,0:T(8,128)(2,1)S(1)}, /*index=5*/s32[1024]{0:...) while((s32[]{:T(128)}, f32[512,512]{1,0:T(8,128)S(1)}, ...), condition=%wide.region_13.16_spmd, body=%wide.region_12.15_spmd.sunk | while | flops 68161032 | bytes 3551915 | solution.py:111
  377.6 1.5 convolution_add_fusion.17
  382.1 1.5 convolution_add_fusion.17
  386.6 1.5 convolution_add_fusion.17
  391.1 1.5 convolution_add_fusion.17
  395.6 1.5 convolution_add_fusion.17
  400.1 1.5 convolution_add_fusion.17
  402.2 2.8 convolution_multiply_fusion
  406.7 2.7 fusion.44
  409.4 142.5 %all-reduce.15.cloned.1.call-done = (f32[512,512]{1,0:T(8,128)}, f32[512,512]{1,0:T(8,128)}, f32[512,512]{1,0:T(8,128)}) async-done(((f32[512,512]{1,0:T(8,128)}, f32[512,512]{1,0:T(8,128)}, f32[512,512]{1,0:T(8,128)}), (f32[512,512]{1,0:T(8,128)}, f32[512,512]{1,0:T(8,128)}, f32[512,512]{1,0:T(8,128)})) %all-reduce.15.cloned.1.call-update) | async-done | bytes 3145744 | tf_op jit(solution)/shard_map/psum | solution.py:230
  551.9 2.4 copy.68
  (186 shorter events, 53.3 us)
Async XLA Ops:
  7.2 161.1 %copy-start = (bf16[512,512]{1,0:T(8,128)(2,1)S(1)}, bf16[512,512]{1,0:T(8,128)(2,1)}, u32[]{:S(2)}) copy-start(bf16[512,512]{1,0:T(8,128)(2,1)} %param.40) | copy-start | bytes 1572868
  7.2 9.8 %copy-start.5 = (bf16[512,512]{1,0:T(8,128)(2,1)S(1)}, bf16[512,512]{1,0:T(8,128)(2,1)}, u32[]{:S(2)}) copy-start(bf16[512,512]{1,0:T(8,128)(2,1)} %param.37) | copy-start | bytes 1572868
  7.2 78.7 %all-reduce.7.cloned.1.call-start = ((), (), s32[]{:S(2)}) async-start(), calls=%async_computation | async-start | bytes 524288 | tf_op jit(solution)/shard_map/psum | solution.py:159
  7.2 6.5 %collective-permute-start = (bf16[128,512]{1,0:T(8,128)(2,1)}, bf16[128,512]{1,0:T(8,128)(2,1)S(1)}, u32[]{:S(2)}, u32[]{:S(2)}) collective-permute-start(bf16[128,512]{1,0:T(8,128)(2,1)} %param.27), channel_id=1, source_target_pairs={{0,1},{1,2},{2,3},{3,4},{4,5},{5,6},{6,7},{7,8},{8,9},{9,10},{10,1... | collective-permute-start | bytes 393224 | tf_op jit(solution)/shard_map/ppermute | solution.py:17
  9.8 5.6 collective-permute-start.1
  12.5 78.0 %copy-start.21 = (s32[128]{0:T(128)}, s32[128]{0:T(128)S(1)}, u32[]{:S(2)}) copy-start(s32[128]{0:T(128)S(1)} %get-tuple-element.300) | copy-start | bytes 1540
  17.0 24.2 %copy-start.14 = (bf16[128,512]{1,0:T(8,128)(2,1)S(1)}, bf16[128,512]{1,0:T(8,128)(2,1)}, u32[]{:S(2)}) copy-start(bf16[128,512]{1,0:T(8,128)(2,1)} %param.28) | copy-start | bytes 393220
  17.0 68.8 %copy-start.26 = (bf16[512,512]{1,0:T(8,128)(2,1)S(1)}, bf16[512,512]{1,0:T(8,128)(2,1)}, u32[]{:S(2)}) copy-start(bf16[512,512]{1,0:T(8,128)(2,1)} %param.39) | copy-start | bytes 1572868
  41.2 48.0 %copy-start.18 = (s32[1024]{0:T(1024)}, s32[1024]{0:T(1024)S(1)}, u32[]{:S(2)}) copy-start(s32[1024]{0:T(1024)S(1)} %get-tuple-element.780) | copy-start | bytes 12292
  41.2 48.0 %copy-start.19 = (s32[1024]{0:T(1024)}, s32[1024]{0:T(1024)S(1)}, u32[]{:S(2)}) copy-start(s32[1024]{0:T(1024)S(1)} %get-tuple-element.781) | copy-start | bytes 12292
  41.2 46.7 %copy-start.1 = (s32[128]{0:T(128)S(1)}, s32[128]{0:T(128)}, u32[]{:S(2)}) copy-start(s32[128]{0:T(128)} %param.36) | copy-start | bytes 1540
  42.1 126.1 %all-reduce.9.cloned.1.call-start = ((), (), s32[]{:S(2)}) async-start(), calls=%async_computation.1 | async-start | bytes 2097152 | tf_op jit(solution)/shard_map/psum | solution.py:165
  89.2 196.2 %all-reduce.11.cloned.1.call-start = ((), (), s32[]{:S(2)}) async-start(), calls=%async_computation.2 | async-start | bytes 524288 | tf_op jit(solution)/shard_map/psum | solution.py:205
  89.2 2.1 copy-start.22
  90.5 81.3 %copy-start.23 = (pred[128]{0:T(512)(128)(4,1)}, pred[128]{0:T(512)(128)(4,1)S(1)}, u32[]{:S(2)}) copy-start(pred[128]{0:T(512)(128)(4,1)S(1)} %get-tuple-element.298) | copy-start | bytes 388
  91.4 83.6 %copy-start.20 = (s32[512]{0:T(512)S(1)}, s32[512]{0:T(512)}, u32[]{:S(2)}) copy-start(s32[512]{0:T(512)} %param.34) | copy-start | bytes 6148
  91.4 83.6 %copy-start.25 = (s32[512]{0:T(512)S(1)}, s32[512]{0:T(512)}, u32[]{:S(2)}) copy-start(s32[512]{0:T(512)} %param.33) | copy-start | bytes 6148
  170.9 8.2 %copy-start.6 = (bf16[512,512]{1,0:T(8,128)(2,1)S(1)}, bf16[512,512]{1,0:T(8,128)(2,1)}, u32[]{:S(2)}) copy-start(bf16[512,512]{1,0:T(8,128)(2,1)} %param.38) | copy-start | bytes 1572868
  171.9 4.2 collective-permute-start.2
  173.6 4.6 collective-permute-start.3
  179.1 14.4 %copy-start.2 = (bf16[128,512]{1,0:T(8,128)(2,1)S(1)}, bf16[128,512]{1,0:T(8,128)(2,1)}, u32[]{:S(2)}) copy-start(bf16[128,512]{1,0:T(8,128)(2,1)} %param.41) | copy-start | bytes 393220
  192.3 1.0 copy-start.8
  197.3 1.5 copy-start.7
  204.5 1.5 copy-start.7
  208.5 79.4 %copy-start.3 = (f32[512,512]{1,0:T(8,128)}, f32[512,512]{1,0:T(8,128)S(1)}, u32[]{:S(2)}) copy-start(f32[512,512]{1,0:T(8,128)S(1)} %get-tuple-element.208) | copy-start | bytes 3145732
  208.6 20.9 %collective-permute-start.4 = (f32[128,512]{1,0:T(8,128)S(1)}, f32[128,512]{1,0:T(8,128)S(1)}, u32[]{:S(2)}, u32[]{:S(2)}) collective-permute-start(f32[128,512]{1,0:T(8,128)S(1)} %get-tuple-element.309), channel_id=1, source_target_pairs={{1,0},{2,1},{3,2},{4,3},{5,4},{6,5},{7,6},{8,7},{9,8},{10,9},{11,1... | collective-permute-start | bytes 786440 | tf_op jit(solution)/shard_map/ppermute | solution.py:26
  209.9 20.7 %collective-permute-start.5 = (f32[128,512]{1,0:T(8,128)S(1)}, f32[128,512]{1,0:T(8,128)S(1)}, u32[]{:S(2)}, u32[]{:S(2)}) collective-permute-start(f32[128,512]{1,0:T(8,128)S(1)} %get-tuple-element.310), channel_id=1, source_target_pairs={{0,1},{1,2},{2,3},{3,4},{4,5},{5,6},{6,7},{7,8},{8,9},{9,10},{10,1... | collective-permute-start | bytes 786440 | tf_op jit(solution)/shard_map/ppermute | solution.py:26
  230.6 138.9 %copy-start.11 = (f32[128,512]{1,0:T(8,128)}, f32[128,512]{1,0:T(8,128)S(1)}, u32[]{:S(2)}) copy-start(f32[128,512]{1,0:T(8,128)S(1)} %collective-permute-done.5) | copy-start | bytes 786436
  232.2 135.3 %all-reduce.13.cloned.1.call-start = ((), (), s32[]{:S(2)}) async-start(), calls=%async_computation.3 | async-start | bytes 2097152 | tf_op jit(solution)/shard_map/psum | solution.py:207
  287.9 264.0 %all-reduce.15.cloned.1.call-start = ((), (), s32[]{:S(2)}) async-start(), calls=%async_computation.4 | async-start | bytes 6291456 | tf_op jit(solution)/shard_map/psum | solution.py:230
  370.8 2.5 copy-start.16
  370.8 2.5 copy-start.24
  374.6 27.6 %copy-start.15 = (f32[128,512]{1,0:T(8,128)S(1)}, f32[128,512]{1,0:T(8,128)}, u32[]{:S(2)}) copy-start(f32[128,512]{1,0:T(8,128)} %all-reduce.11.cloned.1.call-done) | copy-start | bytes 786436
  374.6 27.6 %copy-start.17 = (bf16[128,512]{1,0:T(8,128)(2,1)S(1)}, bf16[128,512]{1,0:T(8,128)(2,1)}, u32[]{:S(2)}) copy-start(bf16[128,512]{1,0:T(8,128)(2,1)} %copy-done.16) | copy-start | bytes 393220
  402.2 2.8 copy-start.4
  405.0 0.9 copy-start.12
  405.0 1.0 copy-start.13
  551.9 2.4 copy-start.10
  551.9 3.4 copy-start.9
Sparse Core Ops, SparseCore 0:
  42.3 43.5 all-reduce.6
  89.9 78.2 all-reduce.8
  232.4 52.9 all-reduce.10
  289.3 78.2 all-reduce.12
  405.1 146.6 all-reduce.14
where the time goes:
time: 565 us; the launch traced here: 563 us
  waiting for transfers between devices  400 us (71%)
  matrix products  54.6 us (10%)
  local copies, waits for them, and re-layouts  36.6 us (6%)
  starting transfers between devices  27.9 us (5%)
  other arithmetic  17.2 us (3%)
  between operations  14.3 us (3%)
  loops' own time  12.6 us (2%)
    psum x1, waiting for transfers between devices, shards(): lax.psum((encode_local, decode_local, sub_share * middle_local), ('tile',...  143 us
    psum x1, waiting for transfers between devices, shards(): summit_grad_whole = lax.psum(summit_grad_part, 'tile')  79.6 us
    psum x1, waiting for transfers between devices, shards(): summit_whole = lax.psum(summit_part, 'tile')  76.8 us
    psum x1, waiting for transfers between devices, shards(): level_grad = lax.psum(level_part, 'sub')  53.1 us
    psum x1, waiting for transfers between devices, shards(): middle_sum = lax.psum(middle_part, 'sub')  43.7 us
    ppermute x2, starting transfers between devices, from_behind(): return lax.ppermute(x, axis, pairs)  20.8 us
    dot_general x10, matrix products, outer_sum(): lax.dot_general(left, right, (((0,), (0,)), ((), ())), preferred_element_...  17.5 us
    dot_general x8, matrix products, block_step(): jnp.dot(fetched, weight, preferred_element_type=jnp.float32)  13.8 us
  transfers between devices with their start and end apart: 11, of which 8 were waited for; matrix products, arithmetic and copies ran while one was open for 2% of the time, Pallas kernels for 0%

commit v1 on v0

v1 whole, which is shorter than its diff:
```python
import functools

import jax
import jax.numpy as jnp
from jax import lax
from jax.experimental import pallas as pl
from jax.experimental.pallas import tpu as pltpu
from jax.sharding import Mesh, PartitionSpec as P

TOP_NODES = 512
ALL = ("tile", "row", "core")
CHIPS = ("tile", "row")
BF16 = jnp.bfloat16
F32 = jnp.float32
I32 = jnp.int32


def mm(left, right):
    return jnp.dot(left, right, preferred_element_type=F32)


def mm_tn(left, right):
    return lax.dot_general(left, right, (((0,), (0,)), ((), ())), preferred_element_type=F32)


def mm_nt(left, right):
    return lax.dot_general(left, right, (((1,), (1,)), ((), ())), preferred_element_type=F32)


def sigmoid(values):
    return 0.5 + 0.5 * jnp.tanh(0.5 * values)


def rows_onehot(ids, rows):
    n = ids.shape[1]
    hit = lax.broadcasted_iota(I32, (rows, n), 0) == ids
    return jnp.where(hit, 1.0, 0.0).astype(BF16)


def column(ids):
    n = ids.shape[1]
    wide = jnp.broadcast_to(ids.astype(F32), (8, n))
    return wide.T[:, :1].astype(I32)


def cols_onehot(ids, cols):
    n = ids.shape[1]
    hit = lax.broadcasted_iota(I32, (n, cols), 1) == column(ids)
    return jnp.where(hit, 1.0, 0.0).astype(BF16)


def slots(source, device, core, rows):
    rel = source - device * rows
    before = rel < 0
    after = rel >= rows
    shift_before = jnp.where(core == 0, 3 * rows, 2 * rows)
    shift_after = jnp.where(core == 0, 0, rows)
    return rel + jnp.where(before, shift_before, 0) + jnp.where(after, shift_after, 0)


def encode_kernel(
    dev_ref,
    grid_ref,
    partner_ref,
    far_ref,
    mesh_ref,
    edges_ref,
    source_ref,
    target_ref,
    fine_ref,
    weight_ref,
    fetched_ref,
    slope_ref,
    core_ref,
    farpkt_ref,
    keep_ref,
    *,
    subs,
    level_rows,
    factor,
):
    device = dev_ref[0]
    core = device % 2
    rows = grid_ref.shape[0]
    mesh_rows = mesh_ref.shape[0]
    half = level_rows // 2
    picks = cols_onehot(slots(source_ref[...], device, core, rows), 3 * rows)
    fetched = (
        mm(picks[:, :rows], grid_ref[...])
        + mm(picks[:, rows : 2 * rows], partner_ref[...])
        + mm(picks[:, 2 * rows :], far_ref[...])
    ).astype(BF16)
    fetched_ref[...] = fetched
    pre = mm(fetched, weight_ref[...]) + edges_ref[...].astype(F32)
    sig = sigmoid(pre)
    act = (pre * sig).astype(BF16)
    slope_ref[...] = (sig * (1.0 + pre * (1.0 - sig))).astype(BF16)
    raw = target_ref[...]
    aimed = jnp.where(raw >= 0, raw - device * mesh_rows, -1)
    summed = mm(rows_onehot(aimed, mesh_rows), act)
    mid = (mesh_ref[...].astype(F32) + factor * summed).astype(BF16)
    local = fine_ref[...] - (device // subs) * level_rows
    part = mm(rows_onehot(local, level_rows), mid)
    first = part[:half]
    second = part[half:]
    keep_ref[...] = jnp.where(core == 0, first, second)
    core_ref[:half] = jnp.where(core == 0, second, first).astype(BF16)
    core_ref[half : half + mesh_rows] = mid
    farpkt_ref[:mesh_rows] = mid
    features = grid_ref.shape[1]
    spot = (
        lax.broadcasted_iota(I32, (mesh_rows, features), 0)
        == lax.broadcasted_iota(I32, (mesh_rows, features), 1)
    )
    spread = jnp.where(spot, 1.0, 0.0).astype(BF16)
    fine_rows = mm(
        jnp.broadcast_to(local.astype(F32), (16, mesh_rows)).astype(BF16), spread
    ).astype(BF16)[:8]
    core_ref[half + mesh_rows :] = fine_rows
    farpkt_ref[mesh_rows:] = fine_rows


def spread_kernel(dev_ref, mine_ref, other_ref, coarse_ref, out_ref, *, subs, factor):
    device = dev_ref[0]
    core = device % 2
    tile = device // subs
    half, features = mine_ref.shape
    group = features // half
    total = mine_ref[...].astype(F32) + other_ref[...].astype(F32)
    mid = (factor * total).astype(BF16)
    level_rows = coarse_ref.shape[1]
    ids = coarse_ref[...]
    split = jnp.where(
        lax.broadcasted_iota(I32, (16, level_rows), 0) == 0, ids >> 4, ids & 15
    )
    j = lax.broadcasted_iota(I32, (level_rows, features), 0) - core * half
    lane = lax.broadcasted_iota(I32, (level_rows, features), 1) - (tile % group) * half
    sel = (j == lane) & (j >= 0) & (j < half)
    ids_rows = mm(split.astype(F32).astype(BF16), jnp.where(sel, 1.0, 0.0).astype(BF16))
    ids_rows = ids_rows.astype(BF16)[:8]
    for peer in range(out_ref.shape[0]):
        out_ref[peer, :half] = mid
        out_ref[peer, half:] = ids_rows


def middle_kernel(
    dev_ref,
    mine_ref,
    other_ref,
    core_ref,
    farpkt_ref,
    farin_ref,
    grid_ref,
    cot_ref,
    edges_ref,
    source_ref,
    target_ref,
    decode_weight_ref,
    middle_weight_ref,
    summit_weight_ref,
    update_ref,
    dgrad_ref,
    own_ref,
    partner_ref,
    far_ref,
    level_ref,
    middle_slope_ref,
    summit_in_ref,
    summit_slope_ref,
    ids_ref,
    out_scr,
    lift_scr,
    *,
    subs,
    level_rows,
    summit_factor,
    decode_factor,
):
    device = dev_ref[0]
    core = device % 2
    tile = device // subs
    tiles, _, features = mine_ref.shape
    half = level_rows // 2
    group = min(features // half, tiles)
    groups = tiles // group
    chunk = group * half
    for g in range(groups):
        for src, which in ((mine_ref, core), (other_ref, 1 - core)):
            block = src[g * group : (g + 1) * group]
            level_ref[which, g] = block[:, :half].reshape(chunk, features)
            codes = jnp.sum(block[:, half:].astype(F32), axis=0)
            ids = (codes[0:1] * 16.0 + codes[1:2]).astype(I32)[:, :chunk]
            ids_ref[which, g] = jnp.broadcast_to(ids, (8, chunk))
    summed = jnp.zeros((TOP_NODES, features), F32)
    for g in range(groups):
        for h in range(2):
            mid = level_ref[h, g]
            act = mm(mid, middle_weight_ref[...])
            sig = sigmoid(act)
            out = (mid.astype(F32) + act * sig).astype(BF16)
            middle_slope_ref[h, g] = (sig * (1.0 + act * (1.0 - sig))).astype(BF16)
            out_scr[h, pl.ds(g * chunk, chunk)] = out
            summed = summed + mm(rows_onehot(ids_ref[h, g][:1], TOP_NODES), out)
    summit_in = (summit_factor * summed).astype(BF16)
    summit_in_ref[...] = summit_in
    act = mm(summit_in, summit_weight_ref[...])
    sig = sigmoid(act)
    summit_slope_ref[...] = sig * (1.0 + act * (1.0 - sig))
    summit_out = (act * sig).astype(BF16)
    for g in range(groups):
        for h in range(2):
            lift_scr[h, pl.ds(g * chunk, chunk)] = mm_tn(
                rows_onehot(ids_ref[h, g][:1], TOP_NODES), summit_out
            ).astype(BF16)

    mesh_rows = farpkt_ref.shape[0] - 8
    rows = mesh_rows
    sub = device % subs
    far_tile = jnp.where(sub == 0, tile - 1, jnp.where(sub == subs - 1, tile + 1, tile))
    far_tile = jnp.clip(far_tile, 0, tiles - 1)

    def table(ref):
        pieces = []
        for at in (tile, far_tile):
            for h in range(2):
                pieces.append(ref[h, pl.ds(pl.multiple_of(at * half, half), half)])
        return jnp.concatenate(pieces, axis=0)

    own_fine = farpkt_ref[rows:, :rows].astype(F32)[:1].astype(I32)
    partner_fine = core_ref[half + rows :, :rows].astype(F32)[:1].astype(I32)
    far_fine = farin_ref[rows:, :rows].astype(F32)[:1].astype(I32) + level_rows
    fine = jnp.concatenate([own_fine, partner_fine, far_fine], axis=1)
    members = cols_onehot(fine, 2 * level_rows)
    lifted = mm(members, table(out_scr)) + mm(members, table(lift_scr))
    mids = jnp.concatenate(
        [farpkt_ref[:rows], core_ref[half : half + rows], farin_ref[:rows]], axis=0
    )
    wide = (mids.astype(F32) + lifted).astype(BF16)

    place = slots(source_ref[...], device, core, rows)
    fetched = mm(cols_onehot(place, 3 * rows), wide).astype(BF16)
    pre = mm(fetched, decode_weight_ref[...]) + edges_ref[...].astype(F32)
    sig = sigmoid(pre)
    grid_rows = grid_ref.shape[0]
    raw = target_ref[...]
    aimed = jnp.where(raw >= 0, raw - device * grid_rows, -1)
    summed = mm(rows_onehot(aimed, grid_rows), (pre * sig).astype(BF16))
    update_ref[...] = (grid_ref[...].astype(F32) + decode_factor * summed).astype(BF16)
    incoming = mm(cols_onehot(aimed, grid_rows), cot_ref[...]) * decode_factor
    slope = (incoming * (sig * (1.0 + pre * (1.0 - sig)))).astype(BF16)
    dgrad_ref[...] = mm_tn(fetched, slope)
    gathered = mm(rows_onehot(place, 3 * rows), slope).astype(BF16)
    returned = mm_nt(gathered, decode_weight_ref[...])
    own_ref[...] = returned[:rows]
    partner_ref[...] = returned[rows : 2 * rows]
    far_ref[...] = returned[2 * rows :].astype(BF16)


def level_kernel(
    dev_ref, own_ref, farin_ref, partner_ref, farpkt_ref, core_ref,
    sum_ref, pkt_ref, keep_ref, *, level_rows
):
    core = dev_ref[0] % 2
    rows = own_ref.shape[0]
    half = level_rows // 2
    grad = own_ref[...] + farin_ref[...].astype(F32)
    sum_ref[...] = grad
    own_fine = farpkt_ref[rows:, :rows].astype(F32)[:1].astype(I32)
    partner_fine = core_ref[half + rows :, :rows].astype(F32)[:1].astype(I32)
    partner = partner_ref[...].astype(BF16)
    part = mm(rows_onehot(own_fine, level_rows), grad.astype(BF16)) + mm(
        rows_onehot(partner_fine, level_rows), partner
    )
    first = part[:half]
    second = part[half:]
    keep_ref[...] = jnp.where(core == 0, first, second)
    pkt_ref[:half] = jnp.where(core == 0, second, first).astype(BF16)
    pkt_ref[half:] = partner


def copies_kernel(mine_ref, other_ref, out_ref):
    total = (mine_ref[...].astype(F32) + other_ref[...].astype(F32)).astype(BF16)
    for peer in range(out_ref.shape[0]):
        out_ref[peer] = total


def back_kernel(
    dev_ref,
    mine_ref,
    other_ref,
    level_ref,
    middle_slope_ref,
    summit_in_ref,
    summit_slope_ref,
    ids_ref,
    sum_ref,
    partnerin_ref,
    farpkt_ref,
    fetched_ref,
    slope_ref,
    target_ref,
    dgrad_ref,
    middle_weight_ref,
    summit_weight_ref,
    middle_grad_ref,
    summit_grad_ref,
    send_ref,
    keep_ref,
    grad_scr,
    back_scr,
    *,
    subs,
    level_rows,
    summit_factor,
    middle_factor,
    encode_factor,
):
    device = dev_ref[0]
    core = device % 2
    tile = device // subs
    tiles, half, features = mine_ref.shape
    _, groups, chunk, _ = level_ref.shape
    group = chunk // half
    for g in range(groups):
        for src, which in ((mine_ref, core), (other_ref, 1 - core)):
            grad_scr[which, g] = src[g * group : (g + 1) * group].reshape(chunk, features)
    total = jnp.zeros((TOP_NODES, features), F32)
    for g in range(groups):
        for h in range(2):
            total = total + mm(rows_onehot(ids_ref[h, g][:1], TOP_NODES), grad_scr[h, g])
    summit_slope = (total * summit_slope_ref[...]).astype(BF16)
    summit_grad_ref[...] = mm_tn(summit_in_ref[...], summit_slope)
    summit_back = mm_nt(summit_slope, summit_weight_ref[...]).astype(BF16)
    middle_grad = jnp.zeros((features, features), F32)
    for g in range(groups):
        for h in range(2):
            lifted = mm_tn(rows_onehot(ids_ref[h, g][:1], TOP_NODES), summit_back)
            level_total = grad_scr[h, g].astype(F32) + summit_factor * lifted
            back_scr[h, pl.ds(g * chunk, chunk)] = level_total
            slope = (level_total * middle_slope_ref[h, g].astype(F32)).astype(BF16)
            grad_scr[h, g] = slope
            middle_grad = middle_grad + mm_tn(level_ref[h, g], slope)
    middle_grad_ref[...] = middle_grad
    at = pl.multiple_of(tile * half, half)
    spot = pl.multiple_of((tile % group) * half, half)
    level_total = jnp.concatenate([back_scr[h, pl.ds(at, half)] for h in range(2)], axis=0)
    slope = jnp.concatenate(
        [grad_scr[h, tile // group, pl.ds(spot, half)] for h in range(2)], axis=0
    )
    back = (level_total + mm_nt(slope, middle_weight_ref[...])).astype(BF16)
    rows = sum_ref.shape[0]
    own_fine = farpkt_ref[rows:, :rows].astype(F32)[:1].astype(I32)
    mesh_total = (
        sum_ref[...]
        + partnerin_ref[half:].astype(F32)
        + middle_factor * mm(cols_onehot(own_fine, level_rows), back)
    )
    raw = target_ref[...]
    aimed = jnp.where(raw >= 0, raw - device * rows, -1)
    upstream = mm(cols_onehot(aimed, rows), mesh_total.astype(BF16)) * encode_factor
    slope = (upstream * slope_ref[...].astype(F32)).astype(BF16)
    egrad = mm_tn(fetched_ref[...], slope)
    dgrad = dgrad_ref[...]
    send_ref[...] = jnp.where(core == 0, dgrad, egrad).astype(BF16)
    keep_ref[...] = jnp.where(core == 0, egrad, dgrad)


def call(body, outs, args, scratch=(), **static):
    vmem = pl.BlockSpec(memory_space=pltpu.VMEM)
    smem = pl.BlockSpec(memory_space=pltpu.SMEM)
    specs = [smem if a.ndim == 1 else vmem for a in args]
    single = not isinstance(outs, (list, tuple))
    return pl.pallas_call(
        functools.partial(body, **static),
        out_shape=outs,
        in_specs=specs,
        out_specs=vmem if single else [vmem] * len(outs),
        scratch_shapes=list(scratch),
        compiler_params=pltpu.CompilerParams(vmem_limit_bytes=60 * 1024 * 1024),
        name=body.__name__,
    )(*args)


def shape(dims, dtype):
    return jax.ShapeDtypeStruct(dims, dtype)


def shards(
    grid_feats,
    mesh_feats,
    encode_edges,
    decode_edges,
    encode_source,
    encode_target,
    decode_source,
    decode_target,
    owner_fine,
    owner_coarse,
    encode_weight,
    decode_weight,
    middle_weight,
    summit_weight,
    cotangent,
):
    rows, features = grid_feats.shape
    mesh_rows = mesh_feats.shape[0]
    level_rows = owner_coarse.shape[0]
    half = level_rows // 2
    tiles = lax.axis_size("tile")
    subs = lax.axis_size("row") * lax.axis_size("core")
    devices = tiles * subs
    chips = devices // 2
    edges = encode_source.shape[0]
    swap = [(0, 1), (1, 0)]
    beside = []
    for left in range(1, devices - 1, 2):
        beside += [(left, left + 1), (left + 1, left)]
    device = lax.axis_index(ALL).astype(I32)
    dev = device.reshape(1)
    core = device % 2
    encode_factor = mesh_rows / edges
    decode_factor = rows / decode_source.shape[0]
    middle_factor = level_rows / (mesh_rows * subs)
    summit_factor = TOP_NODES / (level_rows * tiles)
    group = min(features // half, tiles)
    groups = tiles // group
    chunk = group * half

    grid_far = lax.ppermute(grid_feats, ALL, beside)
    grid_partner = lax.ppermute(grid_feats, "core", swap)
    fetched, slope, core_pkt, far_pkt, keep = call(
        encode_kernel,
        [
            shape((edges, features), BF16),
            shape((edges, features), BF16),
            shape((half + mesh_rows + 8, features), BF16),
            shape((mesh_rows + 8, features), BF16),
            shape((half, features), F32),
        ],
        [
            dev,
            grid_feats,
            grid_partner,
            grid_far,
            mesh_feats,
            encode_edges,
            encode_source[None],
            encode_target[None],
            owner_fine[None],
            encode_weight,
        ],
        subs=subs,
        level_rows=level_rows,
        factor=encode_factor,
    )
    core_in = lax.ppermute(core_pkt, "core", swap)
    far_in = lax.ppermute(far_pkt, ALL, beside)
    mine = (keep + core_in[:half].astype(F32)).astype(BF16)
    other = lax.ppermute(mine, "row", swap)
    packed = call(
        spread_kernel,
        shape((tiles, half + 8, features), BF16),
        [dev, mine, other, owner_coarse[None]],
        subs=subs,
        factor=middle_factor,
    )
    mids = lax.all_to_all(packed, "tile", 0, 0)
    mids_other = lax.ppermute(mids, "core", swap)
    full = (2, groups, chunk, features)
    (
        grid_update,
        dgrad,
        own,
        partner,
        far,
        level,
        middle_slope,
        summit_in,
        summit_slope,
        ids,
    ) = call(
        middle_kernel,
        [
            shape((rows, features), BF16),
            shape((features, features), F32),
            shape((mesh_rows, features), F32),
            shape((mesh_rows, features), F32),
            shape((mesh_rows, features), BF16),
            shape(full, BF16),
            shape(full, BF16),
            shape((TOP_NODES, features), BF16),
            shape((TOP_NODES, features), F32),
            shape((2, groups, 8, chunk), I32),
        ],
        [
            dev,
            mids,
            mids_other,
            core_in,
            far_pkt,
            far_in,
            grid_feats,
            cotangent,
            decode_edges,
            decode_source[None],
            decode_target[None],
            decode_weight,
            middle_weight,
            summit_weight,
        ],
        scratch=[
            pltpu.VMEM((2, tiles * half, features), BF16),
            pltpu.VMEM((2, tiles * half, features), BF16),
        ],
        subs=subs,
        level_rows=level_rows,
        summit_factor=summit_factor,
        decode_factor=decode_factor,
    )
    far_back = lax.ppermute(far, ALL, beside)
    grad_sum, core_pkt, keep = call(
        level_kernel,
        [
            shape((mesh_rows, features), F32),
            shape((half + mesh_rows, features), BF16),
            shape((half, features), F32),
        ],
        [dev, own, far_back, partner, far_pkt, core_in],
        level_rows=level_rows,
    )
    back_in = lax.ppermute(core_pkt, "core", swap)
    mine = (keep + back_in[:half].astype(F32)).astype(BF16)
    other = lax.ppermute(mine, "row", swap)
    packed = call(copies_kernel, shape((tiles, half, features), BF16), [mine, other])
    grads = lax.all_to_all(packed, "tile", 0, 0)
    grads_other = lax.ppermute(grads, "core", swap)
    middle_grad, summit_grad, send, keep = call(
        back_kernel,
        [
            shape((features, features), F32),
            shape((features, features), F32),
            shape((features, features), BF16),
            shape((features, features), F32),
        ],
        [
            dev,
            grads,
            grads_other,
            level,
            middle_slope,
            summit_in,
            summit_slope,
            ids,
            grad_sum,
            back_in,
            far_pkt,
            fetched,
            slope,
            encode_target[None],
            dgrad,
            middle_weight,
            summit_weight,
        ],
        scratch=[
            pltpu.VMEM(full, BF16),
            pltpu.VMEM((2, tiles * half, features), F32),
        ],
        subs=subs,
        level_rows=level_rows,
        summit_factor=summit_factor,
        middle_factor=middle_factor,
        encode_factor=encode_factor,
    )
    received = lax.ppermute(send, "core", swap)
    share = (keep + received.astype(F32)).astype(BF16)
    share = share.reshape(chips, features // chips, features)
    parts = lax.all_to_all(share, CHIPS, 0, 0)
    summed = jnp.sum(parts.astype(F32), axis=0).astype(BF16)
    copies = jnp.broadcast_to(summed[None], parts.shape)
    mine = lax.all_to_all(copies, CHIPS, 0, 0).reshape(features, features)
    other = lax.ppermute(mine, "core", swap)
    encode_grad = jnp.where(core == 0, mine, other).astype(F32)
    decode_grad = jnp.where(core == 0, other, mine).astype(F32)
    return (grid_update, encode_grad, decode_grad, middle_grad, summit_grad)


def solution(mesh):
    tiles, subs = mesh.devices.shape
    fine = Mesh(mesh.devices.reshape(tiles, subs // 2, 2), ALL)
    placed = (
        P(ALL, None),
        P(ALL, None),
        P(ALL, None),
        P(ALL, None),
        P(ALL),
        P(ALL),
        P(ALL),
        P(ALL),
        P(ALL),
        P("tile"),
        P(),
        P(),
        P(),
        P(),
        P(ALL, None),
    )
    return jax.shard_map(
        shards,
        mesh=fine,
        in_specs=placed,
        out_specs=(P(ALL, None), P(), P(), P(), P()),
        check_vma=False,
    )
```

time: 565 us -> 160 us (0.28)
  waiting for transfers between devices: 400 us -> 15.5 us
  blocking collectives: 0 us -> 79.3 us
  matrix products: 54.6 us -> 0 us
  local copies, waits for them, and re-layouts: 36.6 us -> 4.29 us
  Pallas kernels: 0 us -> 28.9 us
  between operations: 14.3 us -> 0.77 us
  loops' own time: 12.6 us -> 0 us
  other arithmetic: 17.2 us -> 4.93 us
    psum x5 -> x0, waiting for transfers between devices: 396 us -> none  [the longest x1 143 us: shards(): lax.psum((encode_local, decode_local, sub_share * middle_local), ('tile',...]
    all_to_all x0 -> x4, blocking collectives: none -> 79.3 us  [the longest x1 22.9 us: shards(): mids = lax.all_to_all(packed, 'tile', 0, 0)]
    dot_general x38 -> x0, matrix products: 54.6 us -> none  [the longest x10 17.5 us: outer_sum(): lax.dot_general(left, right, (((0,), (0,)), ((), ())), preferred_element_...]
    pallas_call x0 -> x6, Pallas kernels: none -> 28.9 us  [call(): pl.pallas_call(functools.partial(body, **static), out_shape=outs, in_spec...]
    gather x29 -> x0, local copies, waits for them, and re-layouts: 24.5 us -> none  [the longest x16 13.6 us: block_step(): fetched = jnp.take(sources, picked, axis=0)]
    another operation x4 -> x0, loops' own time: 12.6 us -> none  [the longest x2 6.37 us: edge_backward(): return lax.fori_loop(0, blocks, block_step, (start_grad, start_back))]
    ppermute x6 -> x12, waiting for transfers between devices: 3.77 us -> 15.5 us  [the longest x2 5.26 us: shards(): other = lax.ppermute(mine, 'row', swap)]
    and x18 -> x0, other arithmetic: 9.35 us -> none  [the longest x16 9.33 us: block_step(): fetched = jnp.take(sources, picked, axis=0)]
  transfers between devices with their start and end apart: 11 -> 12, of which waited for: 8 -> 9; matrix products, arithmetic and copies ran while one was open for 2% -> 0% of each run, Pallas kernels for 0% -> 0%
where the time goes in v1:
time: 160 us; the launch traced here: 159 us
  blocking collectives  79.3 us (50%)
  Pallas kernels  28.9 us (18%)
  starting transfers between devices  25.4 us (16%)
  waiting for transfers between devices  15.5 us (10%)
  other arithmetic  4.93 us (3%)
  local copies, waits for them, and re-layouts  4.29 us (3%)
    pallas_call x6, Pallas kernels, call(): pl.pallas_call(functools.partial(body, **static), out_shape=outs, in_spec...  28.9 us
    all_to_all x1, blocking collectives, shards(): mids = lax.all_to_all(packed, 'tile', 0, 0)  22.9 us
    all_to_all x1, blocking collectives, shards(): parts = lax.all_to_all(share, CHIPS, 0, 0)  19.3 us
    all_to_all x1, blocking collectives, shards(): grads = lax.all_to_all(packed, 'tile', 0, 0)  18.8 us
    all_to_all x1, blocking collectives, shards(): mine = lax.all_to_all(copies, CHIPS, 0, 0).reshape(features, features)  18.2 us
    ppermute x1, starting transfers between devices, shards(): back_in = lax.ppermute(core_pkt, 'core', swap)  10.7 us
    ppermute x1, starting transfers between devices, shards(): core_in = lax.ppermute(core_pkt, 'core', swap)  6.16 us
    ppermute x2, starting transfers between devices, shards(): other = lax.ppermute(mine, 'row', swap)  5.83 us
  transfers between devices with their start and end apart: 12, of which 9 were waited for; matrix products, arithmetic and copies ran while one was open for 0% of the time, Pallas kernels for 0%

profile of v1, /device:TPU:0, one launch (start us, length us, event | category | flops | bytes accessed | tf_op | source)
XLA Modules:
  0.0 159.0 jit_solution(11335037057282900677)
XLA Ops:
  0.6 0.6 collective-permute-start
  1.2 0.7 collective-permute-start.1
  1.9 0.5 collective-permute-done.partner_ref
  2.4 0.0 collective-permute-done.1.far_ref
  2.4 0.6 copy-done.11
  3.0 0.0 copy-done.12
  3.1 5.3 %encode_kernel.1 = (bf16[1024,512]{1,0:T(8,128)(2,1)}, bf16[1024,512]{1,0:T(8,128)(2,1)}, bf16[200,512]{1,0:T(8,128)(2,1)}, bf16[136,512]{1,0:T(8,128)(2,1)}, f32[64,512]{1,0:T(8,128)}) custom-call(s32[1]{0:T(128)} %bitcast.dev_ref, bf16[128,512]{1,0:T(8,128)(2,1)} %grid_ref.3, bf16[128,512]{1,0:T(8,128)(2,1)} %copy-done.11, bf16[128,512]{1,0:T(8,128)(2,1)} %copy-done.12, ...), custom_call_target="tpu_custom_call" | custom-call | tf_op jit(solution)/shard_map/encode_kernel/pallas_call | solution.py:373
  8.4 6.2 %collective-permute-start.2 = (bf16[200,512]{1,0:T(8,128)(2,1)}, bf16[200,512]{1,0:T(8,128)(2,1)S(1)}, u32[]{:S(2)}, u32[]{:S(2)}) collective-permute-start(bf16[200,512]{1,0:T(8,128)(2,1)} %get-tuple-element.28), channel_id=1, source_target_pairs={{0,1},{1,0},{2,3},{3,2},{4,5},{5,4},{6,7},{7,6},{8,9},{9,8},{10,11... | collective-permute-start | bytes 614408 | tf_op jit(solution)/shard_map/ppermute | solution.py:456
  14.6 1.3 collective-permute-done.2.core_ref
  15.8 1.0 add_convert_fusion.2.mine_ref
  16.8 0.0 copy-start.8
  16.9 3.1 %collective-permute-start.3 = (bf16[64,512]{1,0:T(8,128)(2,1)S(1)}, bf16[64,512]{1,0:T(8,128)(2,1)S(1)}, u32[]{:S(2)}, u32[]{:S(2)}) collective-permute-start(bf16[64,512]{1,0:T(8,128)(2,1)S(1)} %add_convert_fusion.2.mine_ref), channel_id=1, source_target_pairs={{0,2},{2,0},{1,3},{3,1},{4,6},{6,4},{5,7},{7,5},{8,10},{10,8},{9,1... | collective-permute-start | bytes 196616 | tf_op jit(solution)/shard_map/ppermute | solution.py:459
  19.9 2.6 %collective-permute-done.3.other_ref = bf16[64,512]{1,0:T(8,128)(2,1)S(1)} collective-permute-done((bf16[64,512]{1,0:T(8,128)(2,1)S(1)}, bf16[64,512]{1,0:T(8,128)(2,1)S(1)}, u32[]{:S(2)}, u32[]{:S(2)}) %collective-permute-start.3) | collective-permute-done | bytes 65568 | tf_op jit(solution)/shard_map/ppermute | solution.py:459
  22.6 0.6 copy-done.14
  23.2 1.8 %spread_kernel.1 = bf16[8,72,512]{2,1,0:T(8,128)(2,1)} custom-call(s32[1]{0:T(128)} %bitcast.dev_ref, bf16[64,512]{1,0:T(8,128)(2,1)} %copy-done.8, bf16[64,512]{1,0:T(8,128)(2,1)} %copy-done.14, s32[1,128]{1,0:T(1,128)} %bitcast.18), custom_call_target="tpu_custom_call" | custom-call | tf_op jit(solution)/shard_map/spread_kernel/pallas_call | solution.py:373
  25.0 22.9 %all_to_all.20.mine_ref = bf16[8,72,512]{2,1,0:T(8,128)(2,1)S(1)} all-to-all(bf16[8,72,512]{2,1,0:T(8,128)(2,1)} %spread_kernel.1), channel_id=1, replica_groups=mesh['tile'=8,'row'=2,'core'=2] {'tile'}, dimensions={0} | all-to-all | bytes 1179648 | tf_op jit(solution)/shard_map/all_to_all | solution.py:467
  47.9 0.0 collective-permute-start.4
  48.0 0.7 collective-permute-start.5
  48.6 0.0 collective-permute-done.5.farin_ref
  48.7 1.3 collective-permute-done.4.other_ref
  50.0 0.8 copy-done.4
  50.8 9.0 %middle_kernel.1 = (bf16[128,512]{1,0:T(8,128)(2,1)}, f32[512,512]{1,0:T(8,128)}, f32[128,512]{1,0:T(8,128)}, f32[128,512]{1,0:T(8,128)}, bf16[128,512]{1,0:T(8,...) custom-call(s32[1]{0:T(128)} %bitcast.dev_ref, ...), custom_call_target="tpu_custom_call" | custom-call | tf_op jit(solution)/shard_map/middle_kernel/pallas_call | solution.py:373
  59.7 0.7 collective-permute-start.6
  60.4 0.0 collective-permute-done.6.farin_ref
  60.4 0.0 copy-start.10
  60.4 0.6 copy-done.10
  61.1 2.2 %level_kernel.1 = (f32[128,512]{1,0:T(8,128)}, bf16[192,512]{1,0:T(8,128)(2,1)}, f32[64,512]{1,0:T(8,128)}) custom-call(s32[1]{0:T(128)} %bitcast.dev_ref, f32[128,512]{1,0:T(8,128)} %get-tuple-element.31.own_ref, bf16[128,512]{1,0:T(8,128)(2,1)} %copy-done.10, f32[128,512]{1,0:T(8,128)} %get-tuple-element.33.partner_ref, ...), custom_call_target="tpu_custom_call" | custom-call | tf_op jit(solution)/shard_map/level_kernel/pallas_call | solution.py:373
  63.2 10.7 %collective-permute-start.7 = (bf16[192,512]{1,0:T(8,128)(2,1)}, bf16[192,512]{1,0:T(8,128)(2,1)S(1)}, u32[]{:S(2)}, u32[]{:S(2)}) collective-permute-start(bf16[192,512]{1,0:T(8,128)(2,1)} %get-tuple-element.35), channel_id=1, source_target_pairs={{0,1},{1,0},{2,3},{3,2},{4,5},{5,4},{6,7},{7,6},{8,9},{9,8},{10,11... | collective-permute-start | bytes 589832 | tf_op jit(solution)/shard_map/ppermute | solution.py:531
  74.0 1.3 collective-permute-done.7.partnerin_ref
  75.2 1.0 add_convert_fusion.1.mine_ref
  76.2 0.0 copy-start.7
  76.2 2.8 %collective-permute-start.8 = (bf16[64,512]{1,0:T(8,128)(2,1)S(1)}, bf16[64,512]{1,0:T(8,128)(2,1)S(1)}, u32[]{:S(2)}, u32[]{:S(2)}) collective-permute-start(bf16[64,512]{1,0:T(8,128)(2,1)S(1)} %add_convert_fusion.1.mine_ref), channel_id=1, source_target_pairs={{0,2},{2,0},{1,3},{3,1},{4,6},{6,4},{5,7},{7,5},{8,10},{10,8},{9,1... | collective-permute-start | bytes 196616 | tf_op jit(solution)/shard_map/ppermute | solution.py:533
  79.0 2.6 %collective-permute-done.8.other_ref = bf16[64,512]{1,0:T(8,128)(2,1)S(1)} collective-permute-done((bf16[64,512]{1,0:T(8,128)(2,1)S(1)}, bf16[64,512]{1,0:T(8,128)(2,1)S(1)}, u32[]{:S(2)}, u32[]{:S(2)}) %collective-permute-start.8) | collective-permute-done | bytes 65568 | tf_op jit(solution)/shard_map/ppermute | solution.py:533
  81.6 0.6 copy-done.13
  82.3 1.7 %copies_kernel.1 = bf16[8,64,512]{2,1,0:T(8,128)(2,1)} custom-call(bf16[64,512]{1,0:T(8,128)(2,1)} %copy-done.7, bf16[64,512]{1,0:T(8,128)(2,1)} %copy-done.13), custom_call_target="tpu_custom_call" | custom-call | tf_op jit(solution)/shard_map/copies_kernel/pallas_call | solution.py:373
  84.0 18.8 %all_to_all.21.mine_ref = bf16[8,64,512]{2,1,0:T(8,128)(2,1)S(1)} all-to-all(bf16[8,64,512]{2,1,0:T(8,128)(2,1)} %copies_kernel.1), channel_id=1, replica_groups=mesh['tile'=8,'row'=2,'core'=2] {'tile'}, dimensions={0} | all-to-all | bytes 1048576 | tf_op jit(solution)/shard_map/all_to_all | solution.py:535
  102.8 1.9 %collective-permute-done.9.other_ref = bf16[8,64,512]{2,1,0:T(8,128)(2,1)S(1)} collective-permute-done((bf16[8,64,512]{2,1,0:T(8,128)(2,1)S(1)}, bf16[8,64,512]{2,1,0:T(8,128)(2,1)S(1)}, u32[]{:S(2)}, u32[]{:S(2)}) %collective-permute-start.9) | collective-permute-done | bytes 524320 | tf_op jit(solution)/shard_map/ppermute | solution.py:536
  104.7 0.8 copy-done.5
  105.5 8.9 %back_kernel.1 = (f32[512,512]{1,0:T(8,128)}, f32[512,512]{1,0:T(8,128)}, bf16[512,512]{1,0:T(8,128)(2,1)}, f32[512,512]{1,0:T(8,128)}) custom-call(s32[1]{0:T(128)} %bitcast.dev_ref, bf16[8,64,512]{2,1,0:T(8,128)(2,1)} %copy-done.1, bf16[8,64,512]{2,1,0:T(8,128)(2,1)} %copy-done.5, bf16[2,1,512,512]{3,2,1,0:T(8,128)(2,1)} %get-tuple-element.36.level_ref, ...), custom_call_target="tpu_custom_call" | custom-call | tf_op jit(solution)/shard_map/back_kernel/pallas_call | solution.py:373
  114.4 0.1 collective-permute-start.10
  114.6 2.0 %collective-permute-done.10 = bf16[512,512]{1,0:T(8,128)(2,1)S(1)} collective-permute-done((bf16[512,512]{1,0:T(8,128)(2,1)}, bf16[512,512]{1,0:T(8,128)(2,1)S(1)}, u32[]{:S(2)}, u32[]{:S(2)}) %collective-permute-start.10) | collective-permute-done | bytes 524320 | tf_op jit(solution)/shard_map/ppermute | solution.py:574
  116.6 1.4 add_convert_fusion
  117.9 19.3 %all_to_all.22 = bf16[16,32,512]{2,1,0:T(8,128)(2,1)S(1)} all-to-all(bf16[16,32,512]{2,1,0:T(8,128)(2,1)S(1)} %bitcast.12), channel_id=1, replica_groups=mesh['tile'=8,'row'=2,'core'=2] {'tile','row'}, dimensions={0} | all-to-all | bytes 1048576 | tf_op jit(solution)/shard_map/all_to_all | solution.py:577
  137.3 0.1 reduce_sum.12
  137.4 18.2 %all_to_all.23 = bf16[16,32,512]{2,1,0:T(8,128)(2,1)S(1)} all-to-all(bf16[16,32,512]{2,1,0:T(8,128)(2,1)S(1)} %broadcast_in_dim.31), channel_id=1, replica_groups=mesh['tile'=8,'row'=2,'core'=2] {'tile','row'}, dimensions={0} | all-to-all | bytes 1048576 | tf_op jit(solution)/shard_map/all_to_all | solution.py:580
  155.6 0.0 collective-permute-start.11
  155.6 1.9 %collective-permute-done.11 = bf16[512,512]{1,0:T(8,128)(2,1)S(1)} collective-permute-done((bf16[512,512]{1,0:T(8,128)(2,1)S(1)}, bf16[512,512]{1,0:T(8,128)(2,1)S(1)}, u32[]{:S(2)}, u32[]{:S(2)}) %collective-permute-start.11) | collective-permute-done | bytes 524320 | tf_op jit(solution)/shard_map/ppermute | solution.py:581
  157.5 1.5 select_convert_fusion
  (22 shorter events, 0.1 us)
Async XLA Ops:
  0.6 1.8 %collective-permute-start = (bf16[128,512]{1,0:T(8,128)(2,1)}, bf16[128,512]{1,0:T(8,128)(2,1)S(1)}, u32[]{:S(2)}, u32[]{:S(2)}) collective-permute-start(bf16[128,512]{1,0:T(8,128)(2,1)} %grid_ref.3), channel_id=1, source_target_pairs={{0,1},{1,0},{2,3},{3,2},{4,5},{5,4},{6,7},{7,6},{8,9},{9,8},{10,11... | collective-permute-start | bytes 393224 | tf_op jit(solution)/shard_map/ppermute | solution.py:430
  1.2 1.2 collective-permute-start.1
  2.4 0.7 copy-start.11
  2.4 0.7 copy-start.12
  8.4 7.5 %collective-permute-start.2 = (bf16[200,512]{1,0:T(8,128)(2,1)}, bf16[200,512]{1,0:T(8,128)(2,1)S(1)}, u32[]{:S(2)}, u32[]{:S(2)}) collective-permute-start(bf16[200,512]{1,0:T(8,128)(2,1)} %get-tuple-element.28), channel_id=1, source_target_pairs={{0,1},{1,0},{2,3},{3,2},{4,5},{5,4},{6,7},{7,6},{8,9},{9,8},{10,11... | collective-permute-start | bytes 614408 | tf_op jit(solution)/shard_map/ppermute | solution.py:456
  15.8 9.2 %copy-start.3 = (bf16[200,512]{1,0:T(8,128)(2,1)}, bf16[200,512]{1,0:T(8,128)(2,1)S(1)}, u32[]{:S(2)}) copy-start(bf16[200,512]{1,0:T(8,128)(2,1)S(1)} %collective-permute-done.2.core_ref) | copy-start | bytes 614404
  16.8 5.7 %copy-start.8 = (bf16[64,512]{1,0:T(8,128)(2,1)}, bf16[64,512]{1,0:T(8,128)(2,1)S(1)}, u32[]{:S(2)}) copy-start(bf16[64,512]{1,0:T(8,128)(2,1)S(1)} %add_convert_fusion.2.mine_ref) | copy-start | bytes 196612
  16.9 5.7 %collective-permute-start.3 = (bf16[64,512]{1,0:T(8,128)(2,1)S(1)}, bf16[64,512]{1,0:T(8,128)(2,1)S(1)}, u32[]{:S(2)}, u32[]{:S(2)}) collective-permute-start(bf16[64,512]{1,0:T(8,128)(2,1)S(1)} %add_convert_fusion.2.mine_ref), channel_id=1, source_target_pairs={{0,2},{2,0},{1,3},{3,1},{4,6},{6,4},{5,7},{7,5},{8,10},{10,8},{9,1... | collective-permute-start | bytes 196616 | tf_op jit(solution)/shard_map/ppermute | solution.py:459
  22.6 0.6 copy-start.14
  25.0 22.9 %copy-start.2 = (bf16[136,512]{1,0:T(8,128)(2,1)S(1)}, bf16[136,512]{1,0:T(8,128)(2,1)}, u32[]{:S(2)}) copy-start(bf16[136,512]{1,0:T(8,128)(2,1)} %get-tuple-element.29.farpkt_ref) | copy-start | bytes 417796
  47.9 2.0 %copy-start = (bf16[8,72,512]{2,1,0:T(8,128)(2,1)}, bf16[8,72,512]{2,1,0:T(8,128)(2,1)S(1)}, u32[]{:S(2)}) copy-start(bf16[8,72,512]{2,1,0:T(8,128)(2,1)S(1)} %all_to_all.20.mine_ref) | copy-start | bytes 1769476
  47.9 2.0 %collective-permute-start.4 = (bf16[8,72,512]{2,1,0:T(8,128)(2,1)S(1)}, bf16[8,72,512]{2,1,0:T(8,128)(2,1)S(1)}, u32[]{:S(2)}, u32[]{:S(2)}) collective-permute-start(bf16[8,72,512]{2,1,0:T(8,128)(2,1)S(1)} %all_to_all.20.mine_ref), channel_id=1, source_target_pairs={{0,1},{1,0},{2,3},{3,2},{4,5},{5,4},{6,7},{7,6},{8,9},{9,8},{10,11... | collective-permute-start | bytes 1769480 | tf_op jit(solution)/shard_map/ppermute | solution.py:468
  48.0 0.7 collective-permute-start.5
  48.6 1.3 copy-start.9
  49.9 0.8 copy-start.4
  59.7 0.7 collective-permute-start.6
  60.4 0.7 copy-start.10
  63.2 12.0 %collective-permute-start.7 = (bf16[192,512]{1,0:T(8,128)(2,1)}, bf16[192,512]{1,0:T(8,128)(2,1)S(1)}, u32[]{:S(2)}, u32[]{:S(2)}) collective-permute-start(bf16[192,512]{1,0:T(8,128)(2,1)} %get-tuple-element.35), channel_id=1, source_target_pairs={{0,1},{1,0},{2,3},{3,2},{4,5},{5,4},{6,7},{7,6},{8,9},{9,8},{10,11... | collective-permute-start | bytes 589832 | tf_op jit(solution)/shard_map/ppermute | solution.py:531
  75.2 8.7 %copy-start.6 = (bf16[192,512]{1,0:T(8,128)(2,1)}, bf16[192,512]{1,0:T(8,128)(2,1)S(1)}, u32[]{:S(2)}) copy-start(bf16[192,512]{1,0:T(8,128)(2,1)S(1)} %collective-permute-done.7.partnerin_ref) | copy-start | bytes 589828
  76.2 5.4 %copy-start.7 = (bf16[64,512]{1,0:T(8,128)(2,1)}, bf16[64,512]{1,0:T(8,128)(2,1)S(1)}, u32[]{:S(2)}) copy-start(bf16[64,512]{1,0:T(8,128)(2,1)S(1)} %add_convert_fusion.1.mine_ref) | copy-start | bytes 196612
  76.2 5.4 %collective-permute-start.8 = (bf16[64,512]{1,0:T(8,128)(2,1)S(1)}, bf16[64,512]{1,0:T(8,128)(2,1)S(1)}, u32[]{:S(2)}, u32[]{:S(2)}) collective-permute-start(bf16[64,512]{1,0:T(8,128)(2,1)S(1)} %add_convert_fusion.1.mine_ref), channel_id=1, source_target_pairs={{0,2},{2,0},{1,3},{3,1},{4,6},{6,4},{5,7},{7,5},{8,10},{10,8},{9,1... | collective-permute-start | bytes 196616 | tf_op jit(solution)/shard_map/ppermute | solution.py:533
  81.6 0.6 copy-start.13
  102.8 1.9 %copy-start.1 = (bf16[8,64,512]{2,1,0:T(8,128)(2,1)}, bf16[8,64,512]{2,1,0:T(8,128)(2,1)S(1)}, u32[]{:S(2)}) copy-start(bf16[8,64,512]{2,1,0:T(8,128)(2,1)S(1)} %all_to_all.21.mine_ref) | copy-start | bytes 1572868
  102.8 1.9 %collective-permute-start.9 = (bf16[8,64,512]{2,1,0:T(8,128)(2,1)S(1)}, bf16[8,64,512]{2,1,0:T(8,128)(2,1)S(1)}, u32[]{:S(2)}, u32[]{:S(2)}) collective-permute-start(bf16[8,64,512]{2,1,0:T(8,128)(2,1)S(1)} %all_to_all.21.mine_ref), channel_id=1, source_target_pairs={{0,1},{1,0},{2,3},{3,2},{4,5},{5,4},{6,7},{7,6},{8,9},{9,8},{10,11... | collective-permute-start | bytes 1572872 | tf_op jit(solution)/shard_map/ppermute | solution.py:536
  104.7 0.8 copy-start.5
  114.4 2.1 %collective-permute-start.10 = (bf16[512,512]{1,0:T(8,128)(2,1)}, bf16[512,512]{1,0:T(8,128)(2,1)S(1)}, u32[]{:S(2)}, u32[]{:S(2)}) collective-permute-start(bf16[512,512]{1,0:T(8,128)(2,1)} %get-tuple-element.46), channel_id=1, source_target_pairs={{0,1},{1,0},{2,3},{3,2},{4,5},{5,4},{6,7},{7,6},{8,9},{9,8},{10,11... | collective-permute-start | bytes 1572872 | tf_op jit(solution)/shard_map/ppermute | solution.py:574
  155.6 1.9 %collective-permute-start.11 = (bf16[512,512]{1,0:T(8,128)(2,1)S(1)}, bf16[512,512]{1,0:T(8,128)(2,1)S(1)}, u32[]{:S(2)}, u32[]{:S(2)}) collective-permute-start(bf16[512,512]{1,0:T(8,128)(2,1)S(1)} %bitcast.11), channel_id=1, source_target_pairs={{0,1},{1,0},{2,3},{3,2},{4,5},{5,4},{6,7},{7,6},{8,9},{9,8},{10,11... | collective-permute-start | bytes 1572872 | tf_op jit(solution)/shard_map/ppermute | solution.py:581

commit v2 on v1

--- a/solution.py
+++ b/solution.py
@@ -8,6 +8,8 @@
 from jax.sharding import Mesh, PartitionSpec as P
 
 TOP_NODES = 512
+LANES = 128
+WORKING_BYTES = 10 * 2**20
 ALL = ("tile", "row", "core")
 CHIPS = ("tile", "row")
 BF16 = jnp.bfloat16
@@ -47,6 +49,17 @@
     n = ids.shape[1]
     hit = lax.broadcasted_iota(I32, (n, cols), 1) == column(ids)
     return jnp.where(hit, 1.0, 0.0).astype(BF16)
+
+
+def coarse_split(ids):
+    at = lax.broadcasted_iota(I32, (16, ids.shape[1]), 0)
+    parts = jnp.where(at == 0, ids >> 4, jnp.where(at == 1, ids & 15, 0))
+    return parts.astype(F32).astype(BF16)
+
+
+def node_ids(block):
+    codes = block.astype(F32)
+    return (codes[2:3].astype(I32), (codes[0:1] * 16.0 + codes[1:2]).astype(I32))
 
 
 def slots(source, device, core, rows):
@@ -68,6 +81,7 @@
     source_ref,
     target_ref,
     fine_ref,
+    coarse_ref,
     weight_ref,
     fetched_ref,
     slope_ref,
@@ -100,7 +114,8 @@
     summed = mm(rows_onehot(aimed, mesh_rows), act)
     mid = (mesh_ref[...].astype(F32) + factor * summed).astype(BF16)
     local = fine_ref[...] - (device // subs) * level_rows
-    part = mm(rows_onehot(local, level_rows), mid)
+    members = rows_onehot(local, level_rows)
+    part = mm(members, mid)
     first = part[:half]
     second = part[half:]
     keep_ref[...] = jnp.where(core == 0, first, second)
@@ -113,9 +128,10 @@
         == lax.broadcasted_iota(I32, (mesh_rows, features), 1)
     )
     spread = jnp.where(spot, 1.0, 0.0).astype(BF16)
-    fine_rows = mm(
-        jnp.broadcast_to(local.astype(F32), (16, mesh_rows)).astype(BF16), spread
-    ).astype(BF16)[:8]
+    at = lax.broadcasted_iota(I32, (16, mesh_rows), 0)
+    codes = mm(coarse_split(coarse_ref[...]), members)
+    codes = jnp.where(at == 2, local.astype(F32), codes)
+    fine_rows = mm(codes.astype(BF16), spread).astype(BF16)[:8]
     core_ref[half + mesh_rows :] = fine_rows
     farpkt_ref[mesh_rows:] = fine_rows
 
@@ -129,18 +145,20 @@
     total = mine_ref[...].astype(F32) + other_ref[...].astype(F32)
     mid = (factor * total).astype(BF16)
     level_rows = coarse_ref.shape[1]
-    ids = coarse_ref[...]
-    split = jnp.where(
-        lax.broadcasted_iota(I32, (16, level_rows), 0) == 0, ids >> 4, ids & 15
-    )
     j = lax.broadcasted_iota(I32, (level_rows, features), 0) - core * half
     lane = lax.broadcasted_iota(I32, (level_rows, features), 1) - (tile % group) * half
     sel = (j == lane) & (j >= 0) & (j < half)
-    ids_rows = mm(split.astype(F32).astype(BF16), jnp.where(sel, 1.0, 0.0).astype(BF16))
-    ids_rows = ids_rows.astype(BF16)[:8]
+    codes = mm(coarse_split(coarse_ref[...]), jnp.where(sel, 1.0, 0.0).astype(BF16))
+    lanes = out_ref.shape[2]
+    strips = features // lanes
+    tail = jnp.concatenate(
+        [codes[r : r + 1, i * lanes : (i + 1) * lanes] for r in range(2) for i in range(strips)],
+        axis=0,
+    ).astype(BF16)
     for peer in range(out_ref.shape[0]):
-        out_ref[peer, :half] = mid
-        out_ref[peer, half:] = ids_rows
+        for i in range(strips):
+            out_ref[peer, i * half : (i + 1) * half] = mid[:, i * lanes : (i + 1) * lanes]
+        out_ref[peer, strips * half :] = tail
 
 
 def middle_kernel(
@@ -169,7 +187,6 @@
     summit_slope_ref,
     ids_ref,
     out_scr,
-    lift_scr,
     *,
     subs,
     level_rows,
@@ -179,7 +196,9 @@
     device = dev_ref[0]
     core = device % 2
     tile = device // subs
-    tiles, _, features = mine_ref.shape
+    tiles, _, lanes = mine_ref.shape
+    features = grid_ref.shape[1]
+    strips = features // lanes
     half = level_rows // 2
     group = min(features // half, tiles)
     groups = tiles // group
@@ -187,10 +206,14 @@
     for g in range(groups):
         for src, which in ((mine_ref, core), (other_ref, 1 - core)):
             block = src[g * group : (g + 1) * group]
-            level_ref[which, g] = block[:, :half].reshape(chunk, features)
-            codes = jnp.sum(block[:, half:].astype(F32), axis=0)
-            ids = (codes[0:1] * 16.0 + codes[1:2]).astype(I32)[:, :chunk]
-            ids_ref[which, g] = jnp.broadcast_to(ids, (8, chunk))
+            for i in range(strips):
+                level_ref[which, g, :, i * lanes : (i + 1) * lanes] = block[
+                    :, i * half : (i + 1) * half
+                ].reshape(chunk, lanes)
+            codes = jnp.sum(block[:, strips * half :].astype(F32), axis=0)
+            ids = codes[:strips] * 16.0 + codes[strips : 2 * strips]
+            ids = jnp.concatenate([ids[i : i + 1] for i in range(strips)], axis=1)
+            ids_ref[which, g] = jnp.broadcast_to(ids.astype(I32)[:, :chunk], (8, chunk))
     summed = jnp.zeros((TOP_NODES, features), F32)
     for g in range(groups):
         for h in range(2):
@@ -207,11 +230,6 @@
     sig = sigmoid(act)
     summit_slope_ref[...] = sig * (1.0 + act * (1.0 - sig))
     summit_out = (act * sig).astype(BF16)
-    for g in range(groups):
-        for h in range(2):
-            lift_scr[h, pl.ds(g * chunk, chunk)] = mm_tn(
-                rows_onehot(ids_ref[h, g][:1], TOP_NODES), summit_out
-            ).astype(BF16)
 
     mesh_rows = farpkt_ref.shape[0] - 8
     rows = mesh_rows
@@ -226,12 +244,14 @@
                 pieces.append(ref[h, pl.ds(pl.multiple_of(at * half, half), half)])
         return jnp.concatenate(pieces, axis=0)
 
-    own_fine = farpkt_ref[rows:, :rows].astype(F32)[:1].astype(I32)
-    partner_fine = core_ref[half + rows :, :rows].astype(F32)[:1].astype(I32)
-    far_fine = farin_ref[rows:, :rows].astype(F32)[:1].astype(I32) + level_rows
-    fine = jnp.concatenate([own_fine, partner_fine, far_fine], axis=1)
-    members = cols_onehot(fine, 2 * level_rows)
-    lifted = mm(members, table(out_scr)) + mm(members, table(lift_scr))
+    own_fine, own_top = node_ids(farpkt_ref[rows:, :rows])
+    partner_fine, partner_top = node_ids(core_ref[half + rows :, :rows])
+    far_fine, far_top = node_ids(farin_ref[rows:, :rows])
+    fine = jnp.concatenate([own_fine, partner_fine, far_fine + level_rows], axis=1)
+    top = jnp.concatenate([own_top, partner_top, far_top], axis=1)
+    lifted = mm(cols_onehot(fine, 2 * level_rows), table(out_scr)) + mm(
+        cols_onehot(top, TOP_NODES), summit_out
+    )
     mids = jnp.concatenate(
         [farpkt_ref[:rows], core_ref[half : half + rows], farin_ref[:rows]], axis=0
     )
@@ -265,8 +285,8 @@
     half = level_rows // 2
     grad = own_ref[...] + farin_ref[...].astype(F32)
     sum_ref[...] = grad
-    own_fine = farpkt_ref[rows:, :rows].astype(F32)[:1].astype(I32)
-    partner_fine = core_ref[half + rows :, :rows].astype(F32)[:1].astype(I32)
+    own_fine, _ = node_ids(farpkt_ref[rows:, :rows])
+    partner_fine, _ = node_ids(core_ref[half + rows :, :rows])
     partner = partner_ref[...].astype(BF16)
     part = mm(rows_onehot(own_fine, level_rows), grad.astype(BF16)) + mm(
         rows_onehot(partner_fine, level_rows), partner
@@ -276,12 +296,6 @@
     keep_ref[...] = jnp.where(core == 0, first, second)
     pkt_ref[:half] = jnp.where(core == 0, second, first).astype(BF16)
     pkt_ref[half:] = partner
-
-
-def copies_kernel(mine_ref, other_ref, out_ref):
-    total = (mine_ref[...].astype(F32) + other_ref[...].astype(F32)).astype(BF16)
-    for peer in range(out_ref.shape[0]):
-        out_ref[peer] = total
 
 
 def back_kernel(
@@ -349,7 +363,7 @@
     )
     back = (level_total + mm_nt(slope, middle_weight_ref[...])).astype(BF16)
     rows = sum_ref.shape[0]
-    own_fine = farpkt_ref[rows:, :rows].astype(F32)[:1].astype(I32)
+    own_fine, _ = node_ids(farpkt_ref[rows:, :rows])
     mesh_total = (
         sum_ref[...]
         + partnerin_ref[half:].astype(F32)
@@ -370,13 +384,16 @@
     smem = pl.BlockSpec(memory_space=pltpu.SMEM)
     specs = [smem if a.ndim == 1 else vmem for a in args]
     single = not isinstance(outs, (list, tuple))
+    held = [a for a in args if a.ndim > 1] + ([outs] if single else list(outs)) + list(scratch)
+    limit = sum(a.size * a.dtype.itemsize for a in held) + WORKING_BYTES
+    limit = min(limit, 60 * 2**20)
     return pl.pallas_call(
         functools.partial(body, **static),
         out_shape=outs,
         in_specs=specs,
         out_specs=vmem if single else [vmem] * len(outs),
-        scratch_shapes=list(scratch),
-        compiler_params=pltpu.CompilerParams(vmem_limit_bytes=60 * 1024 * 1024),
+        scratch_shapes=[pltpu.VMEM(s.shape, s.dtype) for s in scratch],
+        compiler_params=pltpu.CompilerParams(vmem_limit_bytes=limit),
         name=body.__name__,
     )(*args)
 
@@ -447,6 +464,7 @@
             encode_source[None],
             encode_target[None],
             owner_fine[None],
+            owner_coarse[None],
             encode_weight,
         ],
         subs=subs,
@@ -459,7 +477,7 @@
     other = lax.ppermute(mine, "row", swap)
     packed = call(
         spread_kernel,
-        shape((tiles, half + 8, features), BF16),
+        shape((tiles, (features // LANES) * half + 8, LANES), BF16),
         [dev, mine, other, owner_coarse[None]],
         subs=subs,
         factor=middle_factor,
@@ -509,8 +527,7 @@
             summit_weight,
         ],
         scratch=[
-            pltpu.VMEM((2, tiles * half, features), BF16),
-            pltpu.VMEM((2, tiles * half, features), BF16),
+            shape((2, tiles * half, features), BF16),
         ],
         subs=subs,
         level_rows=level_rows,
@@ -531,7 +548,8 @@
     back_in = lax.ppermute(core_pkt, "core", swap)
     mine = (keep + back_in[:half].astype(F32)).astype(BF16)
     other = lax.ppermute(mine, "row", swap)
-    packed = call(copies_kernel, shape((tiles, half, features), BF16), [mine, other])
+    total = (mine.astype(F32) + other.astype(F32)).astype(BF16)
+    packed = jnp.broadcast_to(total[None], (tiles, half, features))
     grads = lax.all_to_all(packed, "tile", 0, 0)
     grads_other = lax.ppermute(grads, "core", swap)
     middle_grad, summit_grad, send, keep = call(
@@ -562,8 +580,8 @@
             summit_weight,
         ],
         scratch=[
-            pltpu.VMEM(full, BF16),
-            pltpu.VMEM((2, tiles * half, features), F32),
+            shape(full, BF16),
+            shape((2, tiles * half, features), F32),
         ],
         subs=subs,
         level_rows=level_rows,

time: 160 us -> 140 us (0.88)
  Pallas kernels: 28.9 us -> 13.5 us
  other arithmetic: 4.93 us -> 1.82 us
    pallas_call x6 -> x5, Pallas kernels: 28.9 us -> 13.5 us  [call(): pl.pallas_call(functools.partial(body, **static), out_shape=outs, in_spec...]
    unnamed x30 -> x32, local copies, waits for them, and re-layouts: 4.24 us -> 4.8 us
where the time goes in v2:
time: 140 us; the launch traced here: 139 us
  blocking collectives  77.8 us (56%)
  starting transfers between devices  25.6 us (18%)
  waiting for transfers between devices  14.6 us (10%)
  Pallas kernels  13.5 us (10%)
  local copies, waits for them, and re-layouts  4.88 us (3%)
  other arithmetic  1.82 us (1%)
    all_to_all x1, blocking collectives, shards(): mids = lax.all_to_all(packed, 'tile', 0, 0)  21.9 us
    all_to_all x1, blocking collectives, shards(): parts = lax.all_to_all(share, CHIPS, 0, 0)  19.2 us
    all_to_all x1, blocking collectives, shards(): grads = lax.all_to_all(packed, 'tile', 0, 0)  18.6 us
    all_to_all x1, blocking collectives, shards(): mine = lax.all_to_all(copies, CHIPS, 0, 0).reshape(features, features)  18.2 us
    pallas_call x5, Pallas kernels, call(): pl.pallas_call(functools.partial(body, **static), out_shape=outs, in_spec...  13.5 us
    ppermute x1, starting transfers between devices, shards(): back_in = lax.ppermute(core_pkt, 'core', swap)  10.7 us
    ppermute x1, starting transfers between devices, shards(): core_in = lax.ppermute(core_pkt, 'core', swap)  6.21 us
    ppermute x2, starting transfers between devices, shards(): other = lax.ppermute(mine, 'row', swap)  5.85 us
  transfers between devices with their start and end apart: 12, of which 9 were waited for; matrix products, arithmetic and copies ran while one was open for 0% of the time, Pallas kernels for 0%

profile of v2, /device:TPU:0, one launch (start us, length us, event | category | flops | bytes accessed | tf_op | source)
XLA Modules:
  0.0 139.1 jit_solution(782659520526449932)
XLA Ops:
  0.6 0.6 collective-permute-start
  1.2 0.7 collective-permute-start.1
  1.9 0.5 collective-permute-done.partner_ref
  2.4 0.0 collective-permute-done.1.far_ref
  2.4 0.0 copy-start.15
  2.4 0.7 copy-done.11
  3.1 0.0 copy-done.10
  3.1 0.0 copy-done.14
  3.1 0.0 copy-done.15
  3.1 1.2 copy-done.2
  4.3 0.9 copy-done.5
  5.2 1.0 copy-done.7
  6.3 0.9 copy-done.8
  7.2 3.0 %encode_kernel.1 = (bf16[1024,512]{1,0:T(8,128)(2,1)S(1)}, bf16[1024,512]{1,0:T(8,128)(2,1)S(1)}, bf16[200,512]{1,0:T(8,128)(2,1)S(1)}, bf16[136,512]{1,0:T(8,128)(2,1)S(1)}, f32[64,512]{1,0:T(8,128)S(1)}) custom-call(s32[1]{0:T(128)} %bitcast.dev_ref, bf16[128,512]{1,0:T(8,128)(2,1)S(1)} %copy-done.5, ...), custom_call_target="tpu_custom_call" | custom-call | tf_op jit(solution)/shard_map/encode_kernel/pallas_call | solution.py:390
  10.2 6.2 %collective-permute-start.2 = (bf16[200,512]{1,0:T(8,128)(2,1)S(1)}, bf16[200,512]{1,0:T(8,128)(2,1)S(1)}, u32[]{:S(2)}, u32[]{:S(2)}) collective-permute-start(bf16[200,512]{1,0:T(8,128)(2,1)S(1)} %get-tuple-element.28), channel_id=1, source_target_pairs={{0,1},{1,0},{2,3},{3,2},{4,5},{5,4},{6,7},{7,6},{8,9},{9,8},{10,11... | collective-permute-start | bytes 614408 | tf_op jit(solution)/shard_map/ppermute | solution.py:474
  16.4 1.1 collective-permute-done.2.core_ref
  17.5 3.1 %collective-permute-start.3 = (bf16[64,512]{1,0:T(8,128)(2,1)S(1)}, bf16[64,512]{1,0:T(8,128)(2,1)S(1)}, u32[]{:S(2)}, u32[]{:S(2)}) collective-permute-start(bf16[64,512]{1,0:T(8,128)(2,1)S(1)} %add_convert_fusion.3.mine_ref), channel_id=1, source_target_pairs={{0,2},{2,0},{1,3},{3,1},{4,6},{6,4},{5,7},{7,5},{8,10},{10,8},{9,1... | collective-permute-start | bytes 196616 | tf_op jit(solution)/shard_map/ppermute | solution.py:477
  20.6 2.6 %collective-permute-done.3.other_ref = bf16[64,512]{1,0:T(8,128)(2,1)S(1)} collective-permute-done((bf16[64,512]{1,0:T(8,128)(2,1)S(1)}, bf16[64,512]{1,0:T(8,128)(2,1)S(1)}, u32[]{:S(2)}, u32[]{:S(2)}) %collective-permute-start.3) | collective-permute-done | bytes 65568 | tf_op jit(solution)/shard_map/ppermute | solution.py:477
  23.2 0.2 spread_kernel.1
  23.4 0.0 copy-start.1
  23.4 21.9 %all_to_all.20.mine_ref = bf16[8,264,128]{2,1,0:T(8,128)(2,1)S(1)} all-to-all(bf16[8,264,128]{2,1,0:T(8,128)(2,1)S(1)} %spread_kernel.1), channel_id=1, replica_groups=mesh['tile'=8,'row'=2,'core'=2] {'tile'}, dimensions={0} | all-to-all | bytes 1081344 | tf_op jit(solution)/shard_map/all_to_all | solution.py:485
  45.2 0.0 collective-permute-start.4
  45.2 0.8 collective-permute-start.5
  46.0 0.0 collective-permute-done.5.farin_ref
  46.0 1.1 collective-permute-done.4.other_ref
  47.2 0.0 copy-done.4
  47.2 0.0 copy-done.9
  47.2 5.5 %middle_kernel.1 = (bf16[128,512]{1,0:T(8,128)(2,1)}, f32[512,512]{1,0:T(8,128)S(1)}, f32[128,512]{1,0:T(8,128)S(1)}, f32[128,512]{1,0:T(8,128)S(1)}, bf16[128,5...) custom-call(s32[1]{0:T(128)} %bitcast.dev_ref, ...), custom_call_target="tpu_custom_call" | custom-call | tf_op jit(solution)/shard_map/middle_kernel/pallas_call | solution.py:390
  52.7 0.7 collective-permute-start.6
  53.4 0.0 collective-permute-done.6.farin_ref
  53.4 0.2 level_kernel.1
  53.6 10.7 %collective-permute-start.7 = (bf16[192,512]{1,0:T(8,128)(2,1)S(1)}, bf16[192,512]{1,0:T(8,128)(2,1)S(1)}, u32[]{:S(2)}, u32[]{:S(2)}) collective-permute-start(bf16[192,512]{1,0:T(8,128)(2,1)S(1)} %get-tuple-element.35), channel_id=1, source_target_pairs={{0,1},{1,0},{2,3},{3,2},{4,5},{5,4},{6,7},{7,6},{8,9},{9,8},{10,11... | collective-permute-start | bytes 589832 | tf_op jit(solution)/shard_map/ppermute | solution.py:548
  64.4 1.1 collective-permute-done.7.partnerin_ref
  65.5 2.8 %collective-permute-start.8 = (bf16[64,512]{1,0:T(8,128)(2,1)S(1)}, bf16[64,512]{1,0:T(8,128)(2,1)S(1)}, u32[]{:S(2)}, u32[]{:S(2)}) collective-permute-start(bf16[64,512]{1,0:T(8,128)(2,1)S(1)} %add_convert_fusion.2), channel_id=1, source_target_pairs={{0,2},{2,0},{1,3},{3,1},{4,6},{6,4},{5,7},{7,5},{8,10},{10,8},{9,1... | collective-permute-start | bytes 196616 | tf_op jit(solution)/shard_map/ppermute | solution.py:550
  68.3 2.6 %collective-permute-done.8 = bf16[64,512]{1,0:T(8,128)(2,1)S(1)} collective-permute-done((bf16[64,512]{1,0:T(8,128)(2,1)S(1)}, bf16[64,512]{1,0:T(8,128)(2,1)S(1)}, u32[]{:S(2)}, u32[]{:S(2)}) %collective-permute-start.8) | collective-permute-done | bytes 65568 | tf_op jit(solution)/shard_map/ppermute | solution.py:550
  71.0 18.6 %all_to_all.21.mine_ref = bf16[8,64,512]{2,1,0:T(8,128)(2,1)S(1)} all-to-all(bf16[8,64,512]{2,1,0:T(8,128)(2,1)S(1)} %broadcast_in_dim.38), channel_id=1, replica_groups=mesh['tile'=8,'row'=2,'core'=2] {'tile'}, dimensions={0} | all-to-all | bytes 1048576 | tf_op jit(solution)/shard_map/all_to_all | solution.py:553
  89.6 0.0 collective-permute-start.9
  89.6 1.9 %collective-permute-done.9.other_ref = bf16[8,64,512]{2,1,0:T(8,128)(2,1)S(1)} collective-permute-done((bf16[8,64,512]{2,1,0:T(8,128)(2,1)S(1)}, bf16[8,64,512]{2,1,0:T(8,128)(2,1)S(1)}, u32[]{:S(2)}, u32[]{:S(2)}) %collective-permute-start.9) | collective-permute-done | bytes 524320 | tf_op jit(solution)/shard_map/ppermute | solution.py:554
  91.5 4.6 %back_kernel.1 = (f32[512,512]{1,0:T(8,128)}, f32[512,512]{1,0:T(8,128)}, bf16[512,512]{1,0:T(8,128)(2,1)S(1)}, f32[512,512]{1,0:T(8,128)S(1)}) custom-call(s32[1]{0:T(128)} %bitcast.dev_ref, bf16[8,64,512]{2,1,0:T(8,128)(2,1)S(1)} %all_to_all.21.mine_ref, bf16[8,64,512]{2,1,0:T(8,128)(2,1)S(1)} %collective-permute-done.9.other_ref, ...), custom_call_target="tpu_custom_call" | custom-call | tf_op jit(solution)/shard_map/back_kernel/pallas_call | solution.py:390
  96.1 0.1 collective-permute-start.10
  96.2 1.8 %collective-permute-done.10 = bf16[512,512]{1,0:T(8,128)(2,1)S(1)} collective-permute-done((bf16[512,512]{1,0:T(8,128)(2,1)S(1)}, bf16[512,512]{1,0:T(8,128)(2,1)S(1)}, u32[]{:S(2)}, u32[]{:S(2)}) %collective-permute-start.10) | collective-permute-done | bytes 524320 | tf_op jit(solution)/shard_map/ppermute | solution.py:592
  98.0 0.2 add_convert_fusion
  98.2 19.2 %all_to_all.22 = bf16[16,32,512]{2,1,0:T(8,128)(2,1)S(1)} all-to-all(bf16[16,32,512]{2,1,0:T(8,128)(2,1)S(1)} %bitcast.20), channel_id=1, replica_groups=mesh['tile'=8,'row'=2,'core'=2] {'tile','row'}, dimensions={0} | all-to-all | bytes 1048576 | tf_op jit(solution)/shard_map/all_to_all | solution.py:595
  117.4 0.1 reduce_sum.12
  117.5 18.2 %all_to_all.23 = bf16[16,32,512]{2,1,0:T(8,128)(2,1)S(1)} all-to-all(bf16[16,32,512]{2,1,0:T(8,128)(2,1)S(1)} %broadcast_in_dim.39), channel_id=1, replica_groups=mesh['tile'=8,'row'=2,'core'=2] {'tile','row'}, dimensions={0} | all-to-all | bytes 1048576 | tf_op jit(solution)/shard_map/all_to_all | solution.py:598
  135.7 0.0 collective-permute-start.11
  135.7 1.9 %collective-permute-done.11 = bf16[512,512]{1,0:T(8,128)(2,1)S(1)} collective-permute-done((bf16[512,512]{1,0:T(8,128)(2,1)S(1)}, bf16[512,512]{1,0:T(8,128)(2,1)S(1)}, u32[]{:S(2)}, u32[]{:S(2)}) %collective-permute-start.11) | collective-permute-done | bytes 524320 | tf_op jit(solution)/shard_map/ppermute | solution.py:599
  137.6 1.5 %select_convert_fusion = (f32[512,512]{1,0:T(8,128)}, f32[512,512]{1,0:T(8,128)}) fusion(bf16[512,512]{1,0:T(8,128)(2,1)S(1)} %collective-permute-done.11, pred[]{:T(512)S(6)} %eq.6, bf16[16,32,512]{2,1,0:T(8,128)(2,1)S(1)} %all_to_all.23), kind=kLoop, calls=%fused_computation.1 | loop fusion | flops 1048576 | bytes 3145729 | tf_op jit(solution)/shard_map/convert_element_type | solution.py:601
  (25 shorter events, 0.2 us)
Async XLA Ops:
  0.6 1.8 %collective-permute-start = (bf16[128,512]{1,0:T(8,128)(2,1)}, bf16[128,512]{1,0:T(8,128)(2,1)S(1)}, u32[]{:S(2)}, u32[]{:S(2)}) collective-permute-start(bf16[128,512]{1,0:T(8,128)(2,1)} %grid_ref.3), channel_id=1, source_target_pairs={{0,1},{1,0},{2,3},{3,2},{4,5},{5,4},{6,7},{7,6},{8,9},{9,8},{10,11... | collective-permute-start | bytes 393224 | tf_op jit(solution)/shard_map/ppermute | solution.py:447
  1.2 1.2 collective-permute-start.1
  2.4 0.7 copy-start.11
  2.4 0.7 copy-start.10
  2.4 0.7 copy-start.14
  2.4 0.7 copy-start.15
  3.1 1.2 copy-start.2
  4.3 0.9 copy-start.5
  5.2 1.0 copy-start.7
  6.3 0.9 copy-start.8
  7.2 40.0 %copy-start.4 = (bf16[512,512]{1,0:T(8,128)(2,1)S(1)}, bf16[512,512]{1,0:T(8,128)(2,1)}, u32[]{:S(2)}) copy-start(bf16[512,512]{1,0:T(8,128)(2,1)} %decode_weight_ref.1) | copy-start | bytes 1572868
  10.2 7.3 %collective-permute-start.2 = (bf16[200,512]{1,0:T(8,128)(2,1)S(1)}, bf16[200,512]{1,0:T(8,128)(2,1)S(1)}, u32[]{:S(2)}, u32[]{:S(2)}) collective-permute-start(bf16[200,512]{1,0:T(8,128)(2,1)S(1)} %get-tuple-element.28), channel_id=1, source_target_pairs={{0,1},{1,0},{2,3},{3,2},{4,5},{5,4},{6,7},{7,6},{8,9},{9,8},{10,11... | collective-permute-start | bytes 614408 | tf_op jit(solution)/shard_map/ppermute | solution.py:474
  17.5 29.7 %copy-start.9 = (bf16[128,512]{1,0:T(8,128)(2,1)S(1)}, bf16[128,512]{1,0:T(8,128)(2,1)}, u32[]{:S(2)}) copy-start(bf16[128,512]{1,0:T(8,128)(2,1)} %cot_ref.1) | copy-start | bytes 393220
  17.5 5.7 %collective-permute-start.3 = (bf16[64,512]{1,0:T(8,128)(2,1)S(1)}, bf16[64,512]{1,0:T(8,128)(2,1)S(1)}, u32[]{:S(2)}, u32[]{:S(2)}) collective-permute-start(bf16[64,512]{1,0:T(8,128)(2,1)S(1)} %add_convert_fusion.3.mine_ref), channel_id=1, source_target_pairs={{0,2},{2,0},{1,3},{3,1},{4,6},{6,4},{5,7},{7,5},{8,10},{10,8},{9,1... | collective-permute-start | bytes 196616 | tf_op jit(solution)/shard_map/ppermute | solution.py:477
  23.2 24.0 %copy-start.3 = (bf16[512,512]{1,0:T(8,128)(2,1)S(1)}, bf16[512,512]{1,0:T(8,128)(2,1)}, u32[]{:S(2)}) copy-start(bf16[512,512]{1,0:T(8,128)(2,1)} %edges_ref.3) | copy-start | bytes 1572868
  23.2 24.0 %copy-start.6 = (bf16[128,512]{1,0:T(8,128)(2,1)S(1)}, bf16[128,512]{1,0:T(8,128)(2,1)}, u32[]{:S(2)}) copy-start(bf16[128,512]{1,0:T(8,128)(2,1)} %grid_ref.3) | copy-start | bytes 393220
  23.3 23.8 %copy-start = (bf16[512,512]{1,0:T(8,128)(2,1)S(1)}, bf16[512,512]{1,0:T(8,128)(2,1)}, u32[]{:S(2)}) copy-start(bf16[512,512]{1,0:T(8,128)(2,1)} %middle_weight_ref.3) | copy-start | bytes 1572868
  23.4 23.8 %copy-start.1 = (bf16[512,512]{1,0:T(8,128)(2,1)S(1)}, bf16[512,512]{1,0:T(8,128)(2,1)}, u32[]{:S(2)}) copy-start(bf16[512,512]{1,0:T(8,128)(2,1)} %summit_weight_ref.3) | copy-start | bytes 1572868
  45.2 1.9 %collective-permute-start.4 = (bf16[8,264,128]{2,1,0:T(8,128)(2,1)S(1)}, bf16[8,264,128]{2,1,0:T(8,128)(2,1)S(1)}, u32[]{:S(2)}, u32[]{:S(2)}) collective-permute-start(bf16[8,264,128]{2,1,0:T(8,128)(2,1)S(1)} %all_to_all.20.mine_ref), channel_id=1, source_target_pairs={{0,1},{1,0},{2,3},{3,2},{4,5},{5,4},{6,7},{7,6},{8,9},{9,8},{10,11... | collective-permute-start | bytes 1622024 | tf_op jit(solution)/shard_map/ppermute | solution.py:486
  45.2 2.0 %copy-start.13 = (s32[512]{0:T(512)S(1)}, s32[512]{0:T(512)}, u32[]{:S(2)}) copy-start(s32[512]{0:T(512)} %param.22) | copy-start | bytes 6148
  45.2 2.0 %copy-start.12 = (s32[512]{0:T(512)S(1)}, s32[512]{0:T(512)}, u32[]{:S(2)}) copy-start(s32[512]{0:T(512)} %param.21) | copy-start | bytes 6148
  45.2 0.8 collective-permute-start.5
  52.7 0.7 collective-permute-start.6
  53.6 11.8 %collective-permute-start.7 = (bf16[192,512]{1,0:T(8,128)(2,1)S(1)}, bf16[192,512]{1,0:T(8,128)(2,1)S(1)}, u32[]{:S(2)}, u32[]{:S(2)}) collective-permute-start(bf16[192,512]{1,0:T(8,128)(2,1)S(1)} %get-tuple-element.35), channel_id=1, source_target_pairs={{0,1},{1,0},{2,3},{3,2},{4,5},{5,4},{6,7},{7,6},{8,9},{9,8},{10,11... | collective-permute-start | bytes 589832 | tf_op jit(solution)/shard_map/ppermute | solution.py:548
  65.5 5.4 %collective-permute-start.8 = (bf16[64,512]{1,0:T(8,128)(2,1)S(1)}, bf16[64,512]{1,0:T(8,128)(2,1)S(1)}, u32[]{:S(2)}, u32[]{:S(2)}) collective-permute-start(bf16[64,512]{1,0:T(8,128)(2,1)S(1)} %add_convert_fusion.2), channel_id=1, source_target_pairs={{0,2},{2,0},{1,3},{3,1},{4,6},{6,4},{5,7},{7,5},{8,10},{10,8},{9,1... | collective-permute-start | bytes 196616 | tf_op jit(solution)/shard_map/ppermute | solution.py:550
  89.6 1.9 %collective-permute-start.9 = (bf16[8,64,512]{2,1,0:T(8,128)(2,1)S(1)}, bf16[8,64,512]{2,1,0:T(8,128)(2,1)S(1)}, u32[]{:S(2)}, u32[]{:S(2)}) collective-permute-start(bf16[8,64,512]{2,1,0:T(8,128)(2,1)S(1)} %all_to_all.21.mine_ref), channel_id=1, source_target_pairs={{0,1},{1,0},{2,3},{3,2},{4,5},{5,4},{6,7},{7,6},{8,9},{9,8},{10,11... | collective-permute-start | bytes 1572872 | tf_op jit(solution)/shard_map/ppermute | solution.py:554
  96.1 1.9 %collective-permute-start.10 = (bf16[512,512]{1,0:T(8,128)(2,1)S(1)}, bf16[512,512]{1,0:T(8,128)(2,1)S(1)}, u32[]{:S(2)}, u32[]{:S(2)}) collective-permute-start(bf16[512,512]{1,0:T(8,128)(2,1)S(1)} %get-tuple-element.46), channel_id=1, source_target_pairs={{0,1},{1,0},{2,3},{3,2},{4,5},{5,4},{6,7},{7,6},{8,9},{9,8},{10,11... | collective-permute-start | bytes 1572872 | tf_op jit(solution)/shard_map/ppermute | solution.py:592
  135.7 1.9 %collective-permute-start.11 = (bf16[512,512]{1,0:T(8,128)(2,1)S(1)}, bf16[512,512]{1,0:T(8,128)(2,1)S(1)}, u32[]{:S(2)}, u32[]{:S(2)}) collective-permute-start(bf16[512,512]{1,0:T(8,128)(2,1)S(1)} %bitcast.19), channel_id=1, source_target_pairs={{0,1},{1,0},{2,3},{3,2},{4,5},{5,4},{6,7},{7,6},{8,9},{9,8},{10,11... | collective-permute-start | bytes 1572872 | tf_op jit(solution)/shard_map/ppermute | solution.py:599

commit v3 on v2

--- a/solution.py
+++ b/solution.py
@@ -6,6 +6,7 @@
 from jax.experimental import pallas as pl
 from jax.experimental.pallas import tpu as pltpu
 from jax.sharding import Mesh, PartitionSpec as P
+
 
 TOP_NODES = 512
 LANES = 128
@@ -71,69 +72,92 @@
     return rel + jnp.where(before, shift_before, 0) + jnp.where(after, shift_after, 0)
 
 
+def ready_kernel(
+    dev_ref,
+    grid_ref,
+    edges_ref,
+    weight_ref,
+    source_ref,
+    target_ref,
+    fine_ref,
+    coarse_ref,
+    edges_out_ref,
+    weight_out_ref,
+    own_ref,
+    picks_ref,
+    aims_ref,
+    members_ref,
+    nodes_ref,
+    *,
+    subs,
+):
+    device = dev_ref[0]
+    rows, features = grid_ref.shape
+    mesh_rows = fine_ref.shape[1]
+    level_rows = coarse_ref.shape[1]
+    picks = cols_onehot(slots(source_ref[...], device, device % 2, rows), 3 * rows)
+    picks_ref[...] = picks[:, rows:]
+    raw = target_ref[...]
+    aimed = jnp.where(raw >= 0, raw - device * mesh_rows, -1)
+    aims_ref[...] = rows_onehot(aimed, mesh_rows)
+    local = fine_ref[...] - (device // subs) * level_rows
+    members = rows_onehot(local, level_rows)
+    members_ref[...] = members
+    spot = (
+        lax.broadcasted_iota(I32, (mesh_rows, features), 0)
+        == lax.broadcasted_iota(I32, (mesh_rows, features), 1)
+    )
+    spread = jnp.where(spot, 1.0, 0.0).astype(BF16)
+    at = lax.broadcasted_iota(I32, (16, mesh_rows), 0)
+    codes = mm(coarse_split(coarse_ref[...]), members)
+    codes = jnp.where(at == 2, local.astype(F32), codes)
+    nodes_ref[...] = mm(codes.astype(BF16), spread).astype(BF16)[:8]
+    own_ref[...] = mm(picks[:, :rows], grid_ref[...]).astype(BF16)
+    edges_out_ref[...] = edges_ref[...]
+    weight_out_ref[...] = weight_ref[...]
+
+
 def encode_kernel(
     dev_ref,
-    grid_ref,
     partner_ref,
     far_ref,
     mesh_ref,
     edges_ref,
-    source_ref,
-    target_ref,
-    fine_ref,
-    coarse_ref,
     weight_ref,
+    own_ref,
+    picks_ref,
+    aims_ref,
+    members_ref,
+    nodes_ref,
     fetched_ref,
     slope_ref,
     core_ref,
     farpkt_ref,
     keep_ref,
     *,
-    subs,
-    level_rows,
     factor,
 ):
-    device = dev_ref[0]
-    core = device % 2
-    rows = grid_ref.shape[0]
+    core = dev_ref[0] % 2
     mesh_rows = mesh_ref.shape[0]
-    half = level_rows // 2
-    picks = cols_onehot(slots(source_ref[...], device, core, rows), 3 * rows)
-    fetched = (
-        mm(picks[:, :rows], grid_ref[...])
-        + mm(picks[:, rows : 2 * rows], partner_ref[...])
-        + mm(picks[:, 2 * rows :], far_ref[...])
-    ).astype(BF16)
+    half = keep_ref.shape[0]
+    others = jnp.concatenate([partner_ref[...], far_ref[...]], axis=0)
+    fetched = (own_ref[...].astype(F32) + mm(picks_ref[...], others)).astype(BF16)
     fetched_ref[...] = fetched
     pre = mm(fetched, weight_ref[...]) + edges_ref[...].astype(F32)
     sig = sigmoid(pre)
     act = (pre * sig).astype(BF16)
     slope_ref[...] = (sig * (1.0 + pre * (1.0 - sig))).astype(BF16)
-    raw = target_ref[...]
-    aimed = jnp.where(raw >= 0, raw - device * mesh_rows, -1)
-    summed = mm(rows_onehot(aimed, mesh_rows), act)
+    summed = mm(aims_ref[...], act)
     mid = (mesh_ref[...].astype(F32) + factor * summed).astype(BF16)
-    local = fine_ref[...] - (device // subs) * level_rows
-    members = rows_onehot(local, level_rows)
-    part = mm(members, mid)
+    part = mm(members_ref[...], mid)
     first = part[:half]
     second = part[half:]
     keep_ref[...] = jnp.where(core == 0, first, second)
     core_ref[:half] = jnp.where(core == 0, second, first).astype(BF16)
     core_ref[half : half + mesh_rows] = mid
+    core_ref[half + mesh_rows :] = nodes_ref[...]
     farpkt_ref[:mesh_rows] = mid
-    features = grid_ref.shape[1]
-    spot = (
-        lax.broadcasted_iota(I32, (mesh_rows, features), 0)
-        == lax.broadcasted_iota(I32, (mesh_rows, features), 1)
-    )
-    spread = jnp.where(spot, 1.0, 0.0).astype(BF16)
-    at = lax.broadcasted_iota(I32, (16, mesh_rows), 0)
-    codes = mm(coarse_split(coarse_ref[...]), members)
-    codes = jnp.where(at == 2, local.astype(F32), codes)
-    fine_rows = mm(codes.astype(BF16), spread).astype(BF16)[:8]
-    core_ref[half + mesh_rows :] = fine_rows
-    farpkt_ref[mesh_rows:] = fine_rows
+    farpkt_ref[mesh_rows:] = nodes_ref[...]
 
 
 def spread_kernel(dev_ref, mine_ref, other_ref, coarse_ref, out_ref, *, subs, factor):
@@ -302,26 +326,24 @@
     dev_ref,
     mine_ref,
     other_ref,
-    level_ref,
     middle_slope_ref,
-    summit_in_ref,
     summit_slope_ref,
     ids_ref,
     sum_ref,
     partnerin_ref,
     farpkt_ref,
+    coarse_ref,
     fetched_ref,
     slope_ref,
     target_ref,
     dgrad_ref,
     middle_weight_ref,
     summit_weight_ref,
-    middle_grad_ref,
-    summit_grad_ref,
     send_ref,
     keep_ref,
-    grad_scr,
-    back_scr,
+    grad_ref,
+    top_ref,
+    top_back_ref,
     *,
     subs,
     level_rows,
@@ -332,35 +354,30 @@
     device = dev_ref[0]
     core = device % 2
     tile = device // subs
-    tiles, half, features = mine_ref.shape
-    _, groups, chunk, _ = level_ref.shape
+    _, half, features = mine_ref.shape
+    _, groups, chunk, _ = grad_ref.shape
     group = chunk // half
     for g in range(groups):
         for src, which in ((mine_ref, core), (other_ref, 1 - core)):
-            grad_scr[which, g] = src[g * group : (g + 1) * group].reshape(chunk, features)
+            grad_ref[which, g] = src[g * group : (g + 1) * group].reshape(chunk, features)
     total = jnp.zeros((TOP_NODES, features), F32)
     for g in range(groups):
         for h in range(2):
-            total = total + mm(rows_onehot(ids_ref[h, g][:1], TOP_NODES), grad_scr[h, g])
+            total = total + mm(rows_onehot(ids_ref[h, g][:1], TOP_NODES), grad_ref[h, g])
     summit_slope = (total * summit_slope_ref[...]).astype(BF16)
-    summit_grad_ref[...] = mm_tn(summit_in_ref[...], summit_slope)
+    top_ref[...] = summit_slope
     summit_back = mm_nt(summit_slope, summit_weight_ref[...]).astype(BF16)
-    middle_grad = jnp.zeros((features, features), F32)
-    for g in range(groups):
-        for h in range(2):
-            lifted = mm_tn(rows_onehot(ids_ref[h, g][:1], TOP_NODES), summit_back)
-            level_total = grad_scr[h, g].astype(F32) + summit_factor * lifted
-            back_scr[h, pl.ds(g * chunk, chunk)] = level_total
-            slope = (level_total * middle_slope_ref[h, g].astype(F32)).astype(BF16)
-            grad_scr[h, g] = slope
-            middle_grad = middle_grad + mm_tn(level_ref[h, g], slope)
-    middle_grad_ref[...] = middle_grad
-    at = pl.multiple_of(tile * half, half)
+    top_back_ref[...] = summit_back
     spot = pl.multiple_of((tile % group) * half, half)
-    level_total = jnp.concatenate([back_scr[h, pl.ds(at, half)] for h in range(2)], axis=0)
-    slope = jnp.concatenate(
-        [grad_scr[h, tile // group, pl.ds(spot, half)] for h in range(2)], axis=0
-    )
+
+    def own(ref):
+        pieces = [ref[h, tile // group, pl.ds(spot, half)] for h in range(2)]
+        return jnp.concatenate(pieces, axis=0).astype(F32)
+
+    level_total = own(grad_ref) + summit_factor * mm(
+        cols_onehot(coarse_ref[...], TOP_NODES), summit_back
+    )
+    slope = (level_total * own(middle_slope_ref)).astype(BF16)
     back = (level_total + mm_nt(slope, middle_weight_ref[...])).astype(BF16)
     rows = sum_ref.shape[0]
     own_fine, _ = node_ids(farpkt_ref[rows:, :rows])
@@ -377,6 +394,32 @@
     dgrad = dgrad_ref[...]
     send_ref[...] = jnp.where(core == 0, dgrad, egrad).astype(BF16)
     keep_ref[...] = jnp.where(core == 0, egrad, dgrad)
+
+
+def late_kernel(
+    dev_ref,
+    grad_ref,
+    level_ref,
+    middle_slope_ref,
+    summit_in_ref,
+    top_ref,
+    top_back_ref,
+    ids_ref,
+    middle_grad_ref,
+    summit_grad_ref,
+    *,
+    summit_factor,
+):
+    _, groups, _, features = grad_ref.shape
+    summit_grad_ref[...] = mm_tn(summit_in_ref[...], top_ref[...])
+    middle_grad = jnp.zeros((features, features), F32)
+    for g in range(groups):
+        for h in range(2):
+            lifted = mm_tn(rows_onehot(ids_ref[h, g][:1], TOP_NODES), top_back_ref[...])
+            level_total = grad_ref[h, g].astype(F32) + summit_factor * lifted
+            slope = (level_total * middle_slope_ref[h, g].astype(F32)).astype(BF16)
+            middle_grad = middle_grad + mm_tn(level_ref[h, g], slope)
+    middle_grad_ref[...] = middle_grad
 
 
 def call(body, outs, args, scratch=(), **static):
@@ -394,7 +437,6 @@
         out_specs=vmem if single else [vmem] * len(outs),
         scratch_shapes=[pltpu.VMEM(s.shape, s.dtype) for s in scratch],
         compiler_params=pltpu.CompilerParams(vmem_limit_bytes=limit),
-        name=body.__name__,
     )(*args)
 
 
@@ -445,6 +487,29 @@
 
     grid_far = lax.ppermute(grid_feats, ALL, beside)
     grid_partner = lax.ppermute(grid_feats, "core", swap)
+    edges_in, weight_in, own_rows, picks, aims, members, nodes = call(
+        ready_kernel,
+        [
+            shape((edges, features), BF16),
+            shape((features, features), BF16),
+            shape((edges, features), BF16),
+            shape((edges, 2 * rows), BF16),
+            shape((mesh_rows, edges), BF16),
+            shape((level_rows, mesh_rows), BF16),
+            shape((8, features), BF16),
+        ],
+        [
+            dev,
+            grid_feats,
+            encode_edges,
+            encode_weight,
+            encode_source[None],
+            encode_target[None],
+            owner_fine[None],
+            owner_coarse[None],
+        ],
+        subs=subs,
+    )
     fetched, slope, core_pkt, far_pkt, keep = call(
         encode_kernel,
         [
@@ -456,19 +521,17 @@
         ],
         [
             dev,
-            grid_feats,
             grid_partner,
             grid_far,
             mesh_feats,
-            encode_edges,
-            encode_source[None],
-            encode_target[None],
-            owner_fine[None],
-            owner_coarse[None],
-            encode_weight,
-        ],
-        subs=subs,
-        level_rows=level_rows,
+            edges_in,
+            weight_in,
+            own_rows,
+            picks,
+            aims,
+            members,
+            nodes,
+        ],
         factor=encode_factor,
     )
     core_in = lax.ppermute(core_pkt, "core", swap)
@@ -552,26 +615,26 @@
     packed = jnp.broadcast_to(total[None], (tiles, half, features))
     grads = lax.all_to_all(packed, "tile", 0, 0)
     grads_other = lax.ppermute(grads, "core", swap)
-    middle_grad, summit_grad, send, keep = call(
+    send, keep, level_back, top, top_back = call(
         back_kernel,
         [
-            shape((features, features), F32),
-            shape((features, features), F32),
             shape((features, features), BF16),
             shape((features, features), F32),
+            shape(full, BF16),
+            shape((TOP_NODES, features), BF16),
+            shape((TOP_NODES, features), BF16),
         ],
         [
             dev,
             grads,
             grads_other,
-            level,
             middle_slope,
-            summit_in,
             summit_slope,
             ids,
             grad_sum,
             back_in,
             far_pkt,
+            owner_coarse[None],
             fetched,
             slope,
             encode_target[None],
@@ -579,10 +642,6 @@
             middle_weight,
             summit_weight,
         ],
-        scratch=[
-            shape(full, BF16),
-            shape((2, tiles * half, features), F32),
-        ],
         subs=subs,
         level_rows=level_rows,
         summit_factor=summit_factor,
@@ -590,6 +649,12 @@
         encode_factor=encode_factor,
     )
     received = lax.ppermute(send, "core", swap)
+    middle_grad, summit_grad = call(
+        late_kernel,
+        [shape((features, features), F32), shape((features, features), F32)],
+        [dev, level_back, level, middle_slope, summit_in, top, top_back, ids],
+        summit_factor=summit_factor,
+    )
     share = (keep + received.astype(F32)).astype(BF16)
     share = share.reshape(chips, features // chips, features)
     parts = lax.all_to_all(share, CHIPS, 0, 0)

time: 140 us -> 138 us (0.986)
  starting transfers between devices: 25.6 us -> 22.1 us
  local copies, waits for them, and re-layouts: 4.88 us -> 7.11 us
  other arithmetic: 1.82 us -> 3.99 us
  waiting for transfers between devices: 14.6 us -> 12.5 us
    ppermute x1, starting transfers between devices: 6.21 us -> 3.95 us  [shards(): core_in = lax.ppermute(core_pkt, 'core', swap)]
    unnamed x32 -> x44, local copies, waits for them, and re-layouts: 4.8 us -> 7.02 us
    ppermute x1, waiting for transfers between devices: 1.91 us -> 0.01 us  [shards(): other = lax.ppermute(mine, 'core', swap)]
    pallas_call x5 -> x7, Pallas kernels: 13.5 us -> 14.1 us  [call(): pl.pallas_call(functools.partial(body, **static), out_shape=outs, in_spec...]
  transfers between devices with their start and end apart: 12 -> 12, of which waited for: 9 -> 7; matrix products, arithmetic and copies ran while one was open for 0% -> 0% of each run, Pallas kernels for 0% -> 3%
where the time goes in v3:
time: 138 us
  blocking collectives  77 us (56%)
  starting transfers between devices  22.1 us (16%)
  Pallas kernels  14.1 us (10%)
  waiting for transfers between devices  12.5 us (9%)
  local copies, waits for them, and re-layouts  7.11 us (5%)
  other arithmetic  3.99 us (3%)
    all_to_all x1, blocking collectives, shards(): mids = lax.all_to_all(packed, 'tile', 0, 0)  20.8 us
    all_to_all x1, blocking collectives, shards(): parts = lax.all_to_all(share, CHIPS, 0, 0)  19.5 us
    all_to_all x1, blocking collectives, shards(): grads = lax.all_to_all(packed, 'tile', 0, 0)  18.3 us
    all_to_all x1, blocking collectives, shards(): mine = lax.all_to_all(copies, CHIPS, 0, 0).reshape(features, features)  18.3 us
    pallas_call x7, Pallas kernels, call(): pl.pallas_call(functools.partial(body, **static), out_shape=outs, in_spec...  14.1 us
    ppermute x1, starting transfers between devices, shards(): back_in = lax.ppermute(core_pkt, 'core', swap)  10.8 us
    unnamed x44, local copies, waits for them, and re-layouts  7.02 us
    ppermute x2, waiting for transfers between devices, shards(): other = lax.ppermute(mine, 'row', swap)  5.56 us
  transfers between devices with their start and end apart: 12, of which 7 were waited for; matrix products, arithmetic and copies ran while one was open for 0% of the time, Pallas kernels for 3%

profile of v3, /device:TPU:0, one launch (start us, length us, event | category | flops | bytes accessed | tf_op | source)
XLA Modules:
  0.0 137.7 jit_solution(9064666615418134208)
XLA Ops:
  0.6 0.6 collective-permute-start
  1.2 0.7 collective-permute-start.1
  1.9 0.6 copy-done.18
  2.6 0.0 copy-done.16
  2.6 1.2 copy-done.2
  3.8 1.0 copy-done.11
  4.8 0.9 copy-done.12
  5.8 0.9 shard_map.182
  6.7 0.0 collective-permute-done.partner_ref
  6.7 0.0 collective-permute-done.1.far_ref
  6.7 0.0 copy-start.4
  6.7 1.9 %shard_map.183 = (bf16[1024,512]{1,0:T(8,128)(2,1)S(1)}, bf16[1024,512]{1,0:T(8,128)(2,1)S(1)}, bf16[200,512]{1,0:T(8,128)(2,1)S(1)}, bf16[136,512]{1,0:T(8,128)(2,1)S(1)}, f32[64,512]{1,0:T(8,128)S(1)}) custom-call(s32[1]{0:T(128)} %bitcast.dev_ref, bf16[128,512]{1,0:T(8,128)(2,1)S(1)} %collective-permute-done.partner_ref, ...), custom_call_target="tpu_custom_call" | custom-call | tf_op jit(solution)/shard_map/pallas_call | solution.py:433
  8.6 4.0 %collective-permute-start.2 = (bf16[200,512]{1,0:T(8,128)(2,1)S(1)}, bf16[200,512]{1,0:T(8,128)(2,1)S(1)}, u32[]{:S(2)}, u32[]{:S(2)}) collective-permute-start(bf16[200,512]{1,0:T(8,128)(2,1)S(1)} %get-tuple-element.45), channel_id=1, source_target_pairs={{0,1},{1,0},{2,3},{3,2},{4,5},{5,4},{6,7},{7,6},{8,9},{9,8},{10,11... | collective-permute-start | bytes 614408 | tf_op jit(solution)/shard_map/ppermute | solution.py:537
  12.6 1.1 collective-permute-done.2.core_ref
  13.7 1.5 %collective-permute-start.3 = (bf16[64,512]{1,0:T(8,128)(2,1)S(1)}, bf16[64,512]{1,0:T(8,128)(2,1)S(1)}, u32[]{:S(2)}, u32[]{:S(2)}) collective-permute-start(bf16[64,512]{1,0:T(8,128)(2,1)S(1)} %add_convert_fusion.3.mine_ref), channel_id=1, source_target_pairs={{0,2},{2,0},{1,3},{3,1},{4,6},{6,4},{5,7},{7,5},{8,10},{10,8},{9,1... | collective-permute-start | bytes 196616 | tf_op jit(solution)/shard_map/ppermute | solution.py:540
  15.2 2.9 %collective-permute-done.3.other_ref = bf16[64,512]{1,0:T(8,128)(2,1)S(1)} collective-permute-done((bf16[64,512]{1,0:T(8,128)(2,1)S(1)}, bf16[64,512]{1,0:T(8,128)(2,1)S(1)}, u32[]{:S(2)}, u32[]{:S(2)}) %collective-permute-start.3) | collective-permute-done | bytes 65568 | tf_op jit(solution)/shard_map/ppermute | solution.py:540
  18.1 0.2 shard_map.184
  18.3 0.0 copy-start.1
  18.3 20.8 %all_to_all.20.mine_ref = bf16[8,264,128]{2,1,0:T(8,128)(2,1)S(1)} all-to-all(bf16[8,264,128]{2,1,0:T(8,128)(2,1)S(1)} %shard_map.184), channel_id=1, replica_groups=mesh['tile'=8,'row'=2,'core'=2] {'tile'}, dimensions={0} | all-to-all | bytes 1081344 | tf_op jit(solution)/shard_map/all_to_all | solution.py:548
  39.1 0.0 collective-permute-start.4
  39.1 0.8 collective-permute-start.5
  39.9 1.1 collective-permute-done.4.other_ref
  41.1 5.5 %shard_map.185 = (bf16[128,512]{1,0:T(8,128)(2,1)}, f32[512,512]{1,0:T(8,128)S(1)}, f32[128,512]{1,0:T(8,128)S(1)}, f32[128,512]{1,0:T(8,128)S(1)}, bf16[128,512...) custom-call(s32[1]{0:T(128)} %bitcast.dev_ref, ...), custom_call_target="tpu_custom_call" | custom-call | tf_op jit(solution)/shard_map/pallas_call | solution.py:433
  46.6 0.7 collective-permute-start.6
  47.3 0.0 collective-permute-done.6.farin_ref
  47.3 0.2 shard_map.186
  47.6 10.8 %collective-permute-start.7 = (bf16[192,512]{1,0:T(8,128)(2,1)S(1)}, bf16[192,512]{1,0:T(8,128)(2,1)S(1)}, u32[]{:S(2)}, u32[]{:S(2)}) collective-permute-start(bf16[192,512]{1,0:T(8,128)(2,1)S(1)} %get-tuple-element.52), channel_id=1, source_target_pairs={{0,1},{1,0},{2,3},{3,2},{4,5},{5,4},{6,7},{7,6},{8,9},{9,8},{10,11... | collective-permute-start | bytes 589832 | tf_op jit(solution)/shard_map/ppermute | solution.py:611
  58.3 1.1 collective-permute-done.7.partnerin_ref
  59.4 3.0 %collective-permute-start.8 = (bf16[64,512]{1,0:T(8,128)(2,1)S(1)}, bf16[64,512]{1,0:T(8,128)(2,1)S(1)}, u32[]{:S(2)}, u32[]{:S(2)}) collective-permute-start(bf16[64,512]{1,0:T(8,128)(2,1)S(1)} %add_convert_fusion.2), channel_id=1, source_target_pairs={{0,2},{2,0},{1,3},{3,1},{4,6},{6,4},{5,7},{7,5},{8,10},{10,8},{9,1... | collective-permute-start | bytes 196616 | tf_op jit(solution)/shard_map/ppermute | solution.py:613
  62.4 2.6 %collective-permute-done.8 = bf16[64,512]{1,0:T(8,128)(2,1)S(1)} collective-permute-done((bf16[64,512]{1,0:T(8,128)(2,1)S(1)}, bf16[64,512]{1,0:T(8,128)(2,1)S(1)}, u32[]{:S(2)}, u32[]{:S(2)}) %collective-permute-start.8) | collective-permute-done | bytes 65568 | tf_op jit(solution)/shard_map/ppermute | solution.py:613
  65.1 18.3 %all_to_all.21.mine_ref = bf16[8,64,512]{2,1,0:T(8,128)(2,1)S(1)} all-to-all(bf16[8,64,512]{2,1,0:T(8,128)(2,1)S(1)} %broadcast_in_dim.39), channel_id=1, replica_groups=mesh['tile'=8,'row'=2,'core'=2] {'tile'}, dimensions={0} | all-to-all | bytes 1048576 | tf_op jit(solution)/shard_map/all_to_all | solution.py:616
  83.5 1.9 %collective-permute-done.9.other_ref = bf16[8,64,512]{2,1,0:T(8,128)(2,1)S(1)} collective-permute-done((bf16[8,64,512]{2,1,0:T(8,128)(2,1)S(1)}, bf16[8,64,512]{2,1,0:T(8,128)(2,1)S(1)}, u32[]{:S(2)}, u32[]{:S(2)}) %collective-permute-start.9) | collective-permute-done | bytes 524320 | tf_op jit(solution)/shard_map/ppermute | solution.py:617
  85.4 2.6 %shard_map.187 = (bf16[512,512]{1,0:T(8,128)(2,1)S(1)}, f32[512,512]{1,0:T(8,128)S(1)}, bf16[2,1,512,512]{3,2,1,0:T(8,128)(2,1)S(1)}, bf16[512,512]{1,0:T(8,128)(2,1)S(1)}, bf16[512,512]{1,0:T(8,128)(2,1)S(1)}) custom-call(s32[1]{0:T(128)} %bitcast.dev_ref, bf16[8,64,512]{2,1,0:T(8,128)(2,1)S(1)} %all_to_all.21.mine_ref, ...), custom_call_target="tpu_custom_call" | custom-call | tf_op jit(solution)/shard_map/pallas_call | solution.py:433
  88.0 0.0 copy-start.7
  88.1 0.0 copy-start.9
  88.1 0.2 collective-permute-start.10
  88.3 1.8 %collective-permute-done.10 = bf16[512,512]{1,0:T(8,128)(2,1)S(1)} collective-permute-done((bf16[512,512]{1,0:T(8,128)(2,1)S(1)}, bf16[512,512]{1,0:T(8,128)(2,1)S(1)}, u32[]{:S(2)}, u32[]{:S(2)}) %collective-permute-start.10) | collective-permute-done | bytes 524320 | tf_op jit(solution)/shard_map/ppermute | solution.py:651
  90.0 0.2 add_convert_fusion
  90.2 19.5 %all_to_all.22 = bf16[16,32,512]{2,1,0:T(8,128)(2,1)} all-to-all(bf16[16,32,512]{2,1,0:T(8,128)(2,1)S(1)} %bitcast.20), channel_id=1, replica_groups=mesh['tile'=8,'row'=2,'core'=2] {'tile','row'}, dimensions={0} | all-to-all | bytes 1048576 | tf_op jit(solution)/shard_map/all_to_all | solution.py:660
  109.8 1.1 reduce_sum.12
  110.9 18.3 %all_to_all.23 = bf16[16,32,512]{2,1,0:T(8,128)(2,1)} all-to-all(bf16[16,32,512]{2,1,0:T(8,128)(2,1)S(1)} %broadcast_in_dim.40), channel_id=1, replica_groups=mesh['tile'=8,'row'=2,'core'=2] {'tile','row'}, dimensions={0} | all-to-all | bytes 1048576 | tf_op jit(solution)/shard_map/all_to_all | solution.py:663
  129.2 0.0 collective-permute-start.11
  129.2 1.0 copy-done.6
  130.3 1.0 copy-done.8
  131.3 1.0 copy-done.10
  132.3 2.7 %shard_map.188 = (f32[512,512]{1,0:T(8,128)}, f32[512,512]{1,0:T(8,128)}) custom-call(s32[1]{0:T(128)} %bitcast.dev_ref, bf16[2,1,512,512]{3,2,1,0:T(8,128)(2,1)S(1)} %get-tuple-element.62.grad_ref, bf16[2,1,512,512]{3,2,1,0:T(8,128)(2,1)S(1)} %get-tuple-element.63.level_ref, bf16[2,1,512,512]{3,2,1,0:T(8,128)(2,1)S(1)} %get-tuple-element.53.middle_slope_ref, ...), custom_call_target="tpu_custom_call" | custom-call | tf_op jit(solution)/shard_map/pallas_call | solution.py:433
  135.0 0.0 collective-permute-done.11
  135.0 2.7 %select_convert_fusion = (f32[512,512]{1,0:T(8,128)}, f32[512,512]{1,0:T(8,128)}) fusion(bf16[512,512]{1,0:T(8,128)(2,1)} %collective-permute-done.11, pred[]{:T(512)S(6)} %eq.6, bf16[16,32,512]{2,1,0:T(8,128)(2,1)} %all_to_all.23), kind=kLoop, calls=%fused_computation.1 | loop fusion | flops 1048576 | bytes 3145729 | tf_op jit(solution)/shard_map/convert_element_type | solution.py:666
  (39 shorter events, 0.2 us)
Async XLA Ops:
  0.6 6.0 %collective-permute-start = (bf16[128,512]{1,0:T(8,128)(2,1)}, bf16[128,512]{1,0:T(8,128)(2,1)S(1)}, u32[]{:S(2)}, u32[]{:S(2)}) collective-permute-start(bf16[128,512]{1,0:T(8,128)(2,1)} %grid_ref.3), channel_id=1, source_target_pairs={{0,1},{1,0},{2,3},{3,2},{4,5},{5,4},{6,7},{7,6},{8,9},{9,8},{10,11... | collective-permute-start | bytes 393224 | tf_op jit(solution)/shard_map/ppermute | solution.py:489
  1.2 5.5 %collective-permute-start.1 = (bf16[128,512]{1,0:T(8,128)(2,1)}, bf16[128,512]{1,0:T(8,128)(2,1)S(1)}, u32[]{:S(2)}, u32[]{:S(2)}) collective-permute-start(bf16[128,512]{1,0:T(8,128)(2,1)} %grid_ref.3), channel_id=1, source_target_pairs={{1,2},{2,1},{3,4},{4,3},{5,6},{6,5},{7,8},{8,7},{9,10},{10,9},{11,... | collective-permute-start | bytes 393224 | tf_op jit(solution)/shard_map/ppermute | solution.py:488
  1.9 0.7 copy-start.18
  1.9 0.7 copy-start.16
  1.9 0.7 copy-start.17
  1.9 0.7 copy-start.21
  2.6 1.2 copy-start.2
  3.8 1.0 copy-start.11
  4.8 0.9 copy-start.12
  5.7 0.9 copy-start.14
  6.7 34.4 %copy-start.4 = (bf16[512,512]{1,0:T(8,128)(2,1)S(1)}, bf16[512,512]{1,0:T(8,128)(2,1)}, u32[]{:S(2)}) copy-start(bf16[512,512]{1,0:T(8,128)(2,1)} %decode_weight_ref.1) | copy-start | bytes 1572868
  8.6 5.0 %collective-permute-start.2 = (bf16[200,512]{1,0:T(8,128)(2,1)S(1)}, bf16[200,512]{1,0:T(8,128)(2,1)S(1)}, u32[]{:S(2)}, u32[]{:S(2)}) collective-permute-start(bf16[200,512]{1,0:T(8,128)(2,1)S(1)} %get-tuple-element.45), channel_id=1, source_target_pairs={{0,1},{1,0},{2,3},{3,2},{4,5},{5,4},{6,7},{7,6},{8,9},{9,8},{10,11... | collective-permute-start | bytes 614408 | tf_op jit(solution)/shard_map/ppermute | solution.py:537
  13.7 27.4 %copy-start.15 = (bf16[128,512]{1,0:T(8,128)(2,1)S(1)}, bf16[128,512]{1,0:T(8,128)(2,1)}, u32[]{:S(2)}) copy-start(bf16[128,512]{1,0:T(8,128)(2,1)} %cot_ref.1) | copy-start | bytes 393220
  13.7 4.4 %collective-permute-start.3 = (bf16[64,512]{1,0:T(8,128)(2,1)S(1)}, bf16[64,512]{1,0:T(8,128)(2,1)S(1)}, u32[]{:S(2)}, u32[]{:S(2)}) collective-permute-start(bf16[64,512]{1,0:T(8,128)(2,1)S(1)} %add_convert_fusion.3.mine_ref), channel_id=1, source_target_pairs={{0,2},{2,0},{1,3},{3,1},{4,6},{6,4},{5,7},{7,5},{8,10},{10,8},{9,1... | collective-permute-start | bytes 196616 | tf_op jit(solution)/shard_map/ppermute | solution.py:540
  18.1 22.9 %copy-start.3 = (bf16[512,512]{1,0:T(8,128)(2,1)S(1)}, bf16[512,512]{1,0:T(8,128)(2,1)}, u32[]{:S(2)}) copy-start(bf16[512,512]{1,0:T(8,128)(2,1)} %edges_ref.3) | copy-start | bytes 1572868
  18.1 22.9 %copy-start.13 = (bf16[128,512]{1,0:T(8,128)(2,1)S(1)}, bf16[128,512]{1,0:T(8,128)(2,1)}, u32[]{:S(2)}) copy-start(bf16[128,512]{1,0:T(8,128)(2,1)} %grid_ref.3) | copy-start | bytes 393220
  18.3 22.8 %copy-start = (bf16[512,512]{1,0:T(8,128)(2,1)S(1)}, bf16[512,512]{1,0:T(8,128)(2,1)}, u32[]{:S(2)}) copy-start(bf16[512,512]{1,0:T(8,128)(2,1)} %middle_weight_ref.3) | copy-start | bytes 1572868
  18.3 22.8 %copy-start.1 = (bf16[512,512]{1,0:T(8,128)(2,1)S(1)}, bf16[512,512]{1,0:T(8,128)(2,1)}, u32[]{:S(2)}) copy-start(bf16[512,512]{1,0:T(8,128)(2,1)} %summit_weight_ref.3) | copy-start | bytes 1572868
  39.1 1.9 %collective-permute-start.4 = (bf16[8,264,128]{2,1,0:T(8,128)(2,1)S(1)}, bf16[8,264,128]{2,1,0:T(8,128)(2,1)S(1)}, u32[]{:S(2)}, u32[]{:S(2)}) collective-permute-start(bf16[8,264,128]{2,1,0:T(8,128)(2,1)S(1)} %all_to_all.20.mine_ref), channel_id=1, source_target_pairs={{0,1},{1,0},{2,3},{3,2},{4,5},{5,4},{6,7},{7,6},{8,9},{9,8},{10,11... | collective-permute-start | bytes 1622024 | tf_op jit(solution)/shard_map/ppermute | solution.py:549
  39.1 2.0 %copy-start.20 = (s32[512]{0:T(512)S(1)}, s32[512]{0:T(512)}, u32[]{:S(2)}) copy-start(s32[512]{0:T(512)} %param.22) | copy-start | bytes 6148
  39.1 2.0 %copy-start.19 = (s32[512]{0:T(512)S(1)}, s32[512]{0:T(512)}, u32[]{:S(2)}) copy-start(s32[512]{0:T(512)} %param.21) | copy-start | bytes 6148
  39.1 0.8 collective-permute-start.5
  46.6 12.8 %copy-start.5 = (bf16[512,512]{1,0:T(8,128)(2,1)}, bf16[512,512]{1,0:T(8,128)(2,1)S(1)}, u32[]{:S(2)}) copy-start(bf16[512,512]{1,0:T(8,128)(2,1)S(1)} %get-tuple-element.64.summit_in_ref) | copy-start | bytes 1572868
  46.6 0.7 collective-permute-start.6
  47.6 11.8 %collective-permute-start.7 = (bf16[192,512]{1,0:T(8,128)(2,1)S(1)}, bf16[192,512]{1,0:T(8,128)(2,1)S(1)}, u32[]{:S(2)}, u32[]{:S(2)}) collective-permute-start(bf16[192,512]{1,0:T(8,128)(2,1)S(1)} %get-tuple-element.52), channel_id=1, source_target_pairs={{0,1},{1,0},{2,3},{3,2},{4,5},{5,4},{6,7},{7,6},{8,9},{9,8},{10,11... | collective-permute-start | bytes 589832 | tf_op jit(solution)/shard_map/ppermute | solution.py:611
  59.4 5.7 %collective-permute-start.8 = (bf16[64,512]{1,0:T(8,128)(2,1)S(1)}, bf16[64,512]{1,0:T(8,128)(2,1)S(1)}, u32[]{:S(2)}, u32[]{:S(2)}) collective-permute-start(bf16[64,512]{1,0:T(8,128)(2,1)S(1)} %add_convert_fusion.2), channel_id=1, source_target_pairs={{0,2},{2,0},{1,3},{3,1},{4,6},{6,4},{5,7},{7,5},{8,10},{10,8},{9,1... | collective-permute-start | bytes 196616 | tf_op jit(solution)/shard_map/ppermute | solution.py:613
  83.5 1.9 %collective-permute-start.9 = (bf16[8,64,512]{2,1,0:T(8,128)(2,1)S(1)}, bf16[8,64,512]{2,1,0:T(8,128)(2,1)S(1)}, u32[]{:S(2)}, u32[]{:S(2)}) collective-permute-start(bf16[8,64,512]{2,1,0:T(8,128)(2,1)S(1)} %all_to_all.21.mine_ref), channel_id=1, source_target_pairs={{0,1},{1,0},{2,3},{3,2},{4,5},{5,4},{6,7},{7,6},{8,9},{9,8},{10,11... | collective-permute-start | bytes 1572872 | tf_op jit(solution)/shard_map/ppermute | solution.py:617
  88.0 2.2 %copy-start.7 = (bf16[512,512]{1,0:T(8,128)(2,1)}, bf16[512,512]{1,0:T(8,128)(2,1)S(1)}, u32[]{:S(2)}) copy-start(bf16[512,512]{1,0:T(8,128)(2,1)S(1)} %get-tuple-element.65.top_ref) | copy-start | bytes 1572868
  88.1 2.2 %copy-start.9 = (bf16[512,512]{1,0:T(8,128)(2,1)}, bf16[512,512]{1,0:T(8,128)(2,1)S(1)}, u32[]{:S(2)}) copy-start(bf16[512,512]{1,0:T(8,128)(2,1)S(1)} %get-tuple-element.66.top_back_ref) | copy-start | bytes 1572868
  88.1 2.0 %collective-permute-start.10 = (bf16[512,512]{1,0:T(8,128)(2,1)S(1)}, bf16[512,512]{1,0:T(8,128)(2,1)S(1)}, u32[]{:S(2)}, u32[]{:S(2)}) collective-permute-start(bf16[512,512]{1,0:T(8,128)(2,1)S(1)} %get-tuple-element.61), channel_id=1, source_target_pairs={{0,1},{1,0},{2,3},{3,2},{4,5},{5,4},{6,7},{7,6},{8,9},{9,8},{10,11... | collective-permute-start | bytes 1572872 | tf_op jit(solution)/shard_map/ppermute | solution.py:651
  129.2 5.8 %collective-permute-start.11 = (bf16[512,512]{1,0:T(8,128)(2,1)}, bf16[512,512]{1,0:T(8,128)(2,1)}, u32[]{:S(2)}, u32[]{:S(2)}) collective-permute-start(bf16[512,512]{1,0:T(8,128)(2,1)} %bitcast.8), channel_id=1, source_target_pairs={{0,1},{1,0},{2,3},{3,2},{4,5},{5,4},{6,7},{7,6},{8,9},{9,8},{10,11... | collective-permute-start | bytes 1572872 | tf_op jit(solution)/shard_map/ppermute | solution.py:664
  129.2 1.0 copy-start.6
  130.2 1.0 copy-start.8
  131.3 1.0 copy-start.10

commit v4 on v3

--- a/solution.py
+++ b/solution.py
@@ -11,8 +11,9 @@
 TOP_NODES = 512
 LANES = 128
 WORKING_BYTES = 10 * 2**20
-ALL = ("tile", "row", "core")
-CHIPS = ("tile", "row")
+TILE = ("half", "near")
+ALL = TILE + ("row", "core")
+NEAR = ("near", "row")
 BF16 = jnp.bfloat16
 F32 = jnp.float32
 I32 = jnp.int32
@@ -192,7 +193,6 @@
     core_ref,
     farpkt_ref,
     farin_ref,
-    grid_ref,
     cot_ref,
     edges_ref,
     source_ref,
@@ -200,8 +200,9 @@
     decode_weight_ref,
     middle_weight_ref,
     summit_weight_ref,
-    update_ref,
-    dgrad_ref,
+    fetched_ref,
+    slope_ref,
+    act_ref,
     own_ref,
     partner_ref,
     far_ref,
@@ -221,7 +222,7 @@
     core = device % 2
     tile = device // subs
     tiles, _, lanes = mine_ref.shape
-    features = grid_ref.shape[1]
+    features = cot_ref.shape[1]
     strips = features // lanes
     half = level_rows // 2
     group = min(features // half, tiles)
@@ -285,19 +286,30 @@
     fetched = mm(cols_onehot(place, 3 * rows), wide).astype(BF16)
     pre = mm(fetched, decode_weight_ref[...]) + edges_ref[...].astype(F32)
     sig = sigmoid(pre)
-    grid_rows = grid_ref.shape[0]
+    grid_rows = cot_ref.shape[0]
     raw = target_ref[...]
     aimed = jnp.where(raw >= 0, raw - device * grid_rows, -1)
-    summed = mm(rows_onehot(aimed, grid_rows), (pre * sig).astype(BF16))
-    update_ref[...] = (grid_ref[...].astype(F32) + decode_factor * summed).astype(BF16)
+    fetched_ref[...] = fetched
+    act_ref[...] = (pre * sig).astype(BF16)
     incoming = mm(cols_onehot(aimed, grid_rows), cot_ref[...]) * decode_factor
     slope = (incoming * (sig * (1.0 + pre * (1.0 - sig)))).astype(BF16)
-    dgrad_ref[...] = mm_tn(fetched, slope)
+    slope_ref[...] = slope
     gathered = mm(rows_onehot(place, 3 * rows), slope).astype(BF16)
     returned = mm_nt(gathered, decode_weight_ref[...])
     own_ref[...] = returned[:rows]
     partner_ref[...] = returned[rows : 2 * rows]
     far_ref[...] = returned[2 * rows :].astype(BF16)
+
+
+def update_kernel(
+    dev_ref, grid_ref, target_ref, act_ref, fetched_ref, slope_ref, update_ref, dgrad_ref, *, factor
+):
+    grid_rows = grid_ref.shape[0]
+    raw = target_ref[...]
+    aimed = jnp.where(raw >= 0, raw - dev_ref[0] * grid_rows, -1)
+    summed = mm(rows_onehot(aimed, grid_rows), act_ref[...])
+    update_ref[...] = (grid_ref[...].astype(F32) + factor * summed).astype(BF16)
+    dgrad_ref[...] = mm_tn(fetched_ref[...], slope_ref[...])
 
 
 def level_kernel(
@@ -401,17 +413,13 @@
     grad_ref,
     level_ref,
     middle_slope_ref,
-    summit_in_ref,
-    top_ref,
     top_back_ref,
     ids_ref,
     middle_grad_ref,
-    summit_grad_ref,
     *,
     summit_factor,
 ):
     _, groups, _, features = grad_ref.shape
-    summit_grad_ref[...] = mm_tn(summit_in_ref[...], top_ref[...])
     middle_grad = jnp.zeros((features, features), F32)
     for g in range(groups):
         for h in range(2):
@@ -420,6 +428,10 @@
             slope = (level_total * middle_slope_ref[h, g].astype(F32)).astype(BF16)
             middle_grad = middle_grad + mm_tn(level_ref[h, g], slope)
     middle_grad_ref[...] = middle_grad
+
+
+def top_kernel(dev_ref, summit_in_ref, top_ref, summit_grad_ref):
+    summit_grad_ref[...] = mm_tn(summit_in_ref[...], top_ref[...])
 
 
 def call(body, outs, args, scratch=(), **static):
@@ -465,10 +477,10 @@
     mesh_rows = mesh_feats.shape[0]
     level_rows = owner_coarse.shape[0]
     half = level_rows // 2
-    tiles = lax.axis_size("tile")
+    tiles = lax.axis_size(TILE)
     subs = lax.axis_size("row") * lax.axis_size("core")
     devices = tiles * subs
-    chips = devices // 2
+    peers = devices // 4
     edges = encode_source.shape[0]
     swap = [(0, 1), (1, 0)]
     beside = []
@@ -545,12 +557,13 @@
         subs=subs,
         factor=middle_factor,
     )
-    mids = lax.all_to_all(packed, "tile", 0, 0)
+    mids = lax.all_to_all(packed, TILE, 0, 0)
     mids_other = lax.ppermute(mids, "core", swap)
     full = (2, groups, chunk, features)
     (
-        grid_update,
-        dgrad,
+        decode_fetched,
+        decode_slope,
+        decode_act,
         own,
         partner,
         far,
@@ -562,8 +575,9 @@
     ) = call(
         middle_kernel,
         [
-            shape((rows, features), BF16),
-            shape((features, features), F32),
+            shape(decode_edges.shape, BF16),
+            shape(decode_edges.shape, BF16),
+            shape(decode_edges.shape, BF16),
             shape((mesh_rows, features), F32),
             shape((mesh_rows, features), F32),
             shape((mesh_rows, features), BF16),
@@ -580,7 +594,6 @@
             core_in,
             far_pkt,
             far_in,
-            grid_feats,
             cotangent,
             decode_edges,
             decode_source[None],
@@ -598,6 +611,19 @@
         decode_factor=decode_factor,
     )
     far_back = lax.ppermute(far, ALL, beside)
+    grid_update, dgrad = call(
+        update_kernel,
+        [shape((rows, features), BF16), shape((features, features), F32)],
+        [
+            dev,
+            grid_feats,
+            decode_target[None],
+            decode_act,
+            decode_fetched,
+            decode_slope,
+        ],
+        factor=decode_factor,
+    )
     grad_sum, core_pkt, keep = call(
         level_kernel,
         [
@@ -613,7 +639,7 @@
     other = lax.ppermute(mine, "row", swap)
     total = (mine.astype(F32) + other.astype(F32)).astype(BF16)
     packed = jnp.broadcast_to(total[None], (tiles, half, features))
-    grads = lax.all_to_all(packed, "tile", 0, 0)
+    grads = lax.all_to_all(packed, TILE, 0, 0)
     grads_other = lax.ppermute(grads, "core", swap)
     send, keep, level_back, top, top_back = call(
         back_kernel,
@@ -649,19 +675,24 @@
         encode_factor=encode_factor,
     )
     received = lax.ppermute(send, "core", swap)
-    middle_grad, summit_grad = call(
+    middle_grad = call(
         late_kernel,
-        [shape((features, features), F32), shape((features, features), F32)],
-        [dev, level_back, level, middle_slope, summit_in, top, top_back, ids],
+        shape((features, features), F32),
+        [dev, level_back, level, middle_slope, top_back, ids],
         summit_factor=summit_factor,
     )
     share = (keep + received.astype(F32)).astype(BF16)
-    share = share.reshape(chips, features // chips, features)
-    parts = lax.all_to_all(share, CHIPS, 0, 0)
-    summed = jnp.sum(parts.astype(F32), axis=0).astype(BF16)
+    share = share.reshape(peers, features // peers, features)
+    parts = lax.all_to_all(share, NEAR, 0, 0)
+    near = jnp.sum(parts.astype(F32), axis=0).astype(BF16)
+    away = lax.ppermute(near, "half", swap)
+    summed = (near.astype(F32) + away.astype(F32)).astype(BF16)
     copies = jnp.broadcast_to(summed[None], parts.shape)
-    mine = lax.all_to_all(copies, CHIPS, 0, 0).reshape(features, features)
+    mine = lax.all_to_all(copies, NEAR, 0, 0).reshape(features, features)
     other = lax.ppermute(mine, "core", swap)
+    summit_grad = call(
+        top_kernel, shape((features, features), F32), [dev, summit_in, top]
+    )
     encode_grad = jnp.where(core == 0, mine, other).astype(F32)
     decode_grad = jnp.where(core == 0, other, mine).astype(F32)
     return (grid_update, encode_grad, decode_grad, middle_grad, summit_grad)
@@ -669,7 +700,7 @@
 
 def solution(mesh):
     tiles, subs = mesh.devices.shape
-    fine = Mesh(mesh.devices.reshape(tiles, subs // 2, 2), ALL)
+    fine = Mesh(mesh.devices.reshape(2, tiles // 2, subs // 2, 2), ALL)
     placed = (
         P(ALL, None),
         P(ALL, None),
@@ -680,7 +711,7 @@
         P(ALL),
         P(ALL),
         P(ALL),
-        P("tile"),
+        P(TILE),
         P(),
         P(),
         P(),

time: 138 us -> 130 us (0.942)
  blocking collectives: 77 us -> 63.5 us
  waiting for transfers between devices: 12.5 us -> 16.2 us
    all_to_all x4, blocking collectives: 77 us -> 63.5 us  [the longest x1 20.8 us: shards(): mids = lax.all_to_all(packed, TILE, 0, 0)]
    ppermute x0 -> x1, waiting for transfers between devices: none -> 4.62 us  [shards(): away = lax.ppermute(near, 'half', swap)]
    pallas_call x7 -> x9, Pallas kernels: 14.1 us -> 15.1 us  [call(): pl.pallas_call(functools.partial(body, **static), out_shape=outs, in_spec...]
  transfers between devices with their start and end apart: 12 -> 13, of which waited for: 7 -> 8; matrix products, arithmetic and copies ran while one was open for 0% -> 0% of each run, Pallas kernels for 3% -> 4%
where the time goes in v4:
time: 130 us; the launch traced here: 129 us
  blocking collectives  63.5 us (49%)
  starting transfers between devices  23.4 us (18%)
  waiting for transfers between devices  16.2 us (12%)
  Pallas kernels  15.1 us (12%)
  local copies, waits for them, and re-layouts  6.07 us (5%)
  other arithmetic  4 us (3%)
    all_to_all x1, blocking collectives, shards(): mids = lax.all_to_all(packed, TILE, 0, 0)  20.8 us
    all_to_all x1, blocking collectives, shards(): grads = lax.all_to_all(packed, TILE, 0, 0)  18.5 us
    pallas_call x9, Pallas kernels, call(): pl.pallas_call(functools.partial(body, **static), out_shape=outs, in_spec...  15.1 us
    all_to_all x1, blocking collectives, shards(): parts = lax.all_to_all(share, NEAR, 0, 0)  13.1 us
    all_to_all x1, blocking collectives, shards(): mine = lax.all_to_all(copies, NEAR, 0, 0).reshape(features, features)  11.1 us
    ppermute x1, starting transfers between devices, shards(): back_in = lax.ppermute(core_pkt, 'core', swap)  10.7 us
    unnamed x44, local copies, waits for them, and re-layouts  5.99 us
    ppermute x2, waiting for transfers between devices, shards(): other = lax.ppermute(mine, 'row', swap)  5.56 us
  transfers between devices with their start and end apart: 13, of which 8 were waited for; matrix products, arithmetic and copies ran while one was open for 0% of the time, Pallas kernels for 4%

profile of v4, /device:TPU:0, one launch (start us, length us, event | category | flops | bytes accessed | tf_op | source)
XLA Modules:
  0.0 129.3 jit_solution(15281385781564509449)
XLA Ops:
  0.6 0.6 collective-permute-start
  1.2 0.7 collective-permute-start.1
  1.9 0.6 copy-done.19
  2.6 0.0 copy-done.16
  2.6 1.2 copy-done.2
  3.8 1.0 copy-done.11
  4.8 0.9 copy-done.12
  5.8 0.9 shard_map.182
  6.7 0.0 collective-permute-done.partner_ref
  6.7 0.0 copy-start.4
  6.7 1.9 %shard_map.183 = (bf16[1024,512]{1,0:T(8,128)(2,1)S(1)}, bf16[1024,512]{1,0:T(8,128)(2,1)S(1)}, bf16[200,512]{1,0:T(8,128)(2,1)S(1)}, bf16[136,512]{1,0:T(8,128)(2,1)S(1)}, f32[64,512]{1,0:T(8,128)S(1)}) custom-call(s32[1]{0:T(128)} %bitcast.dev_ref, bf16[128,512]{1,0:T(8,128)(2,1)S(1)} %collective-permute-done.partner_ref, ...), custom_call_target="tpu_custom_call" | custom-call | tf_op jit(solution)/shard_map/pallas_call | solution.py:445
  8.6 4.0 %collective-permute-start.2 = (bf16[200,512]{1,0:T(8,128)(2,1)S(1)}, bf16[200,512]{1,0:T(8,128)(2,1)S(1)}, u32[]{:S(2)}, u32[]{:S(2)}) collective-permute-start(bf16[200,512]{1,0:T(8,128)(2,1)S(1)} %get-tuple-element.46), channel_id=1, source_target_pairs={{0,1},{1,0},{2,3},{3,2},{4,5},{5,4},{6,7},{7,6},{8,9},{9,8},{10,11... | collective-permute-start | bytes 614408 | tf_op jit(solution)/shard_map/ppermute | solution.py:549
  12.6 1.1 collective-permute-done.2.core_ref
  13.7 1.5 %collective-permute-start.3 = (bf16[64,512]{1,0:T(8,128)(2,1)S(1)}, bf16[64,512]{1,0:T(8,128)(2,1)S(1)}, u32[]{:S(2)}, u32[]{:S(2)}) collective-permute-start(bf16[64,512]{1,0:T(8,128)(2,1)S(1)} %add_convert_fusion.4.mine_ref), channel_id=1, source_target_pairs={{0,2},{2,0},{1,3},{3,1},{4,6},{6,4},{5,7},{7,5},{8,10},{10,8},{9,1... | collective-permute-start | bytes 196616 | tf_op jit(solution)/shard_map/ppermute | solution.py:552
  15.2 2.9 %collective-permute-done.3.other_ref = bf16[64,512]{1,0:T(8,128)(2,1)S(1)} collective-permute-done((bf16[64,512]{1,0:T(8,128)(2,1)S(1)}, bf16[64,512]{1,0:T(8,128)(2,1)S(1)}, u32[]{:S(2)}, u32[]{:S(2)}) %collective-permute-start.3) | collective-permute-done | bytes 65568 | tf_op jit(solution)/shard_map/ppermute | solution.py:552
  18.1 0.2 shard_map.184
  18.3 0.0 copy-start.1
  18.3 20.8 %all_to_all.20.mine_ref = bf16[8,264,128]{2,1,0:T(8,128)(2,1)S(1)} all-to-all(bf16[8,264,128]{2,1,0:T(8,128)(2,1)S(1)} %shard_map.184), channel_id=1, replica_groups=mesh['half'=2,'near'=4,'row'=2,'core'=2] {'half','near'}, dimensions={0} | all-to-all | bytes 1081344 | tf_op jit(solution)/shard_map/all_to_all | solution.py:560
  39.1 0.8 collective-permute-start.5
  39.9 1.1 collective-permute-done.4.other_ref
  41.1 4.5 %shard_map.185 = (bf16[512,512]{1,0:T(8,128)(2,1)S(1)}, bf16[512,512]{1,0:T(8,128)(2,1)S(1)}, bf16[512,512]{1,0:T(8,128)(2,1)S(1)}, f32[128,512]{1,0:T(8,128)S(1...) custom-call(s32[1]{0:T(128)} %bitcast.dev_ref, ...), custom_call_target="tpu_custom_call" | custom-call | tf_op jit(solution)/shard_map/pallas_call | solution.py:445
  45.6 0.0 copy-start.5
  45.6 0.7 collective-permute-start.6
  46.3 0.2 shard_map.187
  46.6 10.7 %collective-permute-start.7 = (bf16[192,512]{1,0:T(8,128)(2,1)S(1)}, bf16[192,512]{1,0:T(8,128)(2,1)S(1)}, u32[]{:S(2)}, u32[]{:S(2)}) collective-permute-start(bf16[192,512]{1,0:T(8,128)(2,1)S(1)} %get-tuple-element.56), channel_id=1, source_target_pairs={{0,1},{1,0},{2,3},{3,2},{4,5},{5,4},{6,7},{7,6},{8,9},{9,8},{10,11... | collective-permute-start | bytes 589832 | tf_op jit(solution)/shard_map/ppermute | solution.py:637
  57.3 1.1 collective-permute-done.7.partnerin_ref
  58.4 3.0 %collective-permute-start.8 = (bf16[64,512]{1,0:T(8,128)(2,1)S(1)}, bf16[64,512]{1,0:T(8,128)(2,1)S(1)}, u32[]{:S(2)}, u32[]{:S(2)}) collective-permute-start(bf16[64,512]{1,0:T(8,128)(2,1)S(1)} %add_convert_fusion.3), channel_id=1, source_target_pairs={{0,2},{2,0},{1,3},{3,1},{4,6},{6,4},{5,7},{7,5},{8,10},{10,8},{9,1... | collective-permute-start | bytes 196616 | tf_op jit(solution)/shard_map/ppermute | solution.py:639
  61.5 2.6 %collective-permute-done.8 = bf16[64,512]{1,0:T(8,128)(2,1)S(1)} collective-permute-done((bf16[64,512]{1,0:T(8,128)(2,1)S(1)}, bf16[64,512]{1,0:T(8,128)(2,1)S(1)}, u32[]{:S(2)}, u32[]{:S(2)}) %collective-permute-start.8) | collective-permute-done | bytes 65568 | tf_op jit(solution)/shard_map/ppermute | solution.py:639
  64.2 0.0 copy-start.13
  64.2 18.5 %all_to_all.21.mine_ref = bf16[8,64,512]{2,1,0:T(8,128)(2,1)S(1)} all-to-all(bf16[8,64,512]{2,1,0:T(8,128)(2,1)S(1)} %broadcast_in_dim.40), channel_id=1, replica_groups=mesh['half'=2,'near'=4,'row'=2,'core'=2] {'half','near'}, dimensions={0} | all-to-all | bytes 1048576 | tf_op jit(solution)/shard_map/all_to_all | solution.py:642
  82.7 0.9 shard_map.186
  83.6 1.0 collective-permute-done.9.other_ref
  84.6 2.6 %shard_map.188 = (bf16[512,512]{1,0:T(8,128)(2,1)S(1)}, f32[512,512]{1,0:T(8,128)S(1)}, bf16[2,1,512,512]{3,2,1,0:T(8,128)(2,1)S(1)}, bf16[512,512]{1,0:T(8,128)(2,1)S(1)}, bf16[512,512]{1,0:T(8,128)(2,1)S(1)}) custom-call(s32[1]{0:T(128)} %bitcast.dev_ref, bf16[8,64,512]{2,1,0:T(8,128)(2,1)S(1)} %all_to_all.21.mine_ref, ...), custom_call_target="tpu_custom_call" | custom-call | tf_op jit(solution)/shard_map/pallas_call | solution.py:445
  87.2 0.0 copy-start.7
  87.2 0.0 copy-start.9
  87.2 0.2 collective-permute-start.10
  87.4 1.8 %collective-permute-done.10 = bf16[512,512]{1,0:T(8,128)(2,1)S(1)} collective-permute-done((bf16[512,512]{1,0:T(8,128)(2,1)S(1)}, bf16[512,512]{1,0:T(8,128)(2,1)S(1)}, u32[]{:S(2)}, u32[]{:S(2)}) %collective-permute-start.10) | collective-permute-done | bytes 524320 | tf_op jit(solution)/shard_map/ppermute | solution.py:677
  89.2 0.2 add_convert_fusion
  89.4 13.1 %all_to_all.22 = bf16[8,64,512]{2,1,0:T(8,128)(2,1)} all-to-all(bf16[8,64,512]{2,1,0:T(8,128)(2,1)S(1)} %bitcast.21), channel_id=1, replica_groups=mesh['half'=2,'near'=4,'row'=2,'core'=2] {'near','row'}, dimensions={0} | all-to-all | bytes 1048576 | tf_op jit(solution)/shard_map/all_to_all | solution.py:686
  102.5 1.1 reduce_sum.12
  103.6 1.3 %collective-permute-start.11 = (bf16[64,512]{1,0:T(8,128)(2,1)S(1)}, bf16[64,512]{1,0:T(8,128)(2,1)S(1)}, u32[]{:S(2)}, u32[]{:S(2)}) collective-permute-start(bf16[64,512]{1,0:T(8,128)(2,1)S(1)} %reduce_sum.12), channel_id=1, source_target_pairs={{0,16},{16,0},{1,17},{17,1},{2,18},{18,2},{3,19},{19,3},{4,20},{20... | collective-permute-start | bytes 196616 | tf_op jit(solution)/shard_map/ppermute | solution.py:688
  104.9 4.6 %collective-permute-done.11 = bf16[64,512]{1,0:T(8,128)(2,1)S(1)} collective-permute-done((bf16[64,512]{1,0:T(8,128)(2,1)S(1)}, bf16[64,512]{1,0:T(8,128)(2,1)S(1)}, u32[]{:S(2)}, u32[]{:S(2)}) %collective-permute-start.11) | collective-permute-done | bytes 65568 | tf_op jit(solution)/shard_map/ppermute | solution.py:688
  109.6 11.1 %all_to_all.23 = bf16[8,64,512]{2,1,0:T(8,128)(2,1)} all-to-all(bf16[8,64,512]{2,1,0:T(8,128)(2,1)S(1)} %broadcast_in_dim.41), channel_id=1, replica_groups=mesh['half'=2,'near'=4,'row'=2,'core'=2] {'near','row'}, dimensions={0} | all-to-all | bytes 1048576 | tf_op jit(solution)/shard_map/all_to_all | solution.py:691
  120.7 1.0 copy-done.6
  121.8 1.0 copy-done.10
  122.8 1.4 %shard_map.190 = f32[512,512]{1,0:T(8,128)} custom-call(s32[1]{0:T(128)} %bitcast.dev_ref, bf16[512,512]{1,0:T(8,128)(2,1)S(1)} %copy-done.6, bf16[512,512]{1,0:T(8,128)(2,1)S(1)} %copy-done.10), custom_call_target="tpu_custom_call" | custom-call | tf_op jit(solution)/shard_map/pallas_call | solution.py:445
  124.2 2.4 %shard_map.189 = f32[512,512]{1,0:T(8,128)} custom-call(s32[1]{0:T(128)} %bitcast.dev_ref, bf16[2,1,512,512]{3,2,1,0:T(8,128)(2,1)S(1)} %get-tuple-element.66.grad_ref, bf16[2,1,512,512]{3,2,1,0:T(8,128)(2,1)S(1)} %get-tuple-element.67.level_ref, bf16[2,1,512,512]{3,2,1,0:T(8,128)(2,1)S(1)} %get-tuple-element.57.middle_slope_ref, ...), custom_call_target="tpu_custom_call" | custom-call | tf_op jit(solution)/shard_map/pallas_call | solution.py:445
  126.6 2.7 %select_convert_fusion = (f32[512,512]{1,0:T(8,128)}, f32[512,512]{1,0:T(8,128)}) fusion(bf16[512,512]{1,0:T(8,128)(2,1)} %collective-permute-done.12, pred[]{:T(512)S(6)} %eq.6, bf16[8,64,512]{2,1,0:T(8,128)(2,1)} %all_to_all.23), kind=kLoop, calls=%fused_computation.1 | loop fusion | flops 1048576 | bytes 3145729 | tf_op jit(solution)/shard_map/convert_element_type | solution.py:697
  (44 shorter events, 0.2 us)
Async XLA Ops:
  0.6 6.0 %collective-permute-start = (bf16[128,512]{1,0:T(8,128)(2,1)}, bf16[128,512]{1,0:T(8,128)(2,1)S(1)}, u32[]{:S(2)}, u32[]{:S(2)}) collective-permute-start(bf16[128,512]{1,0:T(8,128)(2,1)} %grid_ref.3), channel_id=1, source_target_pairs={{0,1},{1,0},{2,3},{3,2},{4,5},{5,4},{6,7},{7,6},{8,9},{9,8},{10,11... | collective-permute-start | bytes 393224 | tf_op jit(solution)/shard_map/ppermute | solution.py:501
  1.2 5.5 %collective-permute-start.1 = (bf16[128,512]{1,0:T(8,128)(2,1)}, bf16[128,512]{1,0:T(8,128)(2,1)S(1)}, u32[]{:S(2)}, u32[]{:S(2)}) collective-permute-start(bf16[128,512]{1,0:T(8,128)(2,1)} %grid_ref.3), channel_id=1, source_target_pairs={{1,2},{2,1},{3,4},{4,3},{5,6},{6,5},{7,8},{8,7},{9,10},{10,9},{11,... | collective-permute-start | bytes 393224 | tf_op jit(solution)/shard_map/ppermute | solution.py:500
  1.9 0.7 copy-start.19
  1.9 0.7 copy-start.16
  1.9 0.7 copy-start.18
  1.9 0.7 copy-start.21
  2.6 1.2 copy-start.2
  3.8 1.0 copy-start.11
  4.8 0.9 copy-start.12
  5.8 1.0 copy-start.14
  6.7 34.3 %copy-start.4 = (bf16[512,512]{1,0:T(8,128)(2,1)S(1)}, bf16[512,512]{1,0:T(8,128)(2,1)}, u32[]{:S(2)}) copy-start(bf16[512,512]{1,0:T(8,128)(2,1)} %decode_weight_ref.1) | copy-start | bytes 1572868
  8.6 5.0 %collective-permute-start.2 = (bf16[200,512]{1,0:T(8,128)(2,1)S(1)}, bf16[200,512]{1,0:T(8,128)(2,1)S(1)}, u32[]{:S(2)}, u32[]{:S(2)}) collective-permute-start(bf16[200,512]{1,0:T(8,128)(2,1)S(1)} %get-tuple-element.46), channel_id=1, source_target_pairs={{0,1},{1,0},{2,3},{3,2},{4,5},{5,4},{6,7},{7,6},{8,9},{9,8},{10,11... | collective-permute-start | bytes 614408 | tf_op jit(solution)/shard_map/ppermute | solution.py:549
  13.7 4.4 %collective-permute-start.3 = (bf16[64,512]{1,0:T(8,128)(2,1)S(1)}, bf16[64,512]{1,0:T(8,128)(2,1)S(1)}, u32[]{:S(2)}, u32[]{:S(2)}) collective-permute-start(bf16[64,512]{1,0:T(8,128)(2,1)S(1)} %add_convert_fusion.4.mine_ref), channel_id=1, source_target_pairs={{0,2},{2,0},{1,3},{3,1},{4,6},{6,4},{5,7},{7,5},{8,10},{10,8},{9,1... | collective-permute-start | bytes 196616 | tf_op jit(solution)/shard_map/ppermute | solution.py:552
  18.1 22.9 %copy-start.3 = (bf16[512,512]{1,0:T(8,128)(2,1)S(1)}, bf16[512,512]{1,0:T(8,128)(2,1)}, u32[]{:S(2)}) copy-start(bf16[512,512]{1,0:T(8,128)(2,1)} %edges_ref.3) | copy-start | bytes 1572868
  18.1 22.9 %copy-start.15 = (bf16[128,512]{1,0:T(8,128)(2,1)S(1)}, bf16[128,512]{1,0:T(8,128)(2,1)}, u32[]{:S(2)}) copy-start(bf16[128,512]{1,0:T(8,128)(2,1)} %cot_ref.1) | copy-start | bytes 393220
  18.3 22.8 %copy-start = (bf16[512,512]{1,0:T(8,128)(2,1)S(1)}, bf16[512,512]{1,0:T(8,128)(2,1)}, u32[]{:S(2)}) copy-start(bf16[512,512]{1,0:T(8,128)(2,1)} %middle_weight_ref.3) | copy-start | bytes 1572868
  18.3 22.8 %copy-start.1 = (bf16[512,512]{1,0:T(8,128)(2,1)S(1)}, bf16[512,512]{1,0:T(8,128)(2,1)}, u32[]{:S(2)}) copy-start(bf16[512,512]{1,0:T(8,128)(2,1)} %summit_weight_ref.3) | copy-start | bytes 1572868
  39.1 1.9 %collective-permute-start.4 = (bf16[8,264,128]{2,1,0:T(8,128)(2,1)S(1)}, bf16[8,264,128]{2,1,0:T(8,128)(2,1)S(1)}, u32[]{:S(2)}, u32[]{:S(2)}) collective-permute-start(bf16[8,264,128]{2,1,0:T(8,128)(2,1)S(1)} %all_to_all.20.mine_ref), channel_id=1, source_target_pairs={{0,1},{1,0},{2,3},{3,2},{4,5},{5,4},{6,7},{7,6},{8,9},{9,8},{10,11... | collective-permute-start | bytes 1622024 | tf_op jit(solution)/shard_map/ppermute | solution.py:561
  39.1 2.0 %copy-start.20 = (s32[512]{0:T(512)S(1)}, s32[512]{0:T(512)}, u32[]{:S(2)}) copy-start(s32[512]{0:T(512)} %param.21) | copy-start | bytes 6148
  39.1 2.0 %copy-start.17 = (s32[512]{0:T(512)S(1)}, s32[512]{0:T(512)}, u32[]{:S(2)}) copy-start(s32[512]{0:T(512)} %param.22) | copy-start | bytes 6148
  39.1 0.8 collective-permute-start.5
  45.6 12.8 %copy-start.5 = (bf16[512,512]{1,0:T(8,128)(2,1)}, bf16[512,512]{1,0:T(8,128)(2,1)S(1)}, u32[]{:S(2)}) copy-start(bf16[512,512]{1,0:T(8,128)(2,1)S(1)} %get-tuple-element.69.summit_in_ref) | copy-start | bytes 1572868
  45.6 0.7 collective-permute-start.6
  46.6 11.8 %collective-permute-start.7 = (bf16[192,512]{1,0:T(8,128)(2,1)S(1)}, bf16[192,512]{1,0:T(8,128)(2,1)S(1)}, u32[]{:S(2)}, u32[]{:S(2)}) collective-permute-start(bf16[192,512]{1,0:T(8,128)(2,1)S(1)} %get-tuple-element.56), channel_id=1, source_target_pairs={{0,1},{1,0},{2,3},{3,2},{4,5},{5,4},{6,7},{7,6},{8,9},{9,8},{10,11... | collective-permute-start | bytes 589832 | tf_op jit(solution)/shard_map/ppermute | solution.py:637
  58.4 5.7 %collective-permute-start.8 = (bf16[64,512]{1,0:T(8,128)(2,1)S(1)}, bf16[64,512]{1,0:T(8,128)(2,1)S(1)}, u32[]{:S(2)}, u32[]{:S(2)}) collective-permute-start(bf16[64,512]{1,0:T(8,128)(2,1)S(1)} %add_convert_fusion.3), channel_id=1, source_target_pairs={{0,2},{2,0},{1,3},{3,1},{4,6},{6,4},{5,7},{7,5},{8,10},{10,8},{9,1... | collective-permute-start | bytes 196616 | tf_op jit(solution)/shard_map/ppermute | solution.py:639
  64.2 18.5 %copy-start.13 = (bf16[128,512]{1,0:T(8,128)(2,1)S(1)}, bf16[128,512]{1,0:T(8,128)(2,1)}, u32[]{:S(2)}) copy-start(bf16[128,512]{1,0:T(8,128)(2,1)} %grid_ref.3) | copy-start | bytes 393220
  82.6 1.9 %collective-permute-start.9 = (bf16[8,64,512]{2,1,0:T(8,128)(2,1)S(1)}, bf16[8,64,512]{2,1,0:T(8,128)(2,1)S(1)}, u32[]{:S(2)}, u32[]{:S(2)}) collective-permute-start(bf16[8,64,512]{2,1,0:T(8,128)(2,1)S(1)} %all_to_all.21.mine_ref), channel_id=1, source_target_pairs={{0,1},{1,0},{2,3},{3,2},{4,5},{5,4},{6,7},{7,6},{8,9},{9,8},{10,11... | collective-permute-start | bytes 1572872 | tf_op jit(solution)/shard_map/ppermute | solution.py:643
  87.2 2.2 %copy-start.7 = (bf16[512,512]{1,0:T(8,128)(2,1)}, bf16[512,512]{1,0:T(8,128)(2,1)S(1)}, u32[]{:S(2)}) copy-start(bf16[512,512]{1,0:T(8,128)(2,1)S(1)} %get-tuple-element.68.top_back_ref) | copy-start | bytes 1572868
  87.2 2.2 %copy-start.9 = (bf16[512,512]{1,0:T(8,128)(2,1)}, bf16[512,512]{1,0:T(8,128)(2,1)S(1)}, u32[]{:S(2)}) copy-start(bf16[512,512]{1,0:T(8,128)(2,1)S(1)} %get-tuple-element.70.top_ref) | copy-start | bytes 1572868
  87.2 2.0 %collective-permute-start.10 = (bf16[512,512]{1,0:T(8,128)(2,1)S(1)}, bf16[512,512]{1,0:T(8,128)(2,1)S(1)}, u32[]{:S(2)}, u32[]{:S(2)}) collective-permute-start(bf16[512,512]{1,0:T(8,128)(2,1)S(1)} %get-tuple-element.65), channel_id=1, source_target_pairs={{0,1},{1,0},{2,3},{3,2},{4,5},{5,4},{6,7},{7,6},{8,9},{9,8},{10,11... | collective-permute-start | bytes 1572872 | tf_op jit(solution)/shard_map/ppermute | solution.py:677
  103.6 5.9 %collective-permute-start.11 = (bf16[64,512]{1,0:T(8,128)(2,1)S(1)}, bf16[64,512]{1,0:T(8,128)(2,1)S(1)}, u32[]{:S(2)}, u32[]{:S(2)}) collective-permute-start(bf16[64,512]{1,0:T(8,128)(2,1)S(1)} %reduce_sum.12), channel_id=1, source_target_pairs={{0,16},{16,0},{1,17},{17,1},{2,18},{18,2},{3,19},{19,3},{4,20},{20... | collective-permute-start | bytes 196616 | tf_op jit(solution)/shard_map/ppermute | solution.py:688
  120.7 5.9 %collective-permute-start.12 = (bf16[512,512]{1,0:T(8,128)(2,1)}, bf16[512,512]{1,0:T(8,128)(2,1)}, u32[]{:S(2)}, u32[]{:S(2)}) collective-permute-start(bf16[512,512]{1,0:T(8,128)(2,1)} %bitcast.8), channel_id=1, source_target_pairs={{0,1},{1,0},{2,3},{3,2},{4,5},{5,4},{6,7},{7,6},{8,9},{9,8},{10,11... | collective-permute-start | bytes 1572872 | tf_op jit(solution)/shard_map/ppermute | solution.py:692
  120.7 1.0 copy-start.6
  121.8 1.0 copy-start.10
  122.8 1.4 %copy-start.8 = (bf16[512,512]{1,0:T(8,128)(2,1)S(1)}, bf16[512,512]{1,0:T(8,128)(2,1)}, u32[]{:S(2)}) copy-start(bf16[512,512]{1,0:T(8,128)(2,1)} %copy-done.7) | copy-start | bytes 1572868

commit v5 on v4

--- a/solution.py
+++ b/solution.py
@@ -131,7 +131,6 @@
     members_ref,
     nodes_ref,
     fetched_ref,
-    slope_ref,
     core_ref,
     farpkt_ref,
     keep_ref,
@@ -147,7 +146,6 @@
     pre = mm(fetched, weight_ref[...]) + edges_ref[...].astype(F32)
     sig = sigmoid(pre)
     act = (pre * sig).astype(BF16)
-    slope_ref[...] = (sig * (1.0 + pre * (1.0 - sig))).astype(BF16)
     summed = mm(aims_ref[...], act)
     mid = (mesh_ref[...].astype(F32) + factor * summed).astype(BF16)
     part = mm(members_ref[...], mid)
@@ -174,16 +172,32 @@
     lane = lax.broadcasted_iota(I32, (level_rows, features), 1) - (tile % group) * half
     sel = (j == lane) & (j >= 0) & (j < half)
     codes = mm(coarse_split(coarse_ref[...]), jnp.where(sel, 1.0, 0.0).astype(BF16))
-    lanes = out_ref.shape[2]
+    lanes = out_ref.shape[1]
     strips = features // lanes
     tail = jnp.concatenate(
         [codes[r : r + 1, i * lanes : (i + 1) * lanes] for r in range(2) for i in range(strips)],
         axis=0,
     ).astype(BF16)
+    for i in range(strips):
+        out_ref[i * half : (i + 1) * half] = mid[:, i * lanes : (i + 1) * lanes]
+    out_ref[strips * half :] = tail
+
+
+def pair_kernel(dev_ref, mine_ref, away_ref, out_ref):
+    span = mine_ref.shape[0]
     for peer in range(out_ref.shape[0]):
-        for i in range(strips):
-            out_ref[peer, i * half : (i + 1) * half] = mid[:, i * lanes : (i + 1) * lanes]
-        out_ref[peer, strips * half :] = tail
+        out_ref[peer, :span] = mine_ref[...]
+        out_ref[peer, span:] = away_ref[...]
+
+
+def placed_blocks(tile, near, group, half):
+    count = min(group, near)
+    mine = tile // near
+    for part in range(2):
+        side = mine if part == 0 else 1 - mine
+        for first in range(0, near, count):
+            at = side * near + first
+            yield part, first, count, at // group, pl.multiple_of((at % group) * half, half)
 
 
 def middle_kernel(
@@ -207,9 +221,7 @@
     partner_ref,
     far_ref,
     level_ref,
-    middle_slope_ref,
     summit_in_ref,
-    summit_slope_ref,
     ids_ref,
     out_scr,
     *,
@@ -221,24 +233,27 @@
     device = dev_ref[0]
     core = device % 2
     tile = device // subs
-    tiles, _, lanes = mine_ref.shape
+    near, span, lanes = mine_ref.shape
+    tiles = 2 * near
     features = cot_ref.shape[1]
     strips = features // lanes
     half = level_rows // 2
     group = min(features // half, tiles)
     groups = tiles // group
     chunk = group * half
-    for g in range(groups):
+    unit = span // 2
+    ids_ref[...] = jnp.zeros(ids_ref.shape, I32)
+    for part, first, count, g, row in placed_blocks(tile, near, group, half):
         for src, which in ((mine_ref, core), (other_ref, 1 - core)):
-            block = src[g * group : (g + 1) * group]
+            block = src[first : first + count, part * unit : (part + 1) * unit]
             for i in range(strips):
-                level_ref[which, g, :, i * lanes : (i + 1) * lanes] = block[
+                level_ref[which, g, pl.ds(row, count * half), i * lanes : (i + 1) * lanes] = block[
                     :, i * half : (i + 1) * half
-                ].reshape(chunk, lanes)
+                ].reshape(count * half, lanes)
             codes = jnp.sum(block[:, strips * half :].astype(F32), axis=0)
             ids = codes[:strips] * 16.0 + codes[strips : 2 * strips]
             ids = jnp.concatenate([ids[i : i + 1] for i in range(strips)], axis=1)
-            ids_ref[which, g] = jnp.broadcast_to(ids.astype(I32)[:, :chunk], (8, chunk))
+            ids_ref[which, g] += jnp.broadcast_to(ids.astype(I32)[:, :chunk], (8, chunk))
     summed = jnp.zeros((TOP_NODES, features), F32)
     for g in range(groups):
         for h in range(2):
@@ -246,14 +261,12 @@
             act = mm(mid, middle_weight_ref[...])
             sig = sigmoid(act)
             out = (mid.astype(F32) + act * sig).astype(BF16)
-            middle_slope_ref[h, g] = (sig * (1.0 + act * (1.0 - sig))).astype(BF16)
             out_scr[h, pl.ds(g * chunk, chunk)] = out
             summed = summed + mm(rows_onehot(ids_ref[h, g][:1], TOP_NODES), out)
     summit_in = (summit_factor * summed).astype(BF16)
     summit_in_ref[...] = summit_in
     act = mm(summit_in, summit_weight_ref[...])
     sig = sigmoid(act)
-    summit_slope_ref[...] = sig * (1.0 + act * (1.0 - sig))
     summit_out = (act * sig).astype(BF16)
 
     mesh_rows = farpkt_ref.shape[0] - 8
@@ -301,8 +314,33 @@
     far_ref[...] = returned[2 * rows :].astype(BF16)
 
 
+def silu_slope(values):
+    sig = sigmoid(values)
+    return sig * (1.0 + values * (1.0 - sig))
+
+
+def slope_kernel(dev_ref, fetched_ref, edges_ref, weight_ref, slope_ref):
+    pre = mm(fetched_ref[...], weight_ref[...]) + edges_ref[...].astype(F32)
+    slope_ref[...] = silu_slope(pre).astype(BF16)
+
+
 def update_kernel(
-    dev_ref, grid_ref, target_ref, act_ref, fetched_ref, slope_ref, update_ref, dgrad_ref, *, factor
+    dev_ref,
+    grid_ref,
+    target_ref,
+    act_ref,
+    fetched_ref,
+    slope_ref,
+    level_ref,
+    summit_in_ref,
+    middle_weight_ref,
+    summit_weight_ref,
+    update_ref,
+    dgrad_ref,
+    middle_slope_ref,
+    summit_slope_ref,
+    *,
+    factor,
 ):
     grid_rows = grid_ref.shape[0]
     raw = target_ref[...]
@@ -310,6 +348,11 @@
     summed = mm(rows_onehot(aimed, grid_rows), act_ref[...])
     update_ref[...] = (grid_ref[...].astype(F32) + factor * summed).astype(BF16)
     dgrad_ref[...] = mm_tn(fetched_ref[...], slope_ref[...])
+    for h in range(2):
+        for g in range(level_ref.shape[1]):
+            act = mm(level_ref[h, g], middle_weight_ref[...])
+            middle_slope_ref[h, g] = silu_slope(act).astype(BF16)
+    summit_slope_ref[...] = silu_slope(mm(summit_in_ref[...], summit_weight_ref[...]))
 
 
 def level_kernel(
@@ -366,12 +409,15 @@
     device = dev_ref[0]
     core = device % 2
     tile = device // subs
-    _, half, features = mine_ref.shape
+    near, pair, features = mine_ref.shape
+    half = pair // 2
     _, groups, chunk, _ = grad_ref.shape
     group = chunk // half
-    for g in range(groups):
+    for part, first, count, g, row in placed_blocks(tile, near, group, half):
         for src, which in ((mine_ref, core), (other_ref, 1 - core)):
-            grad_ref[which, g] = src[g * group : (g + 1) * group].reshape(chunk, features)
+            grad_ref[which, g, pl.ds(row, count * half)] = src[
+                first : first + count, part * half : (part + 1) * half
+            ].reshape(count * half, features)
     total = jnp.zeros((TOP_NODES, features), F32)
     for g in range(groups):
         for h in range(2):
@@ -481,6 +527,7 @@
     subs = lax.axis_size("row") * lax.axis_size("core")
     devices = tiles * subs
     peers = devices // 4
+    near = tiles // 2
     edges = encode_source.shape[0]
     swap = [(0, 1), (1, 0)]
     beside = []
@@ -522,10 +569,9 @@
         ],
         subs=subs,
     )
-    fetched, slope, core_pkt, far_pkt, keep = call(
+    fetched, core_pkt, far_pkt, keep = call(
         encode_kernel,
         [
-            shape((edges, features), BF16),
             shape((edges, features), BF16),
             shape((half + mesh_rows + 8, features), BF16),
             shape((mesh_rows + 8, features), BF16),
@@ -550,14 +596,21 @@
     far_in = lax.ppermute(far_pkt, ALL, beside)
     mine = (keep + core_in[:half].astype(F32)).astype(BF16)
     other = lax.ppermute(mine, "row", swap)
-    packed = call(
+    packet = call(
         spread_kernel,
-        shape((tiles, (features // LANES) * half + 8, LANES), BF16),
+        shape(((features // LANES) * half + 8, LANES), BF16),
         [dev, mine, other, owner_coarse[None]],
         subs=subs,
         factor=middle_factor,
     )
-    mids = lax.all_to_all(packed, TILE, 0, 0)
+    away = lax.ppermute(packet, "half", swap)
+    slope = call(
+        slope_kernel, shape((edges, features), BF16), [dev, fetched, edges_in, weight_in]
+    )
+    packed = call(
+        pair_kernel, shape((near, 2 * packet.shape[0], LANES), BF16), [dev, packet, away]
+    )
+    mids = lax.all_to_all(packed, "near", 0, 0)
     mids_other = lax.ppermute(mids, "core", swap)
     full = (2, groups, chunk, features)
     (
@@ -568,9 +621,7 @@
         partner,
         far,
         level,
-        middle_slope,
         summit_in,
-        summit_slope,
         ids,
     ) = call(
         middle_kernel,
@@ -582,9 +633,7 @@
             shape((mesh_rows, features), F32),
             shape((mesh_rows, features), BF16),
             shape(full, BF16),
-            shape(full, BF16),
             shape((TOP_NODES, features), BF16),
-            shape((TOP_NODES, features), F32),
             shape((2, groups, 8, chunk), I32),
         ],
         [
@@ -611,9 +660,14 @@
         decode_factor=decode_factor,
     )
     far_back = lax.ppermute(far, ALL, beside)
-    grid_update, dgrad = call(
+    grid_update, dgrad, middle_slope, summit_slope = call(
         update_kernel,
-        [shape((rows, features), BF16), shape((features, features), F32)],
+        [
+            shape((rows, features), BF16),
+            shape((features, features), F32),
+            shape(full, BF16),
+            shape((TOP_NODES, features), F32),
+        ],
         [
             dev,
             grid_feats,
@@ -621,6 +675,10 @@
             decode_act,
             decode_fetched,
             decode_slope,
+            level,
+            summit_in,
+            middle_weight,
+            summit_weight,
         ],
         factor=decode_factor,
     )
@@ -638,8 +696,9 @@
     mine = (keep + back_in[:half].astype(F32)).astype(BF16)
     other = lax.ppermute(mine, "row", swap)
     total = (mine.astype(F32) + other.astype(F32)).astype(BF16)
-    packed = jnp.broadcast_to(total[None], (tiles, half, features))
-    grads = lax.all_to_all(packed, TILE, 0, 0)
+    away = lax.ppermute(total, "half", swap)
+    packed = call(pair_kernel, shape((near, 2 * half, features), BF16), [dev, total, away])
+    grads = lax.all_to_all(packed, "near", 0, 0)
     grads_other = lax.ppermute(grads, "core", swap)
     send, keep, level_back, top, top_back = call(
         back_kernel,
@@ -684,9 +743,9 @@
     share = (keep + received.astype(F32)).astype(BF16)
     share = share.reshape(peers, features // peers, features)
     parts = lax.all_to_all(share, NEAR, 0, 0)
-    near = jnp.sum(parts.astype(F32), axis=0).astype(BF16)
-    away = lax.ppermute(near, "half", swap)
-    summed = (near.astype(F32) + away.astype(F32)).astype(BF16)
+    inside = jnp.sum(parts.astype(F32), axis=0).astype(BF16)
+    away = lax.ppermute(inside, "half", swap)
+    summed = (inside.astype(F32) + away.astype(F32)).astype(BF16)
     copies = jnp.broadcast_to(summed[None], parts.shape)
     mine = lax.all_to_all(copies, NEAR, 0, 0).reshape(features, features)
     other = lax.ppermute(mine, "core", swap)

time: 130 us -> 125 us (0.962)
  blocking collectives: 63.5 us -> 45.1 us
  starting transfers between devices: 23.4 us -> 33.4 us
  waiting for transfers between devices: 16.2 us -> 19.9 us
    all_to_all x2, blocking collectives: 39.3 us -> 20.7 us  [the longest x1 10.6 us: shards(): mids = lax.all_to_all(packed, 'near', 0, 0)]
    ppermute x1 -> x3, starting transfers between devices: 1.31 us -> 10.4 us  [the longest x1 4.96 us: shards(): away = lax.ppermute(total, 'half', swap)]
    ppermute x1 -> x3, waiting for transfers between devices: 4.62 us -> 9.48 us  [the longest x1 4.18 us: shards(): away = lax.ppermute(inside, 'half', swap)]
    pallas_call x9 -> x12, Pallas kernels: 15.1 us -> 16.4 us  [call(): pl.pallas_call(functools.partial(body, **static), out_shape=outs, in_spec...]
    unnamed x44 -> x40, local copies, waits for them, and re-layouts: 5.99 us -> 4.95 us
  transfers between devices with their start and end apart: 13 -> 15, of which waited for: 8 -> 9; matrix products, arithmetic and copies ran while one was open for 0% -> 0% of each run, Pallas kernels for 4% -> 6%
where the time goes in v5:
time: 125 us
  blocking collectives  45.1 us (36%)
  starting transfers between devices  33.4 us (27%)
  waiting for transfers between devices  19.9 us (16%)
  Pallas kernels  16.4 us (13%)
  local copies, waits for them, and re-layouts  4.98 us (4%)
  other arithmetic  4 us (3%)
    pallas_call x12, Pallas kernels, call(): pl.pallas_call(functools.partial(body, **static), out_shape=outs, in_spec...  16.4 us
    all_to_all x1, blocking collectives, shards(): parts = lax.all_to_all(share, NEAR, 0, 0)  13.3 us
    all_to_all x1, blocking collectives, shards(): mine = lax.all_to_all(copies, NEAR, 0, 0).reshape(features, features)  11.1 us
    ppermute x1, starting transfers between devices, shards(): back_in = lax.ppermute(core_pkt, 'core', swap)  10.7 us
    all_to_all x1, blocking collectives, shards(): mids = lax.all_to_all(packed, 'near', 0, 0)  10.6 us
    all_to_all x1, blocking collectives, shards(): grads = lax.all_to_all(packed, 'near', 0, 0)  10.1 us
    ppermute x2, waiting for transfers between devices, shards(): other = lax.ppermute(mine, 'row', swap)  5.57 us
    ppermute x2, starting transfers between devices, shards(): other = lax.ppermute(mine, 'row', swap)  5.07 us
  transfers between devices with their start and end apart: 15, of which 9 were waited for; matrix products, arithmetic and copies ran while one was open for 0% of the time, Pallas kernels for 6%

profile of v5, /device:TPU:0, one launch (start us, length us, event | category | flops | bytes accessed | tf_op | source)
XLA Modules:
  0.0 124.7 jit_solution(7288112518313614143)
XLA Ops:
  0.6 0.6 collective-permute-start
  1.2 0.7 collective-permute-start.1
  1.9 0.6 copy-done.17
  2.6 0.0 copy-done.14
  2.6 1.2 copy-done.4
  3.8 1.0 copy-done.9
  4.8 0.9 copy-done.10
  5.8 0.9 shard_map.182
  6.7 0.0 copy-start.13
  6.7 1.6 %shard_map.183 = (bf16[1024,512]{1,0:T(8,128)(2,1)S(1)}, bf16[200,512]{1,0:T(8,128)(2,1)S(1)}, bf16[136,512]{1,0:T(8,128)(2,1)S(1)}, f32[64,512]{1,0:T(8,128)S(1)}) custom-call(s32[1]{0:T(128)} %bitcast.dev_ref, bf16[128,512]{1,0:T(8,128)(2,1)S(1)} %collective-permute-done.partner_ref, bf16[128,512]{1,0:T(8,128)(2,1)S(1)} %collective-permute-done.1.far_ref, ...), custom_call_target="tpu_custom_call" | custom-call | tf_op jit(solution)/shard_map/pallas_call | solution.py:491
  8.3 4.0 %collective-permute-start.2 = (bf16[200,512]{1,0:T(8,128)(2,1)S(1)}, bf16[200,512]{1,0:T(8,128)(2,1)S(1)}, u32[]{:S(2)}, u32[]{:S(2)}) collective-permute-start(bf16[200,512]{1,0:T(8,128)(2,1)S(1)} %get-tuple-element.45), channel_id=1, source_target_pairs={{0,1},{1,0},{2,3},{3,2},{4,5},{5,4},{6,7},{7,6},{8,9},{9,8},{10,11... | collective-permute-start | bytes 614408 | tf_op jit(solution)/shard_map/ppermute | solution.py:595
  12.3 1.1 collective-permute-done.2.core_ref
  13.4 1.5 %collective-permute-start.3 = (bf16[64,512]{1,0:T(8,128)(2,1)S(1)}, bf16[64,512]{1,0:T(8,128)(2,1)S(1)}, u32[]{:S(2)}, u32[]{:S(2)}) collective-permute-start(bf16[64,512]{1,0:T(8,128)(2,1)S(1)} %add_convert_fusion.4.mine_ref), channel_id=1, source_target_pairs={{0,2},{2,0},{1,3},{3,1},{4,6},{6,4},{5,7},{7,5},{8,10},{10,8},{9,1... | collective-permute-start | bytes 196616 | tf_op jit(solution)/shard_map/ppermute | solution.py:598
  14.9 2.9 %collective-permute-done.3.other_ref = bf16[64,512]{1,0:T(8,128)(2,1)S(1)} collective-permute-done((bf16[64,512]{1,0:T(8,128)(2,1)S(1)}, bf16[64,512]{1,0:T(8,128)(2,1)S(1)}, u32[]{:S(2)}, u32[]{:S(2)}) %collective-permute-start.3) | collective-permute-done | bytes 65568 | tf_op jit(solution)/shard_map/ppermute | solution.py:598
  17.8 0.2 shard_map.184.mine_ref
  18.0 3.6 %collective-permute-start.4 = (bf16[264,128]{1,0:T(8,128)(2,1)S(1)}, bf16[264,128]{1,0:T(8,128)(2,1)S(1)}, u32[]{:S(2)}, u32[]{:S(2)}) collective-permute-start(bf16[264,128]{1,0:T(8,128)(2,1)S(1)} %shard_map.184.mine_ref), channel_id=1, source_target_pairs={{0,16},{16,0},{1,17},{17,1},{2,18},{18,2},{3,19},{19,3},{4,20},{20... | collective-permute-start | bytes 202760 | tf_op jit(solution)/shard_map/ppermute | solution.py:606
  21.6 2.4 %collective-permute-done.4.away_ref = bf16[264,128]{1,0:T(8,128)(2,1)S(1)} collective-permute-done((bf16[264,128]{1,0:T(8,128)(2,1)S(1)}, bf16[264,128]{1,0:T(8,128)(2,1)S(1)}, u32[]{:S(2)}, u32[]{:S(2)}) %collective-permute-start.4) | collective-permute-done | bytes 67616 | tf_op jit(solution)/shard_map/ppermute | solution.py:606
  24.0 0.1 shard_map.185
  24.0 0.0 copy-start
  24.1 10.6 %all_to_all.20.mine_ref = bf16[4,528,128]{2,1,0:T(8,128)(2,1)S(1)} all-to-all(bf16[4,528,128]{2,1,0:T(8,128)(2,1)S(1)} %shard_map.185), channel_id=1, replica_groups=mesh['half'=2,'near'=4,'row'=2,'core'=2] {'near'}, dimensions={0} | all-to-all | bytes 1081344 | tf_op jit(solution)/shard_map/all_to_all | solution.py:613
  34.7 0.8 collective-permute-start.6
  35.5 1.1 collective-permute-done.5.other_ref
  36.7 4.0 %shard_map.186 = (bf16[512,512]{1,0:T(8,128)(2,1)S(1)}, bf16[512,512]{1,0:T(8,128)(2,1)S(1)}, bf16[512,512]{1,0:T(8,128)(2,1)S(1)}, f32[128,512]{1,0:T(8,128)S(1...) custom-call(s32[1]{0:T(128)} %bitcast.dev_ref, ...), custom_call_target="tpu_custom_call" | custom-call | tf_op jit(solution)/shard_map/pallas_call | solution.py:491
  40.7 0.7 collective-permute-start.7
  41.4 0.2 shard_map.188
  41.6 10.7 %collective-permute-start.8 = (bf16[192,512]{1,0:T(8,128)(2,1)S(1)}, bf16[192,512]{1,0:T(8,128)(2,1)S(1)}, u32[]{:S(2)}, u32[]{:S(2)}) collective-permute-start(bf16[192,512]{1,0:T(8,128)(2,1)S(1)} %get-tuple-element.57), channel_id=1, source_target_pairs={{0,1},{1,0},{2,3},{3,2},{4,5},{5,4},{6,7},{7,6},{8,9},{9,8},{10,11... | collective-permute-start | bytes 589832 | tf_op jit(solution)/shard_map/ppermute | solution.py:695
  52.4 1.1 collective-permute-done.8.partnerin_ref
  53.5 3.6 %collective-permute-start.9 = (bf16[64,512]{1,0:T(8,128)(2,1)S(1)}, bf16[64,512]{1,0:T(8,128)(2,1)S(1)}, u32[]{:S(2)}, u32[]{:S(2)}) collective-permute-start(bf16[64,512]{1,0:T(8,128)(2,1)S(1)} %add_convert_fusion.3), channel_id=1, source_target_pairs={{0,2},{2,0},{1,3},{3,1},{4,6},{6,4},{5,7},{7,5},{8,10},{10,8},{9,1... | collective-permute-start | bytes 196616 | tf_op jit(solution)/shard_map/ppermute | solution.py:697
  57.0 2.6 %collective-permute-done.9 = bf16[64,512]{1,0:T(8,128)(2,1)S(1)} collective-permute-done((bf16[64,512]{1,0:T(8,128)(2,1)S(1)}, bf16[64,512]{1,0:T(8,128)(2,1)S(1)}, u32[]{:S(2)}, u32[]{:S(2)}) %collective-permute-start.9) | collective-permute-done | bytes 65568 | tf_op jit(solution)/shard_map/ppermute | solution.py:697
  59.7 5.0 %collective-permute-start.10 = (bf16[64,512]{1,0:T(8,128)(2,1)S(1)}, bf16[64,512]{1,0:T(8,128)(2,1)S(1)}, u32[]{:S(2)}, u32[]{:S(2)}) collective-permute-start(bf16[64,512]{1,0:T(8,128)(2,1)S(1)} %add_convert_fusion.2.mine_ref), channel_id=1, source_target_pairs={{0,16},{16,0},{1,17},{17,1},{2,18},{18,2},{3,19},{19,3},{4,20},{20... | collective-permute-start | bytes 196616 | tf_op jit(solution)/shard_map/ppermute | solution.py:699
  64.6 2.9 %collective-permute-done.10.away_ref = bf16[64,512]{1,0:T(8,128)(2,1)S(1)} collective-permute-done((bf16[64,512]{1,0:T(8,128)(2,1)S(1)}, bf16[64,512]{1,0:T(8,128)(2,1)S(1)}, u32[]{:S(2)}, u32[]{:S(2)}) %collective-permute-start.10) | collective-permute-done | bytes 65568 | tf_op jit(solution)/shard_map/ppermute | solution.py:699
  67.6 10.1 %all_to_all.21.mine_ref = bf16[4,128,512]{2,1,0:T(8,128)(2,1)S(1)} all-to-all(bf16[4,128,512]{2,1,0:T(8,128)(2,1)S(1)} %shard_map.189), channel_id=1, replica_groups=mesh['half'=2,'near'=4,'row'=2,'core'=2] {'near'}, dimensions={0} | all-to-all | bytes 1048576 | tf_op jit(solution)/shard_map/all_to_all | solution.py:701
  77.7 1.2 shard_map.190.slope_ref
  78.9 1.8 %shard_map.187 = (bf16[128,512]{1,0:T(8,128)(2,1)}, f32[512,512]{1,0:T(8,128)S(1)}, bf16[2,1,512,512]{3,2,1,0:T(8,128)(2,1)S(1)}, f32[512,512]{1,0:T(8,128)S(1)}) custom-call(s32[1]{0:T(128)} %bitcast.dev_ref, bf16[128,512]{1,0:T(8,128)(2,1)S(1)} %copy-done.11, s32[1,512]{1,0:T(1,128)S(1)} %bitcast.14, bf16[512,512]{1,0:T(8,128)(2,1)S(1)} %get-tuple-element.47.act_ref, ...), custom_call_target="tpu_custom_call" | custom-call | tf_op jit(solution)/shard_map/pallas_call | solution.py:491
  80.7 2.7 %shard_map.191 = (bf16[512,512]{1,0:T(8,128)(2,1)S(1)}, f32[512,512]{1,0:T(8,128)S(1)}, bf16[2,1,512,512]{3,2,1,0:T(8,128)(2,1)S(1)}, bf16[512,512]{1,0:T(8,128)(2,1)S(1)}, bf16[512,512]{1,0:T(8,128)(2,1)S(1)}) custom-call(s32[1]{0:T(128)} %bitcast.dev_ref, bf16[4,128,512]{2,1,0:T(8,128)(2,1)S(1)} %all_to_all.21.mine_ref, ...), custom_call_target="tpu_custom_call" | custom-call | tf_op jit(solution)/shard_map/pallas_call | solution.py:491
  83.3 0.0 copy-start.7
  83.3 0.6 collective-permute-start.12
  83.9 1.5 %collective-permute-done.12 = bf16[512,512]{1,0:T(8,128)(2,1)S(1)} collective-permute-done((bf16[512,512]{1,0:T(8,128)(2,1)S(1)}, bf16[512,512]{1,0:T(8,128)(2,1)S(1)}, u32[]{:S(2)}, u32[]{:S(2)}) %collective-permute-start.12) | collective-permute-done | bytes 524320 | tf_op jit(solution)/shard_map/ppermute | solution.py:736
  85.5 0.2 add_convert_fusion
  85.6 13.3 %all_to_all.22 = bf16[8,64,512]{2,1,0:T(8,128)(2,1)} all-to-all(bf16[8,64,512]{2,1,0:T(8,128)(2,1)S(1)} %bitcast.21), channel_id=1, replica_groups=mesh['half'=2,'near'=4,'row'=2,'core'=2] {'near','row'}, dimensions={0} | all-to-all | bytes 1048576 | tf_op jit(solution)/shard_map/all_to_all | solution.py:745
  99.0 1.1 reduce_sum.12
  100.1 1.8 %collective-permute-start.13 = (bf16[64,512]{1,0:T(8,128)(2,1)S(1)}, bf16[64,512]{1,0:T(8,128)(2,1)S(1)}, u32[]{:S(2)}, u32[]{:S(2)}) collective-permute-start(bf16[64,512]{1,0:T(8,128)(2,1)S(1)} %reduce_sum.12), channel_id=1, source_target_pairs={{0,16},{16,0},{1,17},{17,1},{2,18},{18,2},{3,19},{19,3},{4,20},{20... | collective-permute-start | bytes 196616 | tf_op jit(solution)/shard_map/ppermute | solution.py:747
  101.8 4.2 %collective-permute-done.13 = bf16[64,512]{1,0:T(8,128)(2,1)S(1)} collective-permute-done((bf16[64,512]{1,0:T(8,128)(2,1)S(1)}, bf16[64,512]{1,0:T(8,128)(2,1)S(1)}, u32[]{:S(2)}, u32[]{:S(2)}) %collective-permute-start.13) | collective-permute-done | bytes 65568 | tf_op jit(solution)/shard_map/ppermute | solution.py:747
  106.1 11.1 %all_to_all.23 = bf16[8,64,512]{2,1,0:T(8,128)(2,1)} all-to-all(bf16[8,64,512]{2,1,0:T(8,128)(2,1)S(1)} %broadcast_in_dim.34), channel_id=1, replica_groups=mesh['half'=2,'near'=4,'row'=2,'core'=2] {'near','row'}, dimensions={0} | all-to-all | bytes 1048576 | tf_op jit(solution)/shard_map/all_to_all | solution.py:750
  117.2 1.0 copy-done.8
  118.2 1.4 %shard_map.193 = f32[512,512]{1,0:T(8,128)} custom-call(s32[1]{0:T(128)} %bitcast.dev_ref, bf16[512,512]{1,0:T(8,128)(2,1)S(1)} %get-tuple-element.51.summit_in_ref, bf16[512,512]{1,0:T(8,128)(2,1)S(1)} %copy-done.8), custom_call_target="tpu_custom_call" | custom-call | tf_op jit(solution)/shard_map/pallas_call | solution.py:491
  119.7 2.4 %shard_map.192 = f32[512,512]{1,0:T(8,128)} custom-call(s32[1]{0:T(128)} %bitcast.dev_ref, bf16[2,1,512,512]{3,2,1,0:T(8,128)(2,1)S(1)} %copy-done.3, bf16[2,1,512,512]{3,2,1,0:T(8,128)(2,1)S(1)} %get-tuple-element.50.level_ref, bf16[2,1,512,512]{3,2,1,0:T(8,128)(2,1)S(1)} %get-tuple-element.58.middle_slope_ref, ...), custom_call_target="tpu_custom_call" | custom-call | tf_op jit(solution)/shard_map/pallas_call | solution.py:491
  122.1 2.7 %select_convert_fusion = (f32[512,512]{1,0:T(8,128)}, f32[512,512]{1,0:T(8,128)}) fusion(bf16[512,512]{1,0:T(8,128)(2,1)} %collective-permute-done.14, pred[]{:T(512)S(6)} %eq.6, bf16[8,64,512]{2,1,0:T(8,128)(2,1)} %all_to_all.23), kind=kLoop, calls=%fused_computation.1 | loop fusion | flops 1048576 | bytes 3145729 | tf_op jit(solution)/shard_map/convert_element_type | solution.py:756
  (46 shorter events, 0.2 us)
Async XLA Ops:
  0.6 6.0 %collective-permute-start = (bf16[128,512]{1,0:T(8,128)(2,1)}, bf16[128,512]{1,0:T(8,128)(2,1)S(1)}, u32[]{:S(2)}, u32[]{:S(2)}) collective-permute-start(bf16[128,512]{1,0:T(8,128)(2,1)} %grid_ref.3), channel_id=1, source_target_pairs={{0,1},{1,0},{2,3},{3,2},{4,5},{5,4},{6,7},{7,6},{8,9},{9,8},{10,11... | collective-permute-start | bytes 393224 | tf_op jit(solution)/shard_map/ppermute | solution.py:548
  1.2 5.5 %collective-permute-start.1 = (bf16[128,512]{1,0:T(8,128)(2,1)}, bf16[128,512]{1,0:T(8,128)(2,1)S(1)}, u32[]{:S(2)}, u32[]{:S(2)}) collective-permute-start(bf16[128,512]{1,0:T(8,128)(2,1)} %grid_ref.3), channel_id=1, source_target_pairs={{1,2},{2,1},{3,4},{4,3},{5,6},{6,5},{7,8},{8,7},{9,10},{10,9},{11,... | collective-permute-start | bytes 393224 | tf_op jit(solution)/shard_map/ppermute | solution.py:547
  1.9 0.7 copy-start.17
  1.9 0.7 copy-start.14
  1.9 0.7 copy-start.16
  1.9 0.7 copy-start.19
  2.6 1.2 copy-start.4
  3.8 1.0 copy-start.9
  4.8 0.9 copy-start.10
  5.8 1.0 copy-start.12
  6.7 29.9 %copy-start.13 = (bf16[128,512]{1,0:T(8,128)(2,1)S(1)}, bf16[128,512]{1,0:T(8,128)(2,1)}, u32[]{:S(2)}) copy-start(bf16[128,512]{1,0:T(8,128)(2,1)} %cot_ref.1) | copy-start | bytes 393220
  8.3 5.0 %collective-permute-start.2 = (bf16[200,512]{1,0:T(8,128)(2,1)S(1)}, bf16[200,512]{1,0:T(8,128)(2,1)S(1)}, u32[]{:S(2)}, u32[]{:S(2)}) collective-permute-start(bf16[200,512]{1,0:T(8,128)(2,1)S(1)} %get-tuple-element.45), channel_id=1, source_target_pairs={{0,1},{1,0},{2,3},{3,2},{4,5},{5,4},{6,7},{7,6},{8,9},{9,8},{10,11... | collective-permute-start | bytes 614408 | tf_op jit(solution)/shard_map/ppermute | solution.py:595
  13.3 23.3 %copy-start.6 = (bf16[512,512]{1,0:T(8,128)(2,1)S(1)}, bf16[512,512]{1,0:T(8,128)(2,1)}, u32[]{:S(2)}) copy-start(bf16[512,512]{1,0:T(8,128)(2,1)} %decode_weight_ref.1) | copy-start | bytes 1572868
  13.4 4.4 %collective-permute-start.3 = (bf16[64,512]{1,0:T(8,128)(2,1)S(1)}, bf16[64,512]{1,0:T(8,128)(2,1)S(1)}, u32[]{:S(2)}, u32[]{:S(2)}) collective-permute-start(bf16[64,512]{1,0:T(8,128)(2,1)S(1)} %add_convert_fusion.4.mine_ref), channel_id=1, source_target_pairs={{0,2},{2,0},{1,3},{3,1},{4,6},{6,4},{5,7},{7,5},{8,10},{10,8},{9,1... | collective-permute-start | bytes 196616 | tf_op jit(solution)/shard_map/ppermute | solution.py:598
  18.0 6.0 %collective-permute-start.4 = (bf16[264,128]{1,0:T(8,128)(2,1)S(1)}, bf16[264,128]{1,0:T(8,128)(2,1)S(1)}, u32[]{:S(2)}, u32[]{:S(2)}) collective-permute-start(bf16[264,128]{1,0:T(8,128)(2,1)S(1)} %shard_map.184.mine_ref), channel_id=1, source_target_pairs={{0,16},{16,0},{1,17},{17,1},{2,18},{18,2},{3,19},{19,3},{4,20},{20... | collective-permute-start | bytes 202760 | tf_op jit(solution)/shard_map/ppermute | solution.py:606
  24.0 12.7 %copy-start.5 = (bf16[512,512]{1,0:T(8,128)(2,1)S(1)}, bf16[512,512]{1,0:T(8,128)(2,1)}, u32[]{:S(2)}) copy-start(bf16[512,512]{1,0:T(8,128)(2,1)} %edges_ref.3) | copy-start | bytes 1572868
  24.0 12.6 %copy-start = (bf16[512,512]{1,0:T(8,128)(2,1)S(1)}, bf16[512,512]{1,0:T(8,128)(2,1)}, u32[]{:S(2)}) copy-start(bf16[512,512]{1,0:T(8,128)(2,1)} %middle_weight_ref.5) | copy-start | bytes 1572868
  24.0 12.6 %copy-start.1 = (bf16[512,512]{1,0:T(8,128)(2,1)S(1)}, bf16[512,512]{1,0:T(8,128)(2,1)}, u32[]{:S(2)}) copy-start(bf16[512,512]{1,0:T(8,128)(2,1)} %summit_weight_ref.5) | copy-start | bytes 1572868
  34.7 1.9 %collective-permute-start.5 = (bf16[4,528,128]{2,1,0:T(8,128)(2,1)S(1)}, bf16[4,528,128]{2,1,0:T(8,128)(2,1)S(1)}, u32[]{:S(2)}, u32[]{:S(2)}) collective-permute-start(bf16[4,528,128]{2,1,0:T(8,128)(2,1)S(1)} %all_to_all.20.mine_ref), channel_id=1, source_target_pairs={{0,1},{1,0},{2,3},{3,2},{4,5},{5,4},{6,7},{7,6},{8,9},{9,8},{10,11... | collective-permute-start | bytes 1622024 | tf_op jit(solution)/shard_map/ppermute | solution.py:614
  34.7 2.0 %copy-start.18 = (s32[512]{0:T(512)S(1)}, s32[512]{0:T(512)}, u32[]{:S(2)}) copy-start(s32[512]{0:T(512)} %param.21) | copy-start | bytes 6148
  34.7 2.0 %copy-start.15 = (s32[512]{0:T(512)S(1)}, s32[512]{0:T(512)}, u32[]{:S(2)}) copy-start(s32[512]{0:T(512)} %param.22) | copy-start | bytes 6148
  34.7 0.8 collective-permute-start.6
  40.7 0.7 collective-permute-start.7
  41.6 11.8 %collective-permute-start.8 = (bf16[192,512]{1,0:T(8,128)(2,1)S(1)}, bf16[192,512]{1,0:T(8,128)(2,1)S(1)}, u32[]{:S(2)}, u32[]{:S(2)}) collective-permute-start(bf16[192,512]{1,0:T(8,128)(2,1)S(1)} %get-tuple-element.57), channel_id=1, source_target_pairs={{0,1},{1,0},{2,3},{3,2},{4,5},{5,4},{6,7},{7,6},{8,9},{9,8},{10,11... | collective-permute-start | bytes 589832 | tf_op jit(solution)/shard_map/ppermute | solution.py:695
  53.5 6.2 %collective-permute-start.9 = (bf16[64,512]{1,0:T(8,128)(2,1)S(1)}, bf16[64,512]{1,0:T(8,128)(2,1)S(1)}, u32[]{:S(2)}, u32[]{:S(2)}) collective-permute-start(bf16[64,512]{1,0:T(8,128)(2,1)S(1)} %add_convert_fusion.3), channel_id=1, source_target_pairs={{0,2},{2,0},{1,3},{3,1},{4,6},{6,4},{5,7},{7,5},{8,10},{10,8},{9,1... | collective-permute-start | bytes 196616 | tf_op jit(solution)/shard_map/ppermute | solution.py:697
  59.7 7.9 %collective-permute-start.10 = (bf16[64,512]{1,0:T(8,128)(2,1)S(1)}, bf16[64,512]{1,0:T(8,128)(2,1)S(1)}, u32[]{:S(2)}, u32[]{:S(2)}) collective-permute-start(bf16[64,512]{1,0:T(8,128)(2,1)S(1)} %add_convert_fusion.2.mine_ref), channel_id=1, source_target_pairs={{0,16},{16,0},{1,17},{17,1},{2,18},{18,2},{3,19},{19,3},{4,20},{20... | collective-permute-start | bytes 196616 | tf_op jit(solution)/shard_map/ppermute | solution.py:699
  77.7 3.0 %collective-permute-start.11 = (bf16[4,128,512]{2,1,0:T(8,128)(2,1)S(1)}, bf16[4,128,512]{2,1,0:T(8,128)(2,1)S(1)}, u32[]{:S(2)}, u32[]{:S(2)}) collective-permute-start(bf16[4,128,512]{2,1,0:T(8,128)(2,1)S(1)} %all_to_all.21.mine_ref), channel_id=1, source_target_pairs={{0,1},{1,0},{2,3},{3,2},{4,5},{5,4},{6,7},{7,6},{8,9},{9,8},{10,11... | collective-permute-start | bytes 1572872 | tf_op jit(solution)/shard_map/ppermute | solution.py:702
  77.7 1.2 copy-start.11
  83.3 2.3 %copy-start.2 = (bf16[2,1,512,512]{3,2,1,0:T(8,128)(2,1)}, bf16[2,1,512,512]{3,2,1,0:T(8,128)(2,1)S(1)}, u32[]{:S(2)}) copy-start(bf16[2,1,512,512]{3,2,1,0:T(8,128)(2,1)S(1)} %get-tuple-element.66.grad_ref) | copy-start | bytes 3145732
  83.3 2.3 %copy-start.7 = (bf16[512,512]{1,0:T(8,128)(2,1)}, bf16[512,512]{1,0:T(8,128)(2,1)S(1)}, u32[]{:S(2)}) copy-start(bf16[512,512]{1,0:T(8,128)(2,1)S(1)} %get-tuple-element.68.top_ref) | copy-start | bytes 1572868
  83.3 2.1 %collective-permute-start.12 = (bf16[512,512]{1,0:T(8,128)(2,1)S(1)}, bf16[512,512]{1,0:T(8,128)(2,1)S(1)}, u32[]{:S(2)}, u32[]{:S(2)}) collective-permute-start(bf16[512,512]{1,0:T(8,128)(2,1)S(1)} %get-tuple-element.65), channel_id=1, source_target_pairs={{0,1},{1,0},{2,3},{3,2},{4,5},{5,4},{6,7},{7,6},{8,9},{9,8},{10,11... | collective-permute-start | bytes 1572872 | tf_op jit(solution)/shard_map/ppermute | solution.py:736
  100.1 5.9 %collective-permute-start.13 = (bf16[64,512]{1,0:T(8,128)(2,1)S(1)}, bf16[64,512]{1,0:T(8,128)(2,1)S(1)}, u32[]{:S(2)}, u32[]{:S(2)}) collective-permute-start(bf16[64,512]{1,0:T(8,128)(2,1)S(1)} %reduce_sum.12), channel_id=1, source_target_pairs={{0,16},{16,0},{1,17},{17,1},{2,18},{18,2},{3,19},{19,3},{4,20},{20... | collective-permute-start | bytes 196616 | tf_op jit(solution)/shard_map/ppermute | solution.py:747
  117.2 4.9 %collective-permute-start.14 = (bf16[512,512]{1,0:T(8,128)(2,1)}, bf16[512,512]{1,0:T(8,128)(2,1)}, u32[]{:S(2)}, u32[]{:S(2)}) collective-permute-start(bf16[512,512]{1,0:T(8,128)(2,1)} %bitcast.8), channel_id=1, source_target_pairs={{0,1},{1,0},{2,3},{3,2},{4,5},{5,4},{6,7},{7,6},{8,9},{9,8},{10,11... | collective-permute-start | bytes 1572872 | tf_op jit(solution)/shard_map/ppermute | solution.py:751
  117.2 1.0 copy-start.8
  118.2 1.4 %copy-start.3 = (bf16[2,1,512,512]{3,2,1,0:T(8,128)(2,1)S(1)}, bf16[2,1,512,512]{3,2,1,0:T(8,128)(2,1)}, u32[]{:S(2)}) copy-start(bf16[2,1,512,512]{3,2,1,0:T(8,128)(2,1)} %copy-done.2) | copy-start | bytes 3145732

commit v6 on v5

--- a/solution.py
+++ b/solution.py
@@ -200,9 +200,48 @@
             yield part, first, count, at // group, pl.multiple_of((at % group) * half, half)
 
 
+def unpack_half(src_ref, tile, level_ref, ids_ref, half):
+    near, span, lanes = src_ref.shape
+    _, chunk, features = level_ref.shape
+    strips = features // lanes
+    unit = span // 2
+    ids_ref[...] = jnp.zeros(ids_ref.shape, I32)
+    for part, first, count, g, row in placed_blocks(tile, near, chunk // half, half):
+        block = src_ref[first : first + count, part * unit : (part + 1) * unit]
+        for i in range(strips):
+            level_ref[g, pl.ds(row, count * half), i * lanes : (i + 1) * lanes] = block[
+                :, i * half : (i + 1) * half
+            ].reshape(count * half, lanes)
+        codes = jnp.sum(block[:, strips * half :].astype(F32), axis=0)
+        ids = codes[:strips] * 16.0 + codes[strips : 2 * strips]
+        ids = jnp.concatenate([ids[i : i + 1] for i in range(strips)], axis=1)
+        ids_ref[g] += jnp.broadcast_to(ids.astype(I32)[:, :chunk], (8, chunk))
+
+
+def pooled(mid, ids, weight_ref):
+    act = mm(mid, weight_ref[...])
+    out = (mid.astype(F32) + act * sigmoid(act)).astype(BF16)
+    return out, mm(rows_onehot(ids[:1], TOP_NODES), out)
+
+
+def first_kernel(
+    dev_ref, mine_ref, weight_ref, level_ref, ids_ref, out_ref, part_ref, *, subs, half
+):
+    unpack_half(mine_ref, dev_ref[0] // subs, level_ref, ids_ref, half)
+    part = jnp.zeros(part_ref.shape, F32)
+    for g in range(level_ref.shape[0]):
+        out, add = pooled(level_ref[g], ids_ref[g], weight_ref)
+        out_ref[g] = out
+        part = part + add
+    part_ref[...] = part
+
+
 def middle_kernel(
     dev_ref,
-    mine_ref,
+    first_level_ref,
+    first_ids_ref,
+    first_out_ref,
+    first_part_ref,
     other_ref,
     core_ref,
     farpkt_ref,
@@ -233,36 +272,22 @@
     device = dev_ref[0]
     core = device % 2
     tile = device // subs
-    near, span, lanes = mine_ref.shape
+    near = other_ref.shape[0]
     tiles = 2 * near
-    features = cot_ref.shape[1]
-    strips = features // lanes
     half = level_rows // 2
-    group = min(features // half, tiles)
-    groups = tiles // group
-    chunk = group * half
-    unit = span // 2
-    ids_ref[...] = jnp.zeros(ids_ref.shape, I32)
-    for part, first, count, g, row in placed_blocks(tile, near, group, half):
-        for src, which in ((mine_ref, core), (other_ref, 1 - core)):
-            block = src[first : first + count, part * unit : (part + 1) * unit]
-            for i in range(strips):
-                level_ref[which, g, pl.ds(row, count * half), i * lanes : (i + 1) * lanes] = block[
-                    :, i * half : (i + 1) * half
-                ].reshape(count * half, lanes)
-            codes = jnp.sum(block[:, strips * half :].astype(F32), axis=0)
-            ids = codes[:strips] * 16.0 + codes[strips : 2 * strips]
-            ids = jnp.concatenate([ids[i : i + 1] for i in range(strips)], axis=1)
-            ids_ref[which, g] += jnp.broadcast_to(ids.astype(I32)[:, :chunk], (8, chunk))
-    summed = jnp.zeros((TOP_NODES, features), F32)
+    _, groups, chunk, _ = level_ref.shape
+    level_ref[core] = first_level_ref[...]
+    ids_ref[core] = first_ids_ref[...]
     for g in range(groups):
-        for h in range(2):
-            mid = level_ref[h, g]
-            act = mm(mid, middle_weight_ref[...])
-            sig = sigmoid(act)
-            out = (mid.astype(F32) + act * sig).astype(BF16)
-            out_scr[h, pl.ds(g * chunk, chunk)] = out
-            summed = summed + mm(rows_onehot(ids_ref[h, g][:1], TOP_NODES), out)
+        out_scr[core, pl.ds(g * chunk, chunk)] = first_out_ref[g]
+    away = 1 - core
+    unpack_half(other_ref, tile, level_ref.at[away], ids_ref.at[away], half)
+    part = jnp.zeros(first_part_ref.shape, F32)
+    for g in range(groups):
+        out, add = pooled(level_ref[away, g], ids_ref[away, g], middle_weight_ref)
+        out_scr[away, pl.ds(g * chunk, chunk)] = out
+        part = part + add
+    summed = first_part_ref[...] + part
     summit_in = (summit_factor * summed).astype(BF16)
     summit_in_ref[...] = summit_in
     act = mm(summit_in, summit_weight_ref[...])
@@ -454,26 +479,41 @@
     keep_ref[...] = jnp.where(core == 0, egrad, dgrad)
 
 
-def late_kernel(
-    dev_ref,
-    grad_ref,
-    level_ref,
-    middle_slope_ref,
-    top_back_ref,
-    ids_ref,
-    middle_grad_ref,
-    *,
-    summit_factor,
+def lift_kernel(
+    dev_ref, grad_ref, middle_slope_ref, top_back_ref, ids_ref, slope_ref, *, summit_factor
 ):
-    _, groups, _, features = grad_ref.shape
-    middle_grad = jnp.zeros((features, features), F32)
-    for g in range(groups):
+    for g in range(grad_ref.shape[1]):
         for h in range(2):
             lifted = mm_tn(rows_onehot(ids_ref[h, g][:1], TOP_NODES), top_back_ref[...])
             level_total = grad_ref[h, g].astype(F32) + summit_factor * lifted
-            slope = (level_total * middle_slope_ref[h, g].astype(F32)).astype(BF16)
-            middle_grad = middle_grad + mm_tn(level_ref[h, g], slope)
+            slope_ref[h, g] = (level_total * middle_slope_ref[h, g].astype(F32)).astype(BF16)
+
+
+def late_kernel(dev_ref, level_ref, slope_ref, middle_grad_ref):
+    middle_grad = jnp.zeros(middle_grad_ref.shape, F32)
+    for g in range(level_ref.shape[1]):
+        for h in range(2):
+            middle_grad = middle_grad + mm_tn(level_ref[h, g], slope_ref[h, g])
     middle_grad_ref[...] = middle_grad
+
+
+def add_kernel(dev_ref, mine_ref, other_ref, out_ref):
+    rows = out_ref.shape[0]
+    total = mine_ref[...].astype(F32) + other_ref[:rows].astype(F32)
+    out_ref[...] = total.astype(BF16)
+
+
+def gather_kernel(dev_ref, parts_ref, out_ref):
+    total = parts_ref[0].astype(F32)
+    for peer in range(1, parts_ref.shape[0]):
+        total = total + parts_ref[peer].astype(F32)
+    out_ref[...] = total.astype(BF16)
+
+
+def copies_kernel(dev_ref, mine_ref, other_ref, out_ref):
+    total = (mine_ref[...].astype(F32) + other_ref[...].astype(F32)).astype(BF16)
+    for peer in range(out_ref.shape[0]):
+        out_ref[peer] = total
 
 
 def top_kernel(dev_ref, summit_in_ref, top_ref, summit_grad_ref):
@@ -594,7 +634,7 @@
     )
     core_in = lax.ppermute(core_pkt, "core", swap)
     far_in = lax.ppermute(far_pkt, ALL, beside)
-    mine = (keep + core_in[:half].astype(F32)).astype(BF16)
+    mine = call(add_kernel, shape((half, features), BF16), [dev, keep, core_in])
     other = lax.ppermute(mine, "row", swap)
     packet = call(
         spread_kernel,
@@ -612,6 +652,18 @@
     )
     mids = lax.all_to_all(packed, "near", 0, 0)
     mids_other = lax.ppermute(mids, "core", swap)
+    firsts = call(
+        first_kernel,
+        [
+            shape((groups, chunk, features), BF16),
+            shape((groups, 8, chunk), I32),
+            shape((groups, chunk, features), BF16),
+            shape((TOP_NODES, features), F32),
+        ],
+        [dev, mids, middle_weight],
+        subs=subs,
+        half=half,
+    )
     full = (2, groups, chunk, features)
     (
         decode_fetched,
@@ -638,7 +690,7 @@
         ],
         [
             dev,
-            mids,
+            *firsts,
             mids_other,
             core_in,
             far_pkt,
@@ -693,9 +745,9 @@
         level_rows=level_rows,
     )
     back_in = lax.ppermute(core_pkt, "core", swap)
-    mine = (keep + back_in[:half].astype(F32)).astype(BF16)
+    mine = call(add_kernel, shape((half, features), BF16), [dev, keep, back_in])
     other = lax.ppermute(mine, "row", swap)
-    total = (mine.astype(F32) + other.astype(F32)).astype(BF16)
+    total = call(add_kernel, shape((half, features), BF16), [dev, mine, other])
     away = lax.ppermute(total, "half", swap)
     packed = call(pair_kernel, shape((near, 2 * half, features), BF16), [dev, total, away])
     grads = lax.all_to_all(packed, "near", 0, 0)
@@ -734,23 +786,25 @@
         encode_factor=encode_factor,
     )
     received = lax.ppermute(send, "core", swap)
-    middle_grad = call(
-        late_kernel,
-        shape((features, features), F32),
-        [dev, level_back, level, middle_slope, top_back, ids],
+    lift_slope = call(
+        lift_kernel,
+        shape(full, BF16),
+        [dev, level_back, middle_slope, top_back, ids],
         summit_factor=summit_factor,
     )
-    share = (keep + received.astype(F32)).astype(BF16)
+    share = call(add_kernel, shape((features, features), BF16), [dev, keep, received])
     share = share.reshape(peers, features // peers, features)
     parts = lax.all_to_all(share, NEAR, 0, 0)
-    inside = jnp.sum(parts.astype(F32), axis=0).astype(BF16)
+    inside = call(gather_kernel, shape(parts.shape[1:], BF16), [dev, parts])
     away = lax.ppermute(inside, "half", swap)
-    summed = (inside.astype(F32) + away.astype(F32)).astype(BF16)
-    copies = jnp.broadcast_to(summed[None], parts.shape)
+    copies = call(copies_kernel, shape(parts.shape, BF16), [dev, inside, away])
     mine = lax.all_to_all(copies, NEAR, 0, 0).reshape(features, features)
     other = lax.ppermute(mine, "core", swap)
     summit_grad = call(
         top_kernel, shape((features, features), F32), [dev, summit_in, top]
+    )
+    middle_grad = call(
+        late_kernel, shape((features, features), F32), [dev, level, lift_slope]
     )
     encode_grad = jnp.where(core == 0, mine, other).astype(F32)
     decode_grad = jnp.where(core == 0, other, mine).astype(F32)

time: 125 us -> 125 us (level)
  local copies, waits for them, and re-layouts: 4.98 us -> 6.82 us
  other arithmetic: 4 us -> 2.65 us
    unnamed x40, local copies, waits for them, and re-layouts: 4.95 us -> 6.82 us
    pallas_call x12 -> x20, Pallas kernels: 16.4 us -> 17.4 us  [call(): pl.pallas_call(functools.partial(body, **static), out_shape=outs, in_spec...]
  transfers between devices with their start and end apart: 15 -> 15, of which waited for: 9 -> 8; matrix products, arithmetic and copies ran while one was open for 0% -> 0% of each run, Pallas kernels for 6% -> 7%
where the time goes in v6:
time: 125 us
  blocking collectives  44.6 us (36%)
  starting transfers between devices  33.2 us (27%)
  waiting for transfers between devices  19 us (15%)
  Pallas kernels  17.4 us (14%)
  local copies, waits for them, and re-layouts  6.82 us (5%)
  other arithmetic  2.65 us (2%)
    pallas_call x20, Pallas kernels, call(): pl.pallas_call(functools.partial(body, **static), out_shape=outs, in_spec...  17.4 us
    all_to_all x1, blocking collectives, shards(): parts = lax.all_to_all(share, NEAR, 0, 0)  12.8 us
    all_to_all x1, blocking collectives, shards(): mine = lax.all_to_all(copies, NEAR, 0, 0).reshape(features, features)  11.1 us
    ppermute x1, starting transfers between devices, shards(): back_in = lax.ppermute(core_pkt, 'core', swap)  10.7 us
    all_to_all x1, blocking collectives, shards(): mids = lax.all_to_all(packed, 'near', 0, 0)  10.6 us
    all_to_all x1, blocking collectives, shards(): grads = lax.all_to_all(packed, 'near', 0, 0)  10.1 us
    unnamed x40, local copies, waits for them, and re-layouts  6.82 us
    ppermute x2, waiting for transfers between devices, shards(): other = lax.ppermute(mine, 'row', swap)  5.56 us
  transfers between devices with their start and end apart: 15, of which 8 were waited for; matrix products, arithmetic and copies ran while one was open for 0% of the time, Pallas kernels for 7%

profile of v6, /device:TPU:0, one launch (start us, length us, event | category | flops | bytes accessed | tf_op | source)
XLA Modules:
  0.0 124.6 jit_solution(15148349925495114765)
XLA Ops:
  0.6 0.6 collective-permute-start
  1.2 0.7 collective-permute-start.1
  1.9 0.6 copy-done.17
  2.6 1.2 copy-done.2
  3.8 1.0 copy-done.7
  4.8 0.9 copy-done.10
  5.8 0.9 shard_map.182
  6.7 1.6 %shard_map.183 = (bf16[1024,512]{1,0:T(8,128)(2,1)S(1)}, bf16[200,512]{1,0:T(8,128)(2,1)S(1)}, bf16[136,512]{1,0:T(8,128)(2,1)S(1)}, f32[64,512]{1,0:T(8,128)S(1)}) custom-call(s32[1]{0:T(128)} %bitcast.dev_ref, bf16[128,512]{1,0:T(8,128)(2,1)S(1)} %collective-permute-done.partner_ref, bf16[128,512]{1,0:T(8,128)(2,1)S(1)} %collective-permute-done.1.far_ref, ...), custom_call_target="tpu_custom_call" | custom-call | tf_op jit(solution)/shard_map/pallas_call | solution.py:531
  8.3 4.0 %collective-permute-start.2 = (bf16[200,512]{1,0:T(8,128)(2,1)S(1)}, bf16[200,512]{1,0:T(8,128)(2,1)S(1)}, u32[]{:S(2)}, u32[]{:S(2)}) collective-permute-start(bf16[200,512]{1,0:T(8,128)(2,1)S(1)} %get-tuple-element.49), channel_id=1, source_target_pairs={{0,1},{1,0},{2,3},{3,2},{4,5},{5,4},{6,7},{7,6},{8,9},{9,8},{10,11... | collective-permute-start | bytes 614408 | tf_op jit(solution)/shard_map/ppermute | solution.py:635
  12.2 1.1 collective-permute-done.2.other_ref.core_ref
  13.3 1.5 %collective-permute-start.3 = (bf16[64,512]{1,0:T(8,128)(2,1)S(1)}, bf16[64,512]{1,0:T(8,128)(2,1)S(1)}, u32[]{:S(2)}, u32[]{:S(2)}) collective-permute-start(bf16[64,512]{1,0:T(8,128)(2,1)S(1)} %shard_map.184.mine_ref), channel_id=1, source_target_pairs={{0,2},{2,0},{1,3},{3,1},{4,6},{6,4},{5,7},{7,5},{8,10},{10,8},{9,1... | collective-permute-start | bytes 196616 | tf_op jit(solution)/shard_map/ppermute | solution.py:638
  14.8 2.9 %collective-permute-done.3.other_ref = bf16[64,512]{1,0:T(8,128)(2,1)S(1)} collective-permute-done((bf16[64,512]{1,0:T(8,128)(2,1)S(1)}, bf16[64,512]{1,0:T(8,128)(2,1)S(1)}, u32[]{:S(2)}, u32[]{:S(2)}) %collective-permute-start.3) | collective-permute-done | bytes 65568 | tf_op jit(solution)/shard_map/ppermute | solution.py:638
  17.8 0.2 shard_map.185.mine_ref
  17.9 3.6 %collective-permute-start.4 = (bf16[264,128]{1,0:T(8,128)(2,1)S(1)}, bf16[264,128]{1,0:T(8,128)(2,1)S(1)}, u32[]{:S(2)}, u32[]{:S(2)}) collective-permute-start(bf16[264,128]{1,0:T(8,128)(2,1)S(1)} %shard_map.185.mine_ref), channel_id=1, source_target_pairs={{0,16},{16,0},{1,17},{17,1},{2,18},{18,2},{3,19},{19,3},{4,20},{20... | collective-permute-start | bytes 202760 | tf_op jit(solution)/shard_map/ppermute | solution.py:646
  21.6 2.4 %collective-permute-done.4.away_ref = bf16[264,128]{1,0:T(8,128)(2,1)S(1)} collective-permute-done((bf16[264,128]{1,0:T(8,128)(2,1)S(1)}, bf16[264,128]{1,0:T(8,128)(2,1)S(1)}, u32[]{:S(2)}, u32[]{:S(2)}) %collective-permute-start.4) | collective-permute-done | bytes 67616 | tf_op jit(solution)/shard_map/ppermute | solution.py:646
  23.9 0.1 shard_map.186
  24.0 10.6 %all_to_all.20.mine_ref = bf16[4,528,128]{2,1,0:T(8,128)(2,1)S(1)} all-to-all(bf16[4,528,128]{2,1,0:T(8,128)(2,1)S(1)} %shard_map.186), channel_id=1, replica_groups=mesh['half'=2,'near'=4,'row'=2,'core'=2] {'near'}, dimensions={0} | all-to-all | bytes 1081344 | tf_op jit(solution)/shard_map/all_to_all | solution.py:653
  34.7 0.8 collective-permute-start.6
  35.5 1.1 shard_map.187
  36.5 0.0 collective-permute-done.5.other_ref
  36.6 0.6 copy-done.18
  37.3 3.4 %shard_map.188 = (bf16[512,512]{1,0:T(8,128)(2,1)S(1)}, bf16[512,512]{1,0:T(8,128)(2,1)S(1)}, bf16[512,512]{1,0:T(8,128)(2,1)S(1)}, f32[128,512]{1,0:T(8,128)S(1...) custom-call(s32[1]{0:T(128)} %bitcast.dev_ref, ...), custom_call_target="tpu_custom_call" | custom-call | tf_op jit(solution)/shard_map/pallas_call | solution.py:531
  40.7 0.7 collective-permute-start.7
  41.3 0.2 shard_map.190
  41.6 10.7 %collective-permute-start.8 = (bf16[192,512]{1,0:T(8,128)(2,1)S(1)}, bf16[192,512]{1,0:T(8,128)(2,1)S(1)}, u32[]{:S(2)}, u32[]{:S(2)}) collective-permute-start(bf16[192,512]{1,0:T(8,128)(2,1)S(1)} %get-tuple-element.65), channel_id=1, source_target_pairs={{0,1},{1,0},{2,3},{3,2},{4,5},{5,4},{6,7},{7,6},{8,9},{9,8},{10,11... | collective-permute-start | bytes 589832 | tf_op jit(solution)/shard_map/ppermute | solution.py:747
  52.3 1.1 collective-permute-done.8.other_ref.partnerin_ref
  53.4 3.6 %collective-permute-start.9 = (bf16[64,512]{1,0:T(8,128)(2,1)S(1)}, bf16[64,512]{1,0:T(8,128)(2,1)S(1)}, u32[]{:S(2)}, u32[]{:S(2)}) collective-permute-start(bf16[64,512]{1,0:T(8,128)(2,1)S(1)} %shard_map.191.mine_ref), channel_id=1, source_target_pairs={{0,2},{2,0},{1,3},{3,1},{4,6},{6,4},{5,7},{7,5},{8,10},{10,8},{9,1... | collective-permute-start | bytes 196616 | tf_op jit(solution)/shard_map/ppermute | solution.py:749
  57.0 2.6 %collective-permute-done.9.other_ref = bf16[64,512]{1,0:T(8,128)(2,1)S(1)} collective-permute-done((bf16[64,512]{1,0:T(8,128)(2,1)S(1)}, bf16[64,512]{1,0:T(8,128)(2,1)S(1)}, u32[]{:S(2)}, u32[]{:S(2)}) %collective-permute-start.9) | collective-permute-done | bytes 65568 | tf_op jit(solution)/shard_map/ppermute | solution.py:749
  59.7 4.9 %collective-permute-start.10 = (bf16[64,512]{1,0:T(8,128)(2,1)S(1)}, bf16[64,512]{1,0:T(8,128)(2,1)S(1)}, u32[]{:S(2)}, u32[]{:S(2)}) collective-permute-start(bf16[64,512]{1,0:T(8,128)(2,1)S(1)} %shard_map.192.mine_ref), channel_id=1, source_target_pairs={{0,16},{16,0},{1,17},{17,1},{2,18},{18,2},{3,19},{19,3},{4,20},{20... | collective-permute-start | bytes 196616 | tf_op jit(solution)/shard_map/ppermute | solution.py:751
  64.6 2.9 %collective-permute-done.10.away_ref = bf16[64,512]{1,0:T(8,128)(2,1)S(1)} collective-permute-done((bf16[64,512]{1,0:T(8,128)(2,1)S(1)}, bf16[64,512]{1,0:T(8,128)(2,1)S(1)}, u32[]{:S(2)}, u32[]{:S(2)}) %collective-permute-start.10) | collective-permute-done | bytes 65568 | tf_op jit(solution)/shard_map/ppermute | solution.py:751
  67.6 10.1 %all_to_all.21.mine_ref = bf16[4,128,512]{2,1,0:T(8,128)(2,1)S(1)} all-to-all(bf16[4,128,512]{2,1,0:T(8,128)(2,1)S(1)} %shard_map.193), channel_id=1, replica_groups=mesh['half'=2,'near'=4,'row'=2,'core'=2] {'near'}, dimensions={0} | all-to-all | bytes 1048576 | tf_op jit(solution)/shard_map/all_to_all | solution.py:753
  77.7 1.2 shard_map.194.slope_ref
  78.8 1.8 %shard_map.189 = (bf16[128,512]{1,0:T(8,128)(2,1)}, f32[512,512]{1,0:T(8,128)S(1)}, bf16[2,1,512,512]{3,2,1,0:T(8,128)(2,1)S(1)}, f32[512,512]{1,0:T(8,128)S(1)}) custom-call(s32[1]{0:T(128)} %bitcast.dev_ref, bf16[128,512]{1,0:T(8,128)(2,1)S(1)} %copy-done.11, s32[1,512]{1,0:T(1,128)S(1)} %bitcast.15, bf16[512,512]{1,0:T(8,128)(2,1)S(1)} %get-tuple-element.55.act_ref, ...), custom_call_target="tpu_custom_call" | custom-call | tf_op jit(solution)/shard_map/pallas_call | solution.py:531
  80.6 2.7 %shard_map.195 = (bf16[512,512]{1,0:T(8,128)(2,1)S(1)}, f32[512,512]{1,0:T(8,128)S(1)}, bf16[2,1,512,512]{3,2,1,0:T(8,128)(2,1)S(1)}, bf16[512,512]{1,0:T(8,128)(2,1)S(1)}, bf16[512,512]{1,0:T(8,128)(2,1)S(1)}) custom-call(s32[1]{0:T(128)} %bitcast.dev_ref, bf16[4,128,512]{2,1,0:T(8,128)(2,1)S(1)} %all_to_all.21.mine_ref, ...), custom_call_target="tpu_custom_call" | custom-call | tf_op jit(solution)/shard_map/pallas_call | solution.py:531
  83.3 0.6 collective-permute-start.12
  83.9 1.5 %collective-permute-done.12.other_ref = bf16[512,512]{1,0:T(8,128)(2,1)S(1)} collective-permute-done((bf16[512,512]{1,0:T(8,128)(2,1)S(1)}, bf16[512,512]{1,0:T(8,128)(2,1)S(1)}, u32[]{:S(2)}, u32[]{:S(2)}) %collective-permute-start.12) | collective-permute-done | bytes 524320 | tf_op jit(solution)/shard_map/ppermute | solution.py:788
  85.4 0.1 shard_map.196
  85.6 12.8 %all_to_all.22.parts_ref = bf16[8,64,512]{2,1,0:T(8,128)(2,1)S(1)} all-to-all(bf16[8,64,512]{2,1,0:T(8,128)(2,1)S(1)} %bitcast.11), channel_id=1, replica_groups=mesh['half'=2,'near'=4,'row'=2,'core'=2] {'near','row'}, dimensions={0} | all-to-all | bytes 1048576 | tf_op jit(solution)/shard_map/all_to_all | solution.py:797
  98.4 0.1 shard_map.197.mine_ref
  98.4 1.6 %collective-permute-start.13 = (bf16[64,512]{1,0:T(8,128)(2,1)S(1)}, bf16[64,512]{1,0:T(8,128)(2,1)S(1)}, u32[]{:S(2)}, u32[]{:S(2)}) collective-permute-start(bf16[64,512]{1,0:T(8,128)(2,1)S(1)} %shard_map.197.mine_ref), channel_id=1, source_target_pairs={{0,16},{16,0},{1,17},{17,1},{2,18},{18,2},{3,19},{19,3},{4,20},{20... | collective-permute-start | bytes 196616 | tf_op jit(solution)/shard_map/ppermute | solution.py:799
  100.0 4.3 %collective-permute-done.13.other_ref = bf16[64,512]{1,0:T(8,128)(2,1)S(1)} collective-permute-done((bf16[64,512]{1,0:T(8,128)(2,1)S(1)}, bf16[64,512]{1,0:T(8,128)(2,1)S(1)}, u32[]{:S(2)}, u32[]{:S(2)}) %collective-permute-start.13) | collective-permute-done | bytes 65568 | tf_op jit(solution)/shard_map/ppermute | solution.py:799
  104.4 11.1 %all_to_all.23 = bf16[8,64,512]{2,1,0:T(8,128)(2,1)} all-to-all(bf16[8,64,512]{2,1,0:T(8,128)(2,1)S(1)} %shard_map.198), channel_id=1, replica_groups=mesh['half'=2,'near'=4,'row'=2,'core'=2] {'near','row'}, dimensions={0} | all-to-all | bytes 1048576 | tf_op jit(solution)/shard_map/all_to_all | solution.py:801
  115.5 1.2 copy-done.4
  116.8 1.0 copy-done.9
  117.8 0.9 shard_map.199.slope_ref
  118.7 1.7 %shard_map.200 = f32[512,512]{1,0:T(8,128)} custom-call(s32[1]{0:T(128)} %bitcast.dev_ref, bf16[2,1,512,512]{3,2,1,0:T(8,128)(2,1)S(1)} %get-tuple-element.58.level_ref, bf16[2,1,512,512]{3,2,1,0:T(8,128)(2,1)S(1)} %shard_map.199.slope_ref), custom_call_target="tpu_custom_call" | custom-call | tf_op jit(solution)/shard_map/pallas_call | solution.py:531
  120.5 1.4 %shard_map.201 = f32[512,512]{1,0:T(8,128)} custom-call(s32[1]{0:T(128)} %bitcast.dev_ref, bf16[512,512]{1,0:T(8,128)(2,1)S(1)} %get-tuple-element.59.summit_in_ref, bf16[512,512]{1,0:T(8,128)(2,1)S(1)} %get-tuple-element.76.top_ref), custom_call_target="tpu_custom_call" | custom-call | tf_op jit(solution)/shard_map/pallas_call | solution.py:531
  121.9 2.7 %select_convert_fusion = (f32[512,512]{1,0:T(8,128)}, f32[512,512]{1,0:T(8,128)}) fusion(bf16[512,512]{1,0:T(8,128)(2,1)} %collective-permute-done.14, pred[]{:T(512)S(6)} %eq.6, bf16[8,64,512]{2,1,0:T(8,128)(2,1)} %all_to_all.23), kind=kLoop, calls=%fused_computation | loop fusion | flops 1048576 | bytes 3145729 | tf_op jit(solution)/shard_map/convert_element_type | solution.py:810
  (47 shorter events, 0.2 us)
Async XLA Ops:
  0.6 6.0 %collective-permute-start = (bf16[128,512]{1,0:T(8,128)(2,1)}, bf16[128,512]{1,0:T(8,128)(2,1)S(1)}, u32[]{:S(2)}, u32[]{:S(2)}) collective-permute-start(bf16[128,512]{1,0:T(8,128)(2,1)} %grid_ref.3), channel_id=1, source_target_pairs={{0,1},{1,0},{2,3},{3,2},{4,5},{5,4},{6,7},{7,6},{8,9},{9,8},{10,11... | collective-permute-start | bytes 393224 | tf_op jit(solution)/shard_map/ppermute | solution.py:588
  1.2 5.5 %collective-permute-start.1 = (bf16[128,512]{1,0:T(8,128)(2,1)}, bf16[128,512]{1,0:T(8,128)(2,1)S(1)}, u32[]{:S(2)}, u32[]{:S(2)}) collective-permute-start(bf16[128,512]{1,0:T(8,128)(2,1)} %grid_ref.3), channel_id=1, source_target_pairs={{1,2},{2,1},{3,4},{4,3},{5,6},{6,5},{7,8},{8,7},{9,10},{10,9},{11,... | collective-permute-start | bytes 393224 | tf_op jit(solution)/shard_map/ppermute | solution.py:587
  1.9 0.7 copy-start.17
  1.9 0.7 copy-start.14
  1.9 0.7 copy-start.16
  1.9 0.7 copy-start.19
  2.6 1.2 copy-start.2
  3.8 1.0 copy-start.7
  4.8 0.9 copy-start.10
  5.8 1.0 copy-start.12
  8.3 5.0 %collective-permute-start.2 = (bf16[200,512]{1,0:T(8,128)(2,1)S(1)}, bf16[200,512]{1,0:T(8,128)(2,1)S(1)}, u32[]{:S(2)}, u32[]{:S(2)}) collective-permute-start(bf16[200,512]{1,0:T(8,128)(2,1)S(1)} %get-tuple-element.49), channel_id=1, source_target_pairs={{0,1},{1,0},{2,3},{3,2},{4,5},{5,4},{6,7},{7,6},{8,9},{9,8},{10,11... | collective-permute-start | bytes 614408 | tf_op jit(solution)/shard_map/ppermute | solution.py:635
  13.3 4.4 %collective-permute-start.3 = (bf16[64,512]{1,0:T(8,128)(2,1)S(1)}, bf16[64,512]{1,0:T(8,128)(2,1)S(1)}, u32[]{:S(2)}, u32[]{:S(2)}) collective-permute-start(bf16[64,512]{1,0:T(8,128)(2,1)S(1)} %shard_map.184.mine_ref), channel_id=1, source_target_pairs={{0,2},{2,0},{1,3},{3,1},{4,6},{6,4},{5,7},{7,5},{8,10},{10,8},{9,1... | collective-permute-start | bytes 196616 | tf_op jit(solution)/shard_map/ppermute | solution.py:638
  17.9 6.0 %collective-permute-start.4 = (bf16[264,128]{1,0:T(8,128)(2,1)S(1)}, bf16[264,128]{1,0:T(8,128)(2,1)S(1)}, u32[]{:S(2)}, u32[]{:S(2)}) collective-permute-start(bf16[264,128]{1,0:T(8,128)(2,1)S(1)} %shard_map.185.mine_ref), channel_id=1, source_target_pairs={{0,16},{16,0},{1,17},{17,1},{2,18},{18,2},{3,19},{19,3},{4,20},{20... | collective-permute-start | bytes 202760 | tf_op jit(solution)/shard_map/ppermute | solution.py:646
  23.9 12.7 %copy-start.13 = (bf16[128,512]{1,0:T(8,128)(2,1)S(1)}, bf16[128,512]{1,0:T(8,128)(2,1)}, u32[]{:S(2)}) copy-start(bf16[128,512]{1,0:T(8,128)(2,1)} %cot_ref.1) | copy-start | bytes 393220
  24.0 11.5 %copy-start = (bf16[512,512]{1,0:T(8,128)(2,1)S(1)}, bf16[512,512]{1,0:T(8,128)(2,1)}, u32[]{:S(2)}) copy-start(bf16[512,512]{1,0:T(8,128)(2,1)} %middle_weight_ref.5) | copy-start | bytes 1572868
  24.0 12.6 %copy-start.6 = (bf16[512,512]{1,0:T(8,128)(2,1)S(1)}, bf16[512,512]{1,0:T(8,128)(2,1)}, u32[]{:S(2)}) copy-start(bf16[512,512]{1,0:T(8,128)(2,1)} %decode_weight_ref.1) | copy-start | bytes 1572868
  34.7 1.9 %collective-permute-start.5 = (bf16[4,528,128]{2,1,0:T(8,128)(2,1)S(1)}, bf16[4,528,128]{2,1,0:T(8,128)(2,1)S(1)}, u32[]{:S(2)}, u32[]{:S(2)}) collective-permute-start(bf16[4,528,128]{2,1,0:T(8,128)(2,1)S(1)} %all_to_all.20.mine_ref), channel_id=1, source_target_pairs={{0,1},{1,0},{2,3},{3,2},{4,5},{5,4},{6,7},{7,6},{8,9},{9,8},{10,11... | collective-permute-start | bytes 1622024 | tf_op jit(solution)/shard_map/ppermute | solution.py:654
  34.7 1.9 %copy-start.1 = (bf16[512,512]{1,0:T(8,128)(2,1)S(1)}, bf16[512,512]{1,0:T(8,128)(2,1)}, u32[]{:S(2)}) copy-start(bf16[512,512]{1,0:T(8,128)(2,1)} %summit_weight_ref.5) | copy-start | bytes 1572868
  34.7 2.0 %copy-start.5 = (bf16[512,512]{1,0:T(8,128)(2,1)S(1)}, bf16[512,512]{1,0:T(8,128)(2,1)}, u32[]{:S(2)}) copy-start(bf16[512,512]{1,0:T(8,128)(2,1)} %edges_ref.3) | copy-start | bytes 1572868
  34.7 1.9 %collective-permute-start.6 = (bf16[136,512]{1,0:T(8,128)(2,1)S(1)}, bf16[136,512]{1,0:T(8,128)(2,1)S(1)}, u32[]{:S(2)}, u32[]{:S(2)}) collective-permute-start(bf16[136,512]{1,0:T(8,128)(2,1)S(1)} %get-tuple-element.54.farpkt_ref), channel_id=1, source_target_pairs={{1,2},{2,1},{3,4},{4,3},{5,6},{6,5},{7,8},{8,7},{9,10},{10,9},{11,... | collective-permute-start | bytes 417800 | tf_op jit(solution)/shard_map/ppermute | solution.py:636
  36.6 0.7 copy-start.18
  36.6 0.7 copy-start.15
  40.7 0.7 collective-permute-start.7
  41.6 11.8 %collective-permute-start.8 = (bf16[192,512]{1,0:T(8,128)(2,1)S(1)}, bf16[192,512]{1,0:T(8,128)(2,1)S(1)}, u32[]{:S(2)}, u32[]{:S(2)}) collective-permute-start(bf16[192,512]{1,0:T(8,128)(2,1)S(1)} %get-tuple-element.65), channel_id=1, source_target_pairs={{0,1},{1,0},{2,3},{3,2},{4,5},{5,4},{6,7},{7,6},{8,9},{9,8},{10,11... | collective-permute-start | bytes 589832 | tf_op jit(solution)/shard_map/ppermute | solution.py:747
  53.4 6.2 %collective-permute-start.9 = (bf16[64,512]{1,0:T(8,128)(2,1)S(1)}, bf16[64,512]{1,0:T(8,128)(2,1)S(1)}, u32[]{:S(2)}, u32[]{:S(2)}) collective-permute-start(bf16[64,512]{1,0:T(8,128)(2,1)S(1)} %shard_map.191.mine_ref), channel_id=1, source_target_pairs={{0,2},{2,0},{1,3},{3,1},{4,6},{6,4},{5,7},{7,5},{8,10},{10,8},{9,1... | collective-permute-start | bytes 196616 | tf_op jit(solution)/shard_map/ppermute | solution.py:749
  59.7 7.9 %collective-permute-start.10 = (bf16[64,512]{1,0:T(8,128)(2,1)S(1)}, bf16[64,512]{1,0:T(8,128)(2,1)S(1)}, u32[]{:S(2)}, u32[]{:S(2)}) collective-permute-start(bf16[64,512]{1,0:T(8,128)(2,1)S(1)} %shard_map.192.mine_ref), channel_id=1, source_target_pairs={{0,16},{16,0},{1,17},{17,1},{2,18},{18,2},{3,19},{19,3},{4,20},{20... | collective-permute-start | bytes 196616 | tf_op jit(solution)/shard_map/ppermute | solution.py:751
  77.7 3.0 %collective-permute-start.11 = (bf16[4,128,512]{2,1,0:T(8,128)(2,1)S(1)}, bf16[4,128,512]{2,1,0:T(8,128)(2,1)S(1)}, u32[]{:S(2)}, u32[]{:S(2)}) collective-permute-start(bf16[4,128,512]{2,1,0:T(8,128)(2,1)S(1)} %all_to_all.21.mine_ref), channel_id=1, source_target_pairs={{0,1},{1,0},{2,3},{3,2},{4,5},{5,4},{6,7},{7,6},{8,9},{9,8},{10,11... | collective-permute-start | bytes 1572872 | tf_op jit(solution)/shard_map/ppermute | solution.py:754
  77.7 1.2 copy-start.11
  83.3 2.2 %copy-start.3 = (bf16[2,1,512,512]{3,2,1,0:T(8,128)(2,1)}, bf16[2,1,512,512]{3,2,1,0:T(8,128)(2,1)S(1)}, u32[]{:S(2)}) copy-start(bf16[2,1,512,512]{3,2,1,0:T(8,128)(2,1)S(1)} %get-tuple-element.74.grad_ref) | copy-start | bytes 3145732
  83.3 2.2 %copy-start.8 = (bf16[512,512]{1,0:T(8,128)(2,1)}, bf16[512,512]{1,0:T(8,128)(2,1)S(1)}, u32[]{:S(2)}) copy-start(bf16[512,512]{1,0:T(8,128)(2,1)S(1)} %get-tuple-element.75.top_back_ref) | copy-start | bytes 1572868
  83.3 2.1 %collective-permute-start.12 = (bf16[512,512]{1,0:T(8,128)(2,1)S(1)}, bf16[512,512]{1,0:T(8,128)(2,1)S(1)}, u32[]{:S(2)}, u32[]{:S(2)}) collective-permute-start(bf16[512,512]{1,0:T(8,128)(2,1)S(1)} %get-tuple-element.73), channel_id=1, source_target_pairs={{0,1},{1,0},{2,3},{3,2},{4,5},{5,4},{6,7},{7,6},{8,9},{9,8},{10,11... | collective-permute-start | bytes 1572872 | tf_op jit(solution)/shard_map/ppermute | solution.py:788
  98.4 5.9 %collective-permute-start.13 = (bf16[64,512]{1,0:T(8,128)(2,1)S(1)}, bf16[64,512]{1,0:T(8,128)(2,1)S(1)}, u32[]{:S(2)}, u32[]{:S(2)}) collective-permute-start(bf16[64,512]{1,0:T(8,128)(2,1)S(1)} %shard_map.197.mine_ref), channel_id=1, source_target_pairs={{0,16},{16,0},{1,17},{17,1},{2,18},{18,2},{3,19},{19,3},{4,20},{20... | collective-permute-start | bytes 196616 | tf_op jit(solution)/shard_map/ppermute | solution.py:799
  115.5 6.4 %collective-permute-start.14 = (bf16[512,512]{1,0:T(8,128)(2,1)}, bf16[512,512]{1,0:T(8,128)(2,1)}, u32[]{:S(2)}, u32[]{:S(2)}) collective-permute-start(bf16[512,512]{1,0:T(8,128)(2,1)} %bitcast.8), channel_id=1, source_target_pairs={{0,1},{1,0},{2,3},{3,2},{4,5},{5,4},{6,7},{7,6},{8,9},{9,8},{10,11... | collective-permute-start | bytes 1572872 | tf_op jit(solution)/shard_map/ppermute | solution.py:802
  115.5 1.2 copy-start.4
  116.7 1.0 copy-start.9

commit v7 on v6

--- a/solution.py
+++ b/solution.py
@@ -246,10 +246,10 @@
     core_ref,
     farpkt_ref,
     farin_ref,
-    cot_ref,
+    picks_ref,
+    returns_ref,
+    incoming_ref,
     edges_ref,
-    source_ref,
-    target_ref,
     decode_weight_ref,
     middle_weight_ref,
     summit_weight_ref,
@@ -267,7 +267,6 @@
     subs,
     level_rows,
     summit_factor,
-    decode_factor,
 ):
     device = dev_ref[0]
     core = device % 2
@@ -320,19 +319,14 @@
     )
     wide = (mids.astype(F32) + lifted).astype(BF16)
 
-    place = slots(source_ref[...], device, core, rows)
-    fetched = mm(cols_onehot(place, 3 * rows), wide).astype(BF16)
+    fetched = mm(picks_ref[...], wide).astype(BF16)
     pre = mm(fetched, decode_weight_ref[...]) + edges_ref[...].astype(F32)
     sig = sigmoid(pre)
-    grid_rows = cot_ref.shape[0]
-    raw = target_ref[...]
-    aimed = jnp.where(raw >= 0, raw - device * grid_rows, -1)
     fetched_ref[...] = fetched
     act_ref[...] = (pre * sig).astype(BF16)
-    incoming = mm(cols_onehot(aimed, grid_rows), cot_ref[...]) * decode_factor
-    slope = (incoming * (sig * (1.0 + pre * (1.0 - sig)))).astype(BF16)
+    slope = (incoming_ref[...] * (sig * (1.0 + pre * (1.0 - sig)))).astype(BF16)
     slope_ref[...] = slope
-    gathered = mm(rows_onehot(place, 3 * rows), slope).astype(BF16)
+    gathered = mm(returns_ref[...], slope).astype(BF16)
     returned = mm_nt(gathered, decode_weight_ref[...])
     own_ref[...] = returned[:rows]
     partner_ref[...] = returned[rows : 2 * rows]
@@ -344,7 +338,37 @@
     return sig * (1.0 + values * (1.0 - sig))
 
 
-def slope_kernel(dev_ref, fetched_ref, edges_ref, weight_ref, slope_ref):
+def slope_kernel(
+    dev_ref,
+    fetched_ref,
+    edges_ref,
+    weight_ref,
+    source_ref,
+    target_ref,
+    encode_target_ref,
+    cot_ref,
+    slope_ref,
+    picks_ref,
+    returns_ref,
+    aims_ref,
+    incoming_ref,
+    back_aims_ref,
+    *,
+    factor,
+):
+    device = dev_ref[0]
+    rows = cot_ref.shape[0]
+    place = slots(source_ref[...], device, device % 2, rows)
+    picks_ref[...] = cols_onehot(place, 3 * rows)
+    returns_ref[...] = rows_onehot(place, 3 * rows)
+    raw = target_ref[...]
+    aimed = jnp.where(raw >= 0, raw - device * rows, -1)
+    aims_ref[...] = rows_onehot(aimed, rows)
+    incoming_ref[...] = mm(cols_onehot(aimed, rows), cot_ref[...]) * factor
+    raw = encode_target_ref[...]
+    mesh_rows = back_aims_ref.shape[1]
+    aimed = jnp.where(raw >= 0, raw - device * mesh_rows, -1)
+    back_aims_ref[...] = cols_onehot(aimed, mesh_rows)
     pre = mm(fetched_ref[...], weight_ref[...]) + edges_ref[...].astype(F32)
     slope_ref[...] = silu_slope(pre).astype(BF16)
 
@@ -352,7 +376,7 @@
 def update_kernel(
     dev_ref,
     grid_ref,
-    target_ref,
+    aims_ref,
     act_ref,
     fetched_ref,
     slope_ref,
@@ -367,10 +391,7 @@
     *,
     factor,
 ):
-    grid_rows = grid_ref.shape[0]
-    raw = target_ref[...]
-    aimed = jnp.where(raw >= 0, raw - dev_ref[0] * grid_rows, -1)
-    summed = mm(rows_onehot(aimed, grid_rows), act_ref[...])
+    summed = mm(aims_ref[...], act_ref[...])
     update_ref[...] = (grid_ref[...].astype(F32) + factor * summed).astype(BF16)
     dgrad_ref[...] = mm_tn(fetched_ref[...], slope_ref[...])
     for h in range(2):
@@ -402,20 +423,30 @@
     pkt_ref[half:] = partner
 
 
+def tops_kernel(dev_ref, ids_ref, coarse_ref, farpkt_ref, tops_ref, lifts_ref, fine_ref):
+    for h in range(2):
+        for g in range(ids_ref.shape[1]):
+            tops_ref[h, g] = rows_onehot(ids_ref[h, g][:1], TOP_NODES)
+    lifts_ref[...] = cols_onehot(coarse_ref[...], TOP_NODES)
+    rows = fine_ref.shape[0]
+    own_fine, _ = node_ids(farpkt_ref[rows:, :rows])
+    fine_ref[...] = cols_onehot(own_fine, fine_ref.shape[1])
+
+
 def back_kernel(
     dev_ref,
     mine_ref,
     other_ref,
     middle_slope_ref,
     summit_slope_ref,
-    ids_ref,
+    tops_ref,
     sum_ref,
     partnerin_ref,
-    farpkt_ref,
-    coarse_ref,
+    fine_ref,
+    lifts_ref,
     fetched_ref,
     slope_ref,
-    target_ref,
+    aims_ref,
     dgrad_ref,
     middle_weight_ref,
     summit_weight_ref,
@@ -426,7 +457,6 @@
     top_back_ref,
     *,
     subs,
-    level_rows,
     summit_factor,
     middle_factor,
     encode_factor,
@@ -446,7 +476,7 @@
     total = jnp.zeros((TOP_NODES, features), F32)
     for g in range(groups):
         for h in range(2):
-            total = total + mm(rows_onehot(ids_ref[h, g][:1], TOP_NODES), grad_ref[h, g])
+            total = total + mm(tops_ref[h, g], grad_ref[h, g])
     summit_slope = (total * summit_slope_ref[...]).astype(BF16)
     top_ref[...] = summit_slope
     summit_back = mm_nt(summit_slope, summit_weight_ref[...]).astype(BF16)
@@ -457,21 +487,15 @@
         pieces = [ref[h, tile // group, pl.ds(spot, half)] for h in range(2)]
         return jnp.concatenate(pieces, axis=0).astype(F32)
 
-    level_total = own(grad_ref) + summit_factor * mm(
-        cols_onehot(coarse_ref[...], TOP_NODES), summit_back
-    )
+    level_total = own(grad_ref) + summit_factor * mm(lifts_ref[...], summit_back)
     slope = (level_total * own(middle_slope_ref)).astype(BF16)
     back = (level_total + mm_nt(slope, middle_weight_ref[...])).astype(BF16)
-    rows = sum_ref.shape[0]
-    own_fine, _ = node_ids(farpkt_ref[rows:, :rows])
     mesh_total = (
         sum_ref[...]
         + partnerin_ref[half:].astype(F32)
-        + middle_factor * mm(cols_onehot(own_fine, level_rows), back)
-    )
-    raw = target_ref[...]
-    aimed = jnp.where(raw >= 0, raw - device * rows, -1)
-    upstream = mm(cols_onehot(aimed, rows), mesh_total.astype(BF16)) * encode_factor
+        + middle_factor * mm(fine_ref[...], back)
+    )
+    upstream = mm(aims_ref[...], mesh_total.astype(BF16)) * encode_factor
     slope = (upstream * slope_ref[...].astype(F32)).astype(BF16)
     egrad = mm_tn(fetched_ref[...], slope)
     dgrad = dgrad_ref[...]
@@ -480,11 +504,11 @@
 
 
 def lift_kernel(
-    dev_ref, grad_ref, middle_slope_ref, top_back_ref, ids_ref, slope_ref, *, summit_factor
+    dev_ref, grad_ref, middle_slope_ref, top_back_ref, tops_ref, slope_ref, *, summit_factor
 ):
     for g in range(grad_ref.shape[1]):
         for h in range(2):
-            lifted = mm_tn(rows_onehot(ids_ref[h, g][:1], TOP_NODES), top_back_ref[...])
+            lifted = mm_tn(tops_ref[h, g], top_back_ref[...])
             level_total = grad_ref[h, g].astype(F32) + summit_factor * lifted
             slope_ref[h, g] = (level_total * middle_slope_ref[h, g].astype(F32)).astype(BF16)
 
@@ -644,8 +668,27 @@
         factor=middle_factor,
     )
     away = lax.ppermute(packet, "half", swap)
-    slope = call(
-        slope_kernel, shape((edges, features), BF16), [dev, fetched, edges_in, weight_in]
+    slope, picks, returns, aims, incoming, back_aims = call(
+        slope_kernel,
+        [
+            shape((edges, features), BF16),
+            shape((decode_source.shape[0], 3 * mesh_rows), BF16),
+            shape((3 * mesh_rows, decode_source.shape[0]), BF16),
+            shape((rows, decode_source.shape[0]), BF16),
+            shape(decode_edges.shape, F32),
+            shape((edges, mesh_rows), BF16),
+        ],
+        [
+            dev,
+            fetched,
+            edges_in,
+            weight_in,
+            decode_source[None],
+            decode_target[None],
+            encode_target[None],
+            cotangent,
+        ],
+        factor=decode_factor,
     )
     packed = call(
         pair_kernel, shape((near, 2 * packet.shape[0], LANES), BF16), [dev, packet, away]
@@ -695,10 +738,10 @@
             core_in,
             far_pkt,
             far_in,
-            cotangent,
+            picks,
+            returns,
+            incoming,
             decode_edges,
-            decode_source[None],
-            decode_target[None],
             decode_weight,
             middle_weight,
             summit_weight,
@@ -709,7 +752,6 @@
         subs=subs,
         level_rows=level_rows,
         summit_factor=summit_factor,
-        decode_factor=decode_factor,
     )
     far_back = lax.ppermute(far, ALL, beside)
     grid_update, dgrad, middle_slope, summit_slope = call(
@@ -723,7 +765,7 @@
         [
             dev,
             grid_feats,
-            decode_target[None],
+            aims,
             decode_act,
             decode_fetched,
             decode_slope,
@@ -749,6 +791,15 @@
     other = lax.ppermute(mine, "row", swap)
     total = call(add_kernel, shape((half, features), BF16), [dev, mine, other])
     away = lax.ppermute(total, "half", swap)
+    tops, lifts, fines = call(
+        tops_kernel,
+        [
+            shape((2, groups, TOP_NODES, chunk), BF16),
+            shape((level_rows, TOP_NODES), BF16),
+            shape((mesh_rows, level_rows), BF16),
+        ],
+        [dev, ids, owner_coarse[None], far_pkt],
+    )
     packed = call(pair_kernel, shape((near, 2 * half, features), BF16), [dev, total, away])
     grads = lax.all_to_all(packed, "near", 0, 0)
     grads_other = lax.ppermute(grads, "core", swap)
@@ -767,20 +818,19 @@
             grads_other,
             middle_slope,
             summit_slope,
-            ids,
+            tops,
             grad_sum,
             back_in,
-            far_pkt,
-            owner_coarse[None],
+            fines,
+            lifts,
             fetched,
             slope,
-            encode_target[None],
+            back_aims,
             dgrad,
             middle_weight,
             summit_weight,
         ],
         subs=subs,
-        level_rows=level_rows,
         summit_factor=summit_factor,
         middle_factor=middle_factor,
         encode_factor=encode_factor,
@@ -789,7 +839,7 @@
     lift_slope = call(
         lift_kernel,
         shape(full, BF16),
-        [dev, level_back, middle_slope, top_back, ids],
+        [dev, level_back, middle_slope, top_back, tops],
         summit_factor=summit_factor,
     )
     share = call(add_kernel, shape((features, features), BF16), [dev, keep, received])

time: 125 us -> 124 us (level)
  starting transfers between devices: 33.2 us -> 30.2 us
    ppermute x1, starting transfers between devices: 10.7 us -> 8.75 us  [shards(): back_in = lax.ppermute(core_pkt, 'core', swap)]
    pallas_call x20 -> x21, Pallas kernels: 17.4 us -> 18.4 us  [call(): pl.pallas_call(functools.partial(body, **static), out_shape=outs, in_spec...]
    unnamed x40 -> x48, local copies, waits for them, and re-layouts: 6.82 us -> 7.24 us
  transfers between devices with their start and end apart: 15 -> 15, of which waited for: 8 -> 8; matrix products, arithmetic and copies ran while one was open for 0% -> 0% of each run, Pallas kernels for 7% -> 8%
where the time goes in v7:
time: 124 us; the launch traced here: 123 us
  blocking collectives  44.4 us (36%)
  starting transfers between devices  30.2 us (24%)
  waiting for transfers between devices  19.1 us (15%)
  Pallas kernels  18.4 us (15%)
  local copies, waits for them, and re-layouts  7.24 us (6%)
  other arithmetic  2.65 us (2%)
    pallas_call x21, Pallas kernels, call(): pl.pallas_call(functools.partial(body, **static), out_shape=outs, in_spec...  18.4 us
    all_to_all x1, blocking collectives, shards(): parts = lax.all_to_all(share, NEAR, 0, 0)  13.2 us
    all_to_all x1, blocking collectives, shards(): mine = lax.all_to_all(copies, NEAR, 0, 0).reshape(features, features)  11.1 us
    all_to_all x1, blocking collectives, shards(): mids = lax.all_to_all(packed, 'near', 0, 0)  10.6 us
    all_to_all x1, blocking collectives, shards(): grads = lax.all_to_all(packed, 'near', 0, 0)  9.53 us
    ppermute x1, starting transfers between devices, shards(): back_in = lax.ppermute(core_pkt, 'core', swap)  8.75 us
    unnamed x48, local copies, waits for them, and re-layouts  7.24 us
    ppermute x2, waiting for transfers between devices, shards(): other = lax.ppermute(mine, 'row', swap)  5.56 us
  transfers between devices with their start and end apart: 15, of which 8 were waited for; matrix products, arithmetic and copies ran while one was open for 0% of the time, Pallas kernels for 8%

profile of v7, /device:TPU:0, one launch (start us, length us, event | category | flops | bytes accessed | tf_op | source)
XLA Modules:
  0.0 123.0 jit_solution(13052916801777944717)
XLA Ops:
  0.6 0.6 collective-permute-start
  1.2 0.7 collective-permute-start.1
  1.9 0.6 copy-done.20
  2.6 1.2 copy-done.6
  3.8 1.0 copy-done.13
  4.8 0.9 copy-done.14
  5.8 0.9 shard_map.182
  6.7 1.6 %shard_map.183 = (bf16[1024,512]{1,0:T(8,128)(2,1)S(1)}, bf16[200,512]{1,0:T(8,128)(2,1)S(1)}, bf16[136,512]{1,0:T(8,128)(2,1)S(1)}, f32[64,512]{1,0:T(8,128)S(1)}) custom-call(s32[1]{0:T(128)} %bitcast.dev_ref, bf16[128,512]{1,0:T(8,128)(2,1)S(1)} %collective-permute-done.partner_ref, bf16[128,512]{1,0:T(8,128)(2,1)S(1)} %collective-permute-done.1.far_ref, ...), custom_call_target="tpu_custom_call" | custom-call | tf_op jit(solution)/shard_map/pallas_call | solution.py:555
  8.3 4.0 %collective-permute-start.2 = (bf16[200,512]{1,0:T(8,128)(2,1)S(1)}, bf16[200,512]{1,0:T(8,128)(2,1)S(1)}, u32[]{:S(2)}, u32[]{:S(2)}) collective-permute-start(bf16[200,512]{1,0:T(8,128)(2,1)S(1)} %get-tuple-element.60), channel_id=1, source_target_pairs={{0,1},{1,0},{2,3},{3,2},{4,5},{5,4},{6,7},{7,6},{8,9},{9,8},{10,11... | collective-permute-start | bytes 614408 | tf_op jit(solution)/shard_map/ppermute | solution.py:659
  12.2 1.1 collective-permute-done.2.other_ref.core_ref
  13.3 1.5 %collective-permute-start.3 = (bf16[64,512]{1,0:T(8,128)(2,1)S(1)}, bf16[64,512]{1,0:T(8,128)(2,1)S(1)}, u32[]{:S(2)}, u32[]{:S(2)}) collective-permute-start(bf16[64,512]{1,0:T(8,128)(2,1)S(1)} %shard_map.185.mine_ref), channel_id=1, source_target_pairs={{0,2},{2,0},{1,3},{3,1},{4,6},{6,4},{5,7},{7,5},{8,10},{10,8},{9,1... | collective-permute-start | bytes 196616 | tf_op jit(solution)/shard_map/ppermute | solution.py:662
  14.8 2.9 %collective-permute-done.3.other_ref = bf16[64,512]{1,0:T(8,128)(2,1)S(1)} collective-permute-done((bf16[64,512]{1,0:T(8,128)(2,1)S(1)}, bf16[64,512]{1,0:T(8,128)(2,1)S(1)}, u32[]{:S(2)}, u32[]{:S(2)}) %collective-permute-start.3) | collective-permute-done | bytes 65568 | tf_op jit(solution)/shard_map/ppermute | solution.py:662
  17.8 0.2 shard_map.186.mine_ref
  17.9 3.7 %collective-permute-start.4 = (bf16[264,128]{1,0:T(8,128)(2,1)S(1)}, bf16[264,128]{1,0:T(8,128)(2,1)S(1)}, u32[]{:S(2)}, u32[]{:S(2)}) collective-permute-start(bf16[264,128]{1,0:T(8,128)(2,1)S(1)} %shard_map.186.mine_ref), channel_id=1, source_target_pairs={{0,16},{16,0},{1,17},{17,1},{2,18},{18,2},{3,19},{19,3},{4,20},{20... | collective-permute-start | bytes 202760 | tf_op jit(solution)/shard_map/ppermute | solution.py:670
  21.6 2.3 %collective-permute-done.4.away_ref = bf16[264,128]{1,0:T(8,128)(2,1)S(1)} collective-permute-done((bf16[264,128]{1,0:T(8,128)(2,1)S(1)}, bf16[264,128]{1,0:T(8,128)(2,1)S(1)}, u32[]{:S(2)}, u32[]{:S(2)}) %collective-permute-start.4) | collective-permute-done | bytes 67616 | tf_op jit(solution)/shard_map/ppermute | solution.py:670
  23.9 0.1 shard_map.187
  24.0 10.6 %all_to_all.20.mine_ref = bf16[4,528,128]{2,1,0:T(8,128)(2,1)S(1)} all-to-all(bf16[4,528,128]{2,1,0:T(8,128)(2,1)S(1)} %shard_map.187), channel_id=1, replica_groups=mesh['half'=2,'near'=4,'row'=2,'core'=2] {'near'}, dimensions={0} | all-to-all | bytes 1081344 | tf_op jit(solution)/shard_map/all_to_all | solution.py:696
  34.7 0.7 collective-permute-start.6
  35.4 0.7 copy-done.22
  36.0 1.8 %shard_map.184 = (bf16[1024,512]{1,0:T(8,128)(2,1)S(1)}, bf16[512,384]{1,0:T(8,128)(2,1)S(1)}, bf16[384,512]{1,0:T(8,128)(2,1)S(1)}, bf16[128,512]{1,0:T(8,128)(...) custom-call(s32[1]{0:T(128)} %bitcast.dev_ref, bf16[1024,512]{1,0:T(8,128)(2,1)S(1)} %get-tuple-element.57.fetched_ref, ...), custom_call_target="tpu_custom_call" | custom-call | tf_op jit(solution)/shard_map/pallas_call | solution.py:555
  37.9 1.1 shard_map.188
  39.1 3.3 %shard_map.189 = (bf16[512,512]{1,0:T(8,128)(2,1)S(1)}, bf16[512,512]{1,0:T(8,128)(2,1)S(1)}, bf16[512,512]{1,0:T(8,128)(2,1)S(1)}, f32[128,512]{1,0:T(8,128)S(1...) custom-call(s32[1]{0:T(128)} %bitcast.dev_ref, ...), custom_call_target="tpu_custom_call" | custom-call | tf_op jit(solution)/shard_map/pallas_call | solution.py:555
  42.4 0.7 collective-permute-start.7
  43.1 0.2 shard_map.191
  43.3 8.7 %collective-permute-start.8 = (bf16[192,512]{1,0:T(8,128)(2,1)S(1)}, bf16[192,512]{1,0:T(8,128)(2,1)S(1)}, u32[]{:S(2)}, u32[]{:S(2)}) collective-permute-start(bf16[192,512]{1,0:T(8,128)(2,1)S(1)} %get-tuple-element.79), channel_id=1, source_target_pairs={{0,1},{1,0},{2,3},{3,2},{4,5},{5,4},{6,7},{7,6},{8,9},{9,8},{10,11... | collective-permute-start | bytes 589832 | tf_op jit(solution)/shard_map/ppermute | solution.py:789
  52.0 1.1 collective-permute-done.8.other_ref.partnerin_ref
  53.1 3.0 %collective-permute-start.9 = (bf16[64,512]{1,0:T(8,128)(2,1)S(1)}, bf16[64,512]{1,0:T(8,128)(2,1)S(1)}, u32[]{:S(2)}, u32[]{:S(2)}) collective-permute-start(bf16[64,512]{1,0:T(8,128)(2,1)S(1)} %shard_map.192.mine_ref), channel_id=1, source_target_pairs={{0,2},{2,0},{1,3},{3,1},{4,6},{6,4},{5,7},{7,5},{8,10},{10,8},{9,1... | collective-permute-start | bytes 196616 | tf_op jit(solution)/shard_map/ppermute | solution.py:791
  56.1 2.6 %collective-permute-done.9.other_ref = bf16[64,512]{1,0:T(8,128)(2,1)S(1)} collective-permute-done((bf16[64,512]{1,0:T(8,128)(2,1)S(1)}, bf16[64,512]{1,0:T(8,128)(2,1)S(1)}, u32[]{:S(2)}, u32[]{:S(2)}) %collective-permute-start.9) | collective-permute-done | bytes 65568 | tf_op jit(solution)/shard_map/ppermute | solution.py:791
  58.8 4.9 %collective-permute-start.10 = (bf16[64,512]{1,0:T(8,128)(2,1)S(1)}, bf16[64,512]{1,0:T(8,128)(2,1)S(1)}, u32[]{:S(2)}, u32[]{:S(2)}) collective-permute-start(bf16[64,512]{1,0:T(8,128)(2,1)S(1)} %shard_map.193.mine_ref), channel_id=1, source_target_pairs={{0,16},{16,0},{1,17},{17,1},{2,18},{18,2},{3,19},{19,3},{4,20},{20... | collective-permute-start | bytes 196616 | tf_op jit(solution)/shard_map/ppermute | solution.py:793
  63.7 2.9 %collective-permute-done.10.away_ref = bf16[64,512]{1,0:T(8,128)(2,1)S(1)} collective-permute-done((bf16[64,512]{1,0:T(8,128)(2,1)S(1)}, bf16[64,512]{1,0:T(8,128)(2,1)S(1)}, u32[]{:S(2)}, u32[]{:S(2)}) %collective-permute-start.10) | collective-permute-done | bytes 65568 | tf_op jit(solution)/shard_map/ppermute | solution.py:793
  66.7 9.5 %all_to_all.21.mine_ref = bf16[4,128,512]{2,1,0:T(8,128)(2,1)S(1)} all-to-all(bf16[4,128,512]{2,1,0:T(8,128)(2,1)S(1)} %shard_map.194), channel_id=1, replica_groups=mesh['half'=2,'near'=4,'row'=2,'core'=2] {'near'}, dimensions={0} | all-to-all | bytes 1048576 | tf_op jit(solution)/shard_map/all_to_all | solution.py:804
  76.2 0.6 shard_map.195
  76.8 0.3 copy-done.15
  77.1 1.8 %shard_map.190 = (bf16[128,512]{1,0:T(8,128)(2,1)}, f32[512,512]{1,0:T(8,128)S(1)}, bf16[2,1,512,512]{3,2,1,0:T(8,128)(2,1)S(1)}, f32[512,512]{1,0:T(8,128)S(1)}) custom-call(s32[1]{0:T(128)} %bitcast.dev_ref, bf16[128,512]{1,0:T(8,128)(2,1)S(1)} %copy-done.15, bf16[128,512]{1,0:T(8,128)(2,1)S(1)} %get-tuple-element.58.aims_ref, ...), custom_call_target="tpu_custom_call" | custom-call | tf_op jit(solution)/shard_map/pallas_call | solution.py:555
  78.9 2.6 %shard_map.196 = (bf16[512,512]{1,0:T(8,128)(2,1)S(1)}, f32[512,512]{1,0:T(8,128)S(1)}, bf16[2,1,512,512]{3,2,1,0:T(8,128)(2,1)S(1)}, bf16[512,512]{1,0:T(8,128)(2,1)S(1)}, bf16[512,512]{1,0:T(8,128)(2,1)S(1)}) custom-call(s32[1]{0:T(128)} %bitcast.dev_ref, bf16[4,128,512]{2,1,0:T(8,128)(2,1)S(1)} %all_to_all.21.mine_ref, ...), custom_call_target="tpu_custom_call" | custom-call | tf_op jit(solution)/shard_map/pallas_call | solution.py:555
  81.6 0.3 collective-permute-start.12
  81.9 1.7 %collective-permute-done.12.other_ref = bf16[512,512]{1,0:T(8,128)(2,1)S(1)} collective-permute-done((bf16[512,512]{1,0:T(8,128)(2,1)S(1)}, bf16[512,512]{1,0:T(8,128)(2,1)S(1)}, u32[]{:S(2)}, u32[]{:S(2)}) %collective-permute-start.12) | collective-permute-done | bytes 524320 | tf_op jit(solution)/shard_map/ppermute | solution.py:838
  83.6 0.1 shard_map.197
  83.7 13.2 %all_to_all.22.parts_ref = bf16[8,64,512]{2,1,0:T(8,128)(2,1)S(1)} all-to-all(bf16[8,64,512]{2,1,0:T(8,128)(2,1)S(1)} %bitcast.11), channel_id=1, replica_groups=mesh['half'=2,'near'=4,'row'=2,'core'=2] {'near','row'}, dimensions={0} | all-to-all | bytes 1048576 | tf_op jit(solution)/shard_map/all_to_all | solution.py:847
  96.9 1.6 %collective-permute-start.13 = (bf16[64,512]{1,0:T(8,128)(2,1)S(1)}, bf16[64,512]{1,0:T(8,128)(2,1)S(1)}, u32[]{:S(2)}, u32[]{:S(2)}) collective-permute-start(bf16[64,512]{1,0:T(8,128)(2,1)S(1)} %shard_map.198.mine_ref), channel_id=1, source_target_pairs={{0,16},{16,0},{1,17},{17,1},{2,18},{18,2},{3,19},{19,3},{4,20},{20... | collective-permute-start | bytes 196616 | tf_op jit(solution)/shard_map/ppermute | solution.py:849
  98.5 4.3 %collective-permute-done.13.other_ref = bf16[64,512]{1,0:T(8,128)(2,1)S(1)} collective-permute-done((bf16[64,512]{1,0:T(8,128)(2,1)S(1)}, bf16[64,512]{1,0:T(8,128)(2,1)S(1)}, u32[]{:S(2)}, u32[]{:S(2)}) %collective-permute-start.13) | collective-permute-done | bytes 65568 | tf_op jit(solution)/shard_map/ppermute | solution.py:849
  102.9 11.1 %all_to_all.23 = bf16[8,64,512]{2,1,0:T(8,128)(2,1)} all-to-all(bf16[8,64,512]{2,1,0:T(8,128)(2,1)S(1)} %shard_map.199), channel_id=1, replica_groups=mesh['half'=2,'near'=4,'row'=2,'core'=2] {'near','row'}, dimensions={0} | all-to-all | bytes 1048576 | tf_op jit(solution)/shard_map/all_to_all | solution.py:851
  114.0 1.2 copy-done.5
  115.3 1.0 copy-done.12
  116.3 0.9 shard_map.200.slope_ref
  117.2 1.7 %shard_map.201 = f32[512,512]{1,0:T(8,128)} custom-call(s32[1]{0:T(128)} %bitcast.dev_ref, bf16[2,1,512,512]{3,2,1,0:T(8,128)(2,1)S(1)} %get-tuple-element.72.level_ref, bf16[2,1,512,512]{3,2,1,0:T(8,128)(2,1)S(1)} %shard_map.200.slope_ref), custom_call_target="tpu_custom_call" | custom-call | tf_op jit(solution)/shard_map/pallas_call | solution.py:555
  118.9 1.4 %shard_map.202 = f32[512,512]{1,0:T(8,128)} custom-call(s32[1]{0:T(128)} %bitcast.dev_ref, bf16[512,512]{1,0:T(8,128)(2,1)S(1)} %copy-done.3, bf16[512,512]{1,0:T(8,128)(2,1)S(1)} %copy-done.10), custom_call_target="tpu_custom_call" | custom-call | tf_op jit(solution)/shard_map/pallas_call | solution.py:555
  120.4 2.7 %select_convert_fusion = (f32[512,512]{1,0:T(8,128)}, f32[512,512]{1,0:T(8,128)}) fusion(bf16[512,512]{1,0:T(8,128)(2,1)} %collective-permute-done.14, pred[]{:T(512)S(6)} %eq.6, bf16[8,64,512]{2,1,0:T(8,128)(2,1)} %all_to_all.23), kind=kLoop, calls=%fused_computation | loop fusion | flops 1048576 | bytes 3145729 | tf_op jit(solution)/shard_map/convert_element_type | solution.py:860
  (56 shorter events, 0.4 us)
Async XLA Ops:
  0.6 6.0 %collective-permute-start = (bf16[128,512]{1,0:T(8,128)(2,1)}, bf16[128,512]{1,0:T(8,128)(2,1)S(1)}, u32[]{:S(2)}, u32[]{:S(2)}) collective-permute-start(bf16[128,512]{1,0:T(8,128)(2,1)} %grid_ref.3), channel_id=1, source_target_pairs={{0,1},{1,0},{2,3},{3,2},{4,5},{5,4},{6,7},{7,6},{8,9},{9,8},{10,11... | collective-permute-start | bytes 393224 | tf_op jit(solution)/shard_map/ppermute | solution.py:612
  1.2 5.5 %collective-permute-start.1 = (bf16[128,512]{1,0:T(8,128)(2,1)}, bf16[128,512]{1,0:T(8,128)(2,1)S(1)}, u32[]{:S(2)}, u32[]{:S(2)}) collective-permute-start(bf16[128,512]{1,0:T(8,128)(2,1)} %grid_ref.3), channel_id=1, source_target_pairs={{1,2},{2,1},{3,4},{4,3},{5,6},{6,5},{7,8},{8,7},{9,10},{10,9},{11,... | collective-permute-start | bytes 393224 | tf_op jit(solution)/shard_map/ppermute | solution.py:611
  1.9 0.7 copy-start.20
  1.9 0.7 copy-start.18
  1.9 0.7 copy-start.19
  1.9 0.7 copy-start.23
  2.6 1.2 copy-start.6
  3.8 1.0 copy-start.13
  4.8 0.9 copy-start.14
  5.8 0.9 copy-start.16
  8.3 5.0 %collective-permute-start.2 = (bf16[200,512]{1,0:T(8,128)(2,1)S(1)}, bf16[200,512]{1,0:T(8,128)(2,1)S(1)}, u32[]{:S(2)}, u32[]{:S(2)}) collective-permute-start(bf16[200,512]{1,0:T(8,128)(2,1)S(1)} %get-tuple-element.60), channel_id=1, source_target_pairs={{0,1},{1,0},{2,3},{3,2},{4,5},{5,4},{6,7},{7,6},{8,9},{9,8},{10,11... | collective-permute-start | bytes 614408 | tf_op jit(solution)/shard_map/ppermute | solution.py:659
  13.3 4.4 %collective-permute-start.3 = (bf16[64,512]{1,0:T(8,128)(2,1)S(1)}, bf16[64,512]{1,0:T(8,128)(2,1)S(1)}, u32[]{:S(2)}, u32[]{:S(2)}) collective-permute-start(bf16[64,512]{1,0:T(8,128)(2,1)S(1)} %shard_map.185.mine_ref), channel_id=1, source_target_pairs={{0,2},{2,0},{1,3},{3,1},{4,6},{6,4},{5,7},{7,5},{8,10},{10,8},{9,1... | collective-permute-start | bytes 196616 | tf_op jit(solution)/shard_map/ppermute | solution.py:662
  17.9 6.0 %collective-permute-start.4 = (bf16[264,128]{1,0:T(8,128)(2,1)S(1)}, bf16[264,128]{1,0:T(8,128)(2,1)S(1)}, u32[]{:S(2)}, u32[]{:S(2)}) collective-permute-start(bf16[264,128]{1,0:T(8,128)(2,1)S(1)} %shard_map.186.mine_ref), channel_id=1, source_target_pairs={{0,16},{16,0},{1,17},{17,1},{2,18},{18,2},{3,19},{19,3},{4,20},{20... | collective-permute-start | bytes 202760 | tf_op jit(solution)/shard_map/ppermute | solution.py:670
  24.0 11.3 %copy-start.17 = (bf16[128,512]{1,0:T(8,128)(2,1)S(1)}, bf16[128,512]{1,0:T(8,128)(2,1)}, u32[]{:S(2)}) copy-start(bf16[128,512]{1,0:T(8,128)(2,1)} %cot_ref.1) | copy-start | bytes 393220
  34.7 4.3 %collective-permute-start.5 = (bf16[4,528,128]{2,1,0:T(8,128)(2,1)S(1)}, bf16[4,528,128]{2,1,0:T(8,128)(2,1)S(1)}, u32[]{:S(2)}, u32[]{:S(2)}) collective-permute-start(bf16[4,528,128]{2,1,0:T(8,128)(2,1)S(1)} %all_to_all.20.mine_ref), channel_id=1, source_target_pairs={{0,1},{1,0},{2,3},{3,2},{4,5},{5,4},{6,7},{7,6},{8,9},{9,8},{10,11... | collective-permute-start | bytes 1622024 | tf_op jit(solution)/shard_map/ppermute | solution.py:697
  34.7 4.3 %collective-permute-start.6 = (bf16[136,512]{1,0:T(8,128)(2,1)S(1)}, bf16[136,512]{1,0:T(8,128)(2,1)S(1)}, u32[]{:S(2)}, u32[]{:S(2)}) collective-permute-start(bf16[136,512]{1,0:T(8,128)(2,1)S(1)} %get-tuple-element.65.farpkt_ref), channel_id=1, source_target_pairs={{1,2},{2,1},{3,4},{4,3},{5,6},{6,5},{7,8},{8,7},{9,10},{10,9},{11,... | collective-permute-start | bytes 417800 | tf_op jit(solution)/shard_map/ppermute | solution.py:660
  35.3 0.7 copy-start.22
  35.3 0.7 copy-start.21
  36.0 1.8 %copy-start = (bf16[512,512]{1,0:T(8,128)(2,1)S(1)}, bf16[512,512]{1,0:T(8,128)(2,1)}, u32[]{:S(2)}) copy-start(bf16[512,512]{1,0:T(8,128)(2,1)} %middle_weight_ref.5) | copy-start | bytes 1572868
  36.0 3.0 %copy-start.8 = (bf16[512,512]{1,0:T(8,128)(2,1)S(1)}, bf16[512,512]{1,0:T(8,128)(2,1)}, u32[]{:S(2)}) copy-start(bf16[512,512]{1,0:T(8,128)(2,1)} %decode_weight_ref.1) | copy-start | bytes 1572868
  37.9 1.1 copy-start.1
  37.9 1.2 copy-start.7
  42.4 34.4 %copy-start.2 = (bf16[512,512]{1,0:T(8,128)(2,1)}, bf16[512,512]{1,0:T(8,128)(2,1)S(1)}, u32[]{:S(2)}) copy-start(bf16[512,512]{1,0:T(8,128)(2,1)S(1)} %get-tuple-element.73.summit_in_ref) | copy-start | bytes 1572868
  42.4 0.7 collective-permute-start.7
  43.3 9.8 %collective-permute-start.8 = (bf16[192,512]{1,0:T(8,128)(2,1)S(1)}, bf16[192,512]{1,0:T(8,128)(2,1)S(1)}, u32[]{:S(2)}, u32[]{:S(2)}) collective-permute-start(bf16[192,512]{1,0:T(8,128)(2,1)S(1)} %get-tuple-element.79), channel_id=1, source_target_pairs={{0,1},{1,0},{2,3},{3,2},{4,5},{5,4},{6,7},{7,6},{8,9},{9,8},{10,11... | collective-permute-start | bytes 589832 | tf_op jit(solution)/shard_map/ppermute | solution.py:789
  53.1 5.6 %collective-permute-start.9 = (bf16[64,512]{1,0:T(8,128)(2,1)S(1)}, bf16[64,512]{1,0:T(8,128)(2,1)S(1)}, u32[]{:S(2)}, u32[]{:S(2)}) collective-permute-start(bf16[64,512]{1,0:T(8,128)(2,1)S(1)} %shard_map.192.mine_ref), channel_id=1, source_target_pairs={{0,2},{2,0},{1,3},{3,1},{4,6},{6,4},{5,7},{7,5},{8,10},{10,8},{9,1... | collective-permute-start | bytes 196616 | tf_op jit(solution)/shard_map/ppermute | solution.py:791
  58.8 7.9 %collective-permute-start.10 = (bf16[64,512]{1,0:T(8,128)(2,1)S(1)}, bf16[64,512]{1,0:T(8,128)(2,1)S(1)}, u32[]{:S(2)}, u32[]{:S(2)}) collective-permute-start(bf16[64,512]{1,0:T(8,128)(2,1)S(1)} %shard_map.193.mine_ref), channel_id=1, source_target_pairs={{0,16},{16,0},{1,17},{17,1},{2,18},{18,2},{3,19},{19,3},{4,20},{20... | collective-permute-start | bytes 196616 | tf_op jit(solution)/shard_map/ppermute | solution.py:793
  76.2 0.9 copy-start.15
  76.2 2.7 %collective-permute-start.11 = (bf16[4,128,512]{2,1,0:T(8,128)(2,1)S(1)}, bf16[4,128,512]{2,1,0:T(8,128)(2,1)S(1)}, u32[]{:S(2)}, u32[]{:S(2)}) collective-permute-start(bf16[4,128,512]{2,1,0:T(8,128)(2,1)S(1)} %all_to_all.21.mine_ref), channel_id=1, source_target_pairs={{0,1},{1,0},{2,3},{3,2},{4,5},{5,4},{6,7},{7,6},{8,9},{9,8},{10,11... | collective-permute-start | bytes 1572872 | tf_op jit(solution)/shard_map/ppermute | solution.py:805
  81.6 2.1 %copy-start.4 = (bf16[2,1,512,512]{3,2,1,0:T(8,128)(2,1)}, bf16[2,1,512,512]{3,2,1,0:T(8,128)(2,1)S(1)}, u32[]{:S(2)}) copy-start(bf16[2,1,512,512]{3,2,1,0:T(8,128)(2,1)S(1)} %get-tuple-element.92.grad_ref) | copy-start | bytes 3145732
  81.6 2.1 %copy-start.9 = (bf16[512,512]{1,0:T(8,128)(2,1)}, bf16[512,512]{1,0:T(8,128)(2,1)S(1)}, u32[]{:S(2)}) copy-start(bf16[512,512]{1,0:T(8,128)(2,1)S(1)} %get-tuple-element.94.top_ref) | copy-start | bytes 1572868
  81.6 2.1 %copy-start.11 = (bf16[512,512]{1,0:T(8,128)(2,1)}, bf16[512,512]{1,0:T(8,128)(2,1)S(1)}, u32[]{:S(2)}) copy-start(bf16[512,512]{1,0:T(8,128)(2,1)S(1)} %get-tuple-element.93.top_back_ref) | copy-start | bytes 1572868
  81.6 2.0 %collective-permute-start.12 = (bf16[512,512]{1,0:T(8,128)(2,1)S(1)}, bf16[512,512]{1,0:T(8,128)(2,1)S(1)}, u32[]{:S(2)}, u32[]{:S(2)}) collective-permute-start(bf16[512,512]{1,0:T(8,128)(2,1)S(1)} %get-tuple-element.91), channel_id=1, source_target_pairs={{0,1},{1,0},{2,3},{3,2},{4,5},{5,4},{6,7},{7,6},{8,9},{9,8},{10,11... | collective-permute-start | bytes 1572872 | tf_op jit(solution)/shard_map/ppermute | solution.py:838
  96.9 5.9 %collective-permute-start.13 = (bf16[64,512]{1,0:T(8,128)(2,1)S(1)}, bf16[64,512]{1,0:T(8,128)(2,1)S(1)}, u32[]{:S(2)}, u32[]{:S(2)}) collective-permute-start(bf16[64,512]{1,0:T(8,128)(2,1)S(1)} %shard_map.198.mine_ref), channel_id=1, source_target_pairs={{0,16},{16,0},{1,17},{17,1},{2,18},{18,2},{3,19},{19,3},{4,20},{20... | collective-permute-start | bytes 196616 | tf_op jit(solution)/shard_map/ppermute | solution.py:849
  114.0 6.3 %collective-permute-start.14 = (bf16[512,512]{1,0:T(8,128)(2,1)}, bf16[512,512]{1,0:T(8,128)(2,1)}, u32[]{:S(2)}, u32[]{:S(2)}) collective-permute-start(bf16[512,512]{1,0:T(8,128)(2,1)} %bitcast.8), channel_id=1, source_target_pairs={{0,1},{1,0},{2,3},{3,2},{4,5},{5,4},{6,7},{7,6},{8,9},{9,8},{10,11... | collective-permute-start | bytes 1572872 | tf_op jit(solution)/shard_map/ppermute | solution.py:852
  114.0 1.2 copy-start.5
  115.3 1.0 copy-start.12
  117.2 1.7 %copy-start.3 = (bf16[512,512]{1,0:T(8,128)(2,1)S(1)}, bf16[512,512]{1,0:T(8,128)(2,1)}, u32[]{:S(2)}) copy-start(bf16[512,512]{1,0:T(8,128)(2,1)} %copy-done.2) | copy-start | bytes 1572868
  117.2 1.7 %copy-start.10 = (bf16[512,512]{1,0:T(8,128)(2,1)S(1)}, bf16[512,512]{1,0:T(8,128)(2,1)}, u32[]{:S(2)}) copy-start(bf16[512,512]{1,0:T(8,128)(2,1)} %copy-done.9) | copy-start | bytes 1572868

commit v8 on v7

--- a/solution.py
+++ b/solution.py
@@ -159,35 +159,50 @@
     farpkt_ref[mesh_rows:] = nodes_ref[...]
 
 
-def spread_kernel(dev_ref, mine_ref, other_ref, coarse_ref, out_ref, *, subs, factor):
+def pack_kernel(dev_ref, keep_ref, core_ref, coarse_ref, out_ref, *, subs):
     device = dev_ref[0]
     core = device % 2
     tile = device // subs
-    half, features = mine_ref.shape
+    half, features = keep_ref.shape
     group = features // half
-    total = mine_ref[...].astype(F32) + other_ref[...].astype(F32)
-    mid = (factor * total).astype(BF16)
     level_rows = coarse_ref.shape[1]
+    out_ref[:half] = (keep_ref[...] + core_ref[:half].astype(F32)).astype(BF16)
     j = lax.broadcasted_iota(I32, (level_rows, features), 0) - core * half
     lane = lax.broadcasted_iota(I32, (level_rows, features), 1) - (tile % group) * half
     sel = (j == lane) & (j >= 0) & (j < half)
     codes = mm(coarse_split(coarse_ref[...]), jnp.where(sel, 1.0, 0.0).astype(BF16))
-    lanes = out_ref.shape[1]
-    strips = features // lanes
+    out_ref[half:] = codes.astype(BF16)[:8]
+
+
+def row_total(dev_ref, mine_ref, first_ref, second_ref, half, subs):
+    row = (dev_ref[0] % subs) // 2
+    mine = mine_ref[:half].astype(F32)
+    second = second_ref[:half].astype(F32)
+    return row, first_ref[:half].astype(F32) + jnp.where(row == 0, mine, second)
+
+
+def spread_kernel(dev_ref, mine_ref, first_ref, second_ref, out_ref, *, subs, half, factor):
+    row, total = row_total(dev_ref, mine_ref, first_ref, second_ref, half, subs)
+    mid = (factor * total).astype(BF16)
+    codes = jnp.where(row == 0, mine_ref[half:].astype(F32), second_ref[half:].astype(F32))
+    lanes = out_ref.shape[2]
+    strips = mine_ref.shape[1] // lanes
     tail = jnp.concatenate(
         [codes[r : r + 1, i * lanes : (i + 1) * lanes] for r in range(2) for i in range(strips)],
         axis=0,
     ).astype(BF16)
-    for i in range(strips):
-        out_ref[i * half : (i + 1) * half] = mid[:, i * lanes : (i + 1) * lanes]
-    out_ref[strips * half :] = tail
-
-
-def pair_kernel(dev_ref, mine_ref, away_ref, out_ref):
-    span = mine_ref.shape[0]
     for peer in range(out_ref.shape[0]):
-        out_ref[peer, :span] = mine_ref[...]
-        out_ref[peer, span:] = away_ref[...]
+        for i in range(strips):
+            out_ref[peer, i * half : (i + 1) * half] = mid[:, i * lanes : (i + 1) * lanes]
+        out_ref[peer, strips * half :] = tail
+
+
+def respread_kernel(dev_ref, mine_ref, first_ref, second_ref, out_ref, *, subs):
+    half = mine_ref.shape[0]
+    _, total = row_total(dev_ref, mine_ref, first_ref, second_ref, half, subs)
+    total = total.astype(BF16)
+    for peer in range(out_ref.shape[0]):
+        out_ref[peer] = total
 
 
 def placed_blocks(tile, near, group, half):
@@ -594,6 +609,8 @@
     near = tiles // 2
     edges = encode_source.shape[0]
     swap = [(0, 1), (1, 0)]
+    turn = [(1, 0), (3, 2), (0, 3), (2, 1)]
+    over = [(1, 3), (3, 1)]
     beside = []
     for left in range(1, devices - 1, 2):
         beside += [(left, left + 1), (left + 1, left)]
@@ -658,16 +675,14 @@
     )
     core_in = lax.ppermute(core_pkt, "core", swap)
     far_in = lax.ppermute(far_pkt, ALL, beside)
-    mine = call(add_kernel, shape((half, features), BF16), [dev, keep, core_in])
-    other = lax.ppermute(mine, "row", swap)
-    packet = call(
-        spread_kernel,
-        shape(((features // LANES) * half + 8, LANES), BF16),
-        [dev, mine, other, owner_coarse[None]],
+    mine = call(
+        pack_kernel,
+        shape((half + 8, features), BF16),
+        [dev, keep, core_in, owner_coarse[None]],
         subs=subs,
-        factor=middle_factor,
-    )
-    away = lax.ppermute(packet, "half", swap)
+    )
+    first_in = lax.ppermute(mine, ("half", "row"), turn)
+    second_in = lax.ppermute(mine, ("half", "row"), over)
     slope, picks, returns, aims, incoming, back_aims = call(
         slope_kernel,
         [
@@ -690,10 +705,16 @@
         ],
         factor=decode_factor,
     )
+    span = (features // LANES) * half + 8
     packed = call(
-        pair_kernel, shape((near, 2 * packet.shape[0], LANES), BF16), [dev, packet, away]
-    )
-    mids = lax.all_to_all(packed, "near", 0, 0)
+        spread_kernel,
+        shape((2 * near, span, LANES), BF16),
+        [dev, mine, first_in, second_in],
+        subs=subs,
+        half=half,
+        factor=middle_factor,
+    )
+    mids = lax.all_to_all(packed, NEAR, 0, 0).reshape(near, 2 * span, LANES)
     mids_other = lax.ppermute(mids, "core", swap)
     firsts = call(
         first_kernel,
@@ -788,9 +809,8 @@
     )
     back_in = lax.ppermute(core_pkt, "core", swap)
     mine = call(add_kernel, shape((half, features), BF16), [dev, keep, back_in])
-    other = lax.ppermute(mine, "row", swap)
-    total = call(add_kernel, shape((half, features), BF16), [dev, mine, other])
-    away = lax.ppermute(total, "half", swap)
+    first_in = lax.ppermute(mine, ("half", "row"), turn)
+    second_in = lax.ppermute(mine, ("half", "row"), over)
     tops, lifts, fines = call(
         tops_kernel,
         [
@@ -800,8 +820,13 @@
         ],
         [dev, ids, owner_coarse[None], far_pkt],
     )
-    packed = call(pair_kernel, shape((near, 2 * half, features), BF16), [dev, total, away])
-    grads = lax.all_to_all(packed, "near", 0, 0)
+    packed = call(
+        respread_kernel,
+        shape((2 * near, half, features), BF16),
+        [dev, mine, first_in, second_in],
+        subs=subs,
+    )
+    grads = lax.all_to_all(packed, NEAR, 0, 0).reshape(near, 2 * half, features)
     grads_other = lax.ppermute(grads, "core", swap)
     send, keep, level_back, top, top_back = call(
         back_kernel,

time: 124 us -> 126 us (1.016)
  blocking collectives: 44.4 us -> 58.3 us
  waiting for transfers between devices: 19.1 us -> 11.2 us
  starting transfers between devices: 30.2 us -> 27 us
    all_to_all x2, blocking collectives: 20.2 us -> 34.7 us  [the longest x1 17.5 us: shards(): mids = lax.all_to_all(packed, NEAR, 0, 0).reshape(near, 2 * span, LANES)]
    ppermute x4, waiting for transfers between devices: 10.9 us -> 2.65 us  [the longest x2 2.65 us: shards(): first_in = lax.ppermute(mine, ('half', 'row'), turn)]
    ppermute x4, starting transfers between devices: 13.1 us -> 10.8 us  [the longest x2 9.51 us: shards(): first_in = lax.ppermute(mine, ('half', 'row'), turn)]
    pallas_call x21 -> x19, Pallas kernels: 18.4 us -> 18.4 us  [call(): pl.pallas_call(functools.partial(body, **static), out_shape=outs, in_spec...]
  transfers between devices with their start and end apart: 15 -> 15, of which waited for: 8 -> 6; matrix products, arithmetic and copies ran while one was open for 0% -> 0% of each run, Pallas kernels for 8% -> 8%
where the time goes in v8:
time: 126 us
  blocking collectives  58.3 us (46%)
  starting transfers between devices  27 us (21%)
  Pallas kernels  18.4 us (15%)
  waiting for transfers between devices  11.2 us (9%)
  local copies, waits for them, and re-layouts  7.24 us (6%)
  other arithmetic  2.65 us (2%)
    pallas_call x19, Pallas kernels, call(): pl.pallas_call(functools.partial(body, **static), out_shape=outs, in_spec...  18.4 us
    all_to_all x1, blocking collectives, shards(): mids = lax.all_to_all(packed, NEAR, 0, 0).reshape(near, 2 * span, LANES)  17.5 us
    all_to_all x1, blocking collectives, shards(): grads = lax.all_to_all(packed, NEAR, 0, 0).reshape(near, 2 * half, features)  17.2 us
    all_to_all x1, blocking collectives, shards(): parts = lax.all_to_all(share, NEAR, 0, 0)  12.5 us
    all_to_all x1, blocking collectives, shards(): mine = lax.all_to_all(copies, NEAR, 0, 0).reshape(features, features)  11.1 us
    ppermute x2, starting transfers between devices, shards(): first_in = lax.ppermute(mine, ('half', 'row'), turn)  9.51 us
    ppermute x1, starting transfers between devices, shards(): back_in = lax.ppermute(core_pkt, 'core', swap)  8.14 us
    unnamed x48, local copies, waits for them, and re-layouts  7.24 us
  transfers between devices with their start and end apart: 15, of which 6 were waited for; matrix products, arithmetic and copies ran while one was open for 0% of the time, Pallas kernels for 8%

profile of v8, /device:TPU:0, one launch (start us, length us, event | category | flops | bytes accessed | tf_op | source)
XLA Modules:
  0.0 125.8 jit_solution(14926465203361211423)
XLA Ops:
  0.6 0.6 collective-permute-start
  1.2 0.7 collective-permute-start.1
  1.9 0.6 copy-done.20
  2.6 1.2 copy-done.6
  3.8 1.0 copy-done.13
  4.8 0.9 copy-done.14
  5.8 0.9 shard_map.182
  6.7 1.6 %shard_map.183 = (bf16[1024,512]{1,0:T(8,128)(2,1)S(1)}, bf16[200,512]{1,0:T(8,128)(2,1)S(1)}, bf16[136,512]{1,0:T(8,128)(2,1)S(1)}, f32[64,512]{1,0:T(8,128)S(1)}) custom-call(s32[1]{0:T(128)} %bitcast.dev_ref, bf16[128,512]{1,0:T(8,128)(2,1)S(1)} %collective-permute-done.partner_ref, bf16[128,512]{1,0:T(8,128)(2,1)S(1)} %collective-permute-done.1.far_ref, ...), custom_call_target="tpu_custom_call" | custom-call | tf_op jit(solution)/shard_map/pallas_call | solution.py:570
  8.3 4.0 %collective-permute-start.2 = (bf16[200,512]{1,0:T(8,128)(2,1)S(1)}, bf16[200,512]{1,0:T(8,128)(2,1)S(1)}, u32[]{:S(2)}, u32[]{:S(2)}) collective-permute-start(bf16[200,512]{1,0:T(8,128)(2,1)S(1)} %get-tuple-element.60), channel_id=1, source_target_pairs={{0,1},{1,0},{2,3},{3,2},{4,5},{5,4},{6,7},{7,6},{8,9},{9,8},{10,11... | collective-permute-start | bytes 614408 | tf_op jit(solution)/shard_map/ppermute | solution.py:676
  12.2 1.1 collective-permute-done.2.core_ref
  13.3 0.2 shard_map.185.mine_ref
  13.5 3.5 %collective-permute-start.3 = (bf16[72,512]{1,0:T(8,128)(2,1)S(1)}, bf16[72,512]{1,0:T(8,128)(2,1)S(1)}, u32[]{:S(2)}, u32[]{:S(2)}) collective-permute-start(bf16[72,512]{1,0:T(8,128)(2,1)S(1)} %shard_map.185.mine_ref), channel_id=1, source_target_pairs={{2,0},{18,16},{0,18},{16,2},{3,1},{19,17},{1,19},{17,3},{6,4},{22,... | collective-permute-start | bytes 221192 | tf_op jit(solution)/shard_map/ppermute | solution.py:684
  16.9 0.7 collective-permute-start.4
  17.6 1.4 %collective-permute-done.3.first_ref = bf16[72,512]{1,0:T(8,128)(2,1)S(1)} collective-permute-done((bf16[72,512]{1,0:T(8,128)(2,1)S(1)}, bf16[72,512]{1,0:T(8,128)(2,1)S(1)}, u32[]{:S(2)}, u32[]{:S(2)}) %collective-permute-start.3) | collective-permute-done | bytes 73760 | tf_op jit(solution)/shard_map/ppermute | solution.py:684
  19.0 0.1 shard_map.186
  19.1 17.5 %all_to_all.20 = bf16[8,264,128]{2,1,0:T(8,128)(2,1)S(1)} all-to-all(bf16[8,264,128]{2,1,0:T(8,128)(2,1)S(1)} %shard_map.186), channel_id=1, replica_groups=mesh['half'=2,'near'=4,'row'=2,'core'=2] {'near','row'}, dimensions={0} | all-to-all | bytes 1081344 | tf_op jit(solution)/shard_map/all_to_all | solution.py:717
  36.6 0.7 collective-permute-start.6
  37.3 0.7 copy-done.22
  38.0 1.8 %shard_map.184 = (bf16[1024,512]{1,0:T(8,128)(2,1)S(1)}, bf16[512,384]{1,0:T(8,128)(2,1)S(1)}, bf16[384,512]{1,0:T(8,128)(2,1)S(1)}, bf16[128,512]{1,0:T(8,128)(...) custom-call(s32[1]{0:T(128)} %bitcast.dev_ref, bf16[1024,512]{1,0:T(8,128)(2,1)S(1)} %get-tuple-element.57.fetched_ref, ...), custom_call_target="tpu_custom_call" | custom-call | tf_op jit(solution)/shard_map/pallas_call | solution.py:570
  39.9 1.1 shard_map.187
  41.0 0.1 copy-done.7
  41.1 3.3 %shard_map.188 = (bf16[512,512]{1,0:T(8,128)(2,1)S(1)}, bf16[512,512]{1,0:T(8,128)(2,1)S(1)}, bf16[512,512]{1,0:T(8,128)(2,1)S(1)}, f32[128,512]{1,0:T(8,128)S(1...) custom-call(s32[1]{0:T(128)} %bitcast.dev_ref, ...), custom_call_target="tpu_custom_call" | custom-call | tf_op jit(solution)/shard_map/pallas_call | solution.py:570
  44.3 0.7 collective-permute-start.7
  45.0 0.2 shard_map.190
  45.3 8.1 %collective-permute-start.8 = (bf16[192,512]{1,0:T(8,128)(2,1)S(1)}, bf16[192,512]{1,0:T(8,128)(2,1)S(1)}, u32[]{:S(2)}, u32[]{:S(2)}) collective-permute-start(bf16[192,512]{1,0:T(8,128)(2,1)S(1)} %get-tuple-element.79), channel_id=1, source_target_pairs={{0,1},{1,0},{2,3},{3,2},{4,5},{5,4},{6,7},{7,6},{8,9},{9,8},{10,11... | collective-permute-start | bytes 589832 | tf_op jit(solution)/shard_map/ppermute | solution.py:810
  53.4 1.1 collective-permute-done.8.other_ref.partnerin_ref
  54.5 6.0 %collective-permute-start.9 = (bf16[64,512]{1,0:T(8,128)(2,1)S(1)}, bf16[64,512]{1,0:T(8,128)(2,1)S(1)}, u32[]{:S(2)}, u32[]{:S(2)}) collective-permute-start(bf16[64,512]{1,0:T(8,128)(2,1)S(1)} %shard_map.191.mine_ref), channel_id=1, source_target_pairs={{2,0},{18,16},{0,18},{16,2},{3,1},{19,17},{1,19},{17,3},{6,4},{22,... | collective-permute-start | bytes 196616 | tf_op jit(solution)/shard_map/ppermute | solution.py:812
  60.5 0.7 collective-permute-start.10
  61.2 1.2 collective-permute-done.9.first_ref
  62.5 17.2 %all_to_all.21 = bf16[8,64,512]{2,1,0:T(8,128)(2,1)S(1)} all-to-all(bf16[8,64,512]{2,1,0:T(8,128)(2,1)S(1)} %shard_map.192), channel_id=1, replica_groups=mesh['half'=2,'near'=4,'row'=2,'core'=2] {'near','row'}, dimensions={0} | all-to-all | bytes 1048576 | tf_op jit(solution)/shard_map/all_to_all | solution.py:829
  79.7 0.6 shard_map.193
  80.2 0.3 copy-done.15
  80.6 1.8 %shard_map.189 = (bf16[128,512]{1,0:T(8,128)(2,1)}, f32[512,512]{1,0:T(8,128)S(1)}, bf16[2,1,512,512]{3,2,1,0:T(8,128)(2,1)S(1)}, f32[512,512]{1,0:T(8,128)S(1)}) custom-call(s32[1]{0:T(128)} %bitcast.dev_ref, bf16[128,512]{1,0:T(8,128)(2,1)S(1)} %copy-done.15, bf16[128,512]{1,0:T(8,128)(2,1)S(1)} %get-tuple-element.58.aims_ref, ...), custom_call_target="tpu_custom_call" | custom-call | tf_op jit(solution)/shard_map/pallas_call | solution.py:570
  82.4 2.6 %shard_map.194 = (bf16[512,512]{1,0:T(8,128)(2,1)S(1)}, f32[512,512]{1,0:T(8,128)S(1)}, bf16[2,1,512,512]{3,2,1,0:T(8,128)(2,1)S(1)}, bf16[512,512]{1,0:T(8,128)(2,1)S(1)}, bf16[512,512]{1,0:T(8,128)(2,1)S(1)}) custom-call(s32[1]{0:T(128)} %bitcast.dev_ref, bf16[4,128,512]{2,1,0:T(8,128)(2,1)S(1)} %bitcast.16, ...), custom_call_target="tpu_custom_call" | custom-call | tf_op jit(solution)/shard_map/pallas_call | solution.py:570
  85.0 0.3 collective-permute-start.12
  85.3 1.7 %collective-permute-done.12.other_ref = bf16[512,512]{1,0:T(8,128)(2,1)S(1)} collective-permute-done((bf16[512,512]{1,0:T(8,128)(2,1)S(1)}, bf16[512,512]{1,0:T(8,128)(2,1)S(1)}, u32[]{:S(2)}, u32[]{:S(2)}) %collective-permute-start.12) | collective-permute-done | bytes 524320 | tf_op jit(solution)/shard_map/ppermute | solution.py:863
  87.0 0.1 shard_map.195
  87.1 12.5 %all_to_all.22.parts_ref = bf16[8,64,512]{2,1,0:T(8,128)(2,1)S(1)} all-to-all(bf16[8,64,512]{2,1,0:T(8,128)(2,1)S(1)} %bitcast.17), channel_id=1, replica_groups=mesh['half'=2,'near'=4,'row'=2,'core'=2] {'near','row'}, dimensions={0} | all-to-all | bytes 1048576 | tf_op jit(solution)/shard_map/all_to_all | solution.py:872
  99.6 0.1 shard_map.196.mine_ref
  99.7 1.3 %collective-permute-start.13 = (bf16[64,512]{1,0:T(8,128)(2,1)S(1)}, bf16[64,512]{1,0:T(8,128)(2,1)S(1)}, u32[]{:S(2)}, u32[]{:S(2)}) collective-permute-start(bf16[64,512]{1,0:T(8,128)(2,1)S(1)} %shard_map.196.mine_ref), channel_id=1, source_target_pairs={{0,16},{16,0},{1,17},{17,1},{2,18},{18,2},{3,19},{19,3},{4,20},{20... | collective-permute-start | bytes 196616 | tf_op jit(solution)/shard_map/ppermute | solution.py:874
  101.0 4.6 %collective-permute-done.13.other_ref = bf16[64,512]{1,0:T(8,128)(2,1)S(1)} collective-permute-done((bf16[64,512]{1,0:T(8,128)(2,1)S(1)}, bf16[64,512]{1,0:T(8,128)(2,1)S(1)}, u32[]{:S(2)}, u32[]{:S(2)}) %collective-permute-start.13) | collective-permute-done | bytes 65568 | tf_op jit(solution)/shard_map/ppermute | solution.py:874
  105.7 11.1 %all_to_all.23 = bf16[8,64,512]{2,1,0:T(8,128)(2,1)} all-to-all(bf16[8,64,512]{2,1,0:T(8,128)(2,1)S(1)} %shard_map.197), channel_id=1, replica_groups=mesh['half'=2,'near'=4,'row'=2,'core'=2] {'near','row'}, dimensions={0} | all-to-all | bytes 1048576 | tf_op jit(solution)/shard_map/all_to_all | solution.py:876
  116.8 1.2 copy-done.5
  118.0 1.0 copy-done.12
  119.1 0.9 shard_map.198.slope_ref
  120.0 1.7 %shard_map.199 = f32[512,512]{1,0:T(8,128)} custom-call(s32[1]{0:T(128)} %bitcast.dev_ref, bf16[2,1,512,512]{3,2,1,0:T(8,128)(2,1)S(1)} %get-tuple-element.72.level_ref, bf16[2,1,512,512]{3,2,1,0:T(8,128)(2,1)S(1)} %shard_map.198.slope_ref), custom_call_target="tpu_custom_call" | custom-call | tf_op jit(solution)/shard_map/pallas_call | solution.py:570
  121.7 1.4 %shard_map.200 = f32[512,512]{1,0:T(8,128)} custom-call(s32[1]{0:T(128)} %bitcast.dev_ref, bf16[512,512]{1,0:T(8,128)(2,1)S(1)} %copy-done.3, bf16[512,512]{1,0:T(8,128)(2,1)S(1)} %copy-done.10), custom_call_target="tpu_custom_call" | custom-call | tf_op jit(solution)/shard_map/pallas_call | solution.py:570
  123.1 2.7 %select_convert_fusion = (f32[512,512]{1,0:T(8,128)}, f32[512,512]{1,0:T(8,128)}) fusion(bf16[512,512]{1,0:T(8,128)(2,1)} %collective-permute-done.14, pred[]{:T(512)S(6)} %eq.6, bf16[8,64,512]{2,1,0:T(8,128)(2,1)} %all_to_all.23), kind=kLoop, calls=%fused_computation | loop fusion | flops 1048576 | bytes 3145729 | tf_op jit(solution)/shard_map/convert_element_type | solution.py:885
  (54 shorter events, 0.3 us)
Async XLA Ops:
  0.6 6.0 %collective-permute-start = (bf16[128,512]{1,0:T(8,128)(2,1)}, bf16[128,512]{1,0:T(8,128)(2,1)S(1)}, u32[]{:S(2)}, u32[]{:S(2)}) collective-permute-start(bf16[128,512]{1,0:T(8,128)(2,1)} %grid_ref.3), channel_id=1, source_target_pairs={{0,1},{1,0},{2,3},{3,2},{4,5},{5,4},{6,7},{7,6},{8,9},{9,8},{10,11... | collective-permute-start | bytes 393224 | tf_op jit(solution)/shard_map/ppermute | solution.py:629
  1.2 5.5 %collective-permute-start.1 = (bf16[128,512]{1,0:T(8,128)(2,1)}, bf16[128,512]{1,0:T(8,128)(2,1)S(1)}, u32[]{:S(2)}, u32[]{:S(2)}) collective-permute-start(bf16[128,512]{1,0:T(8,128)(2,1)} %grid_ref.3), channel_id=1, source_target_pairs={{1,2},{2,1},{3,4},{4,3},{5,6},{6,5},{7,8},{8,7},{9,10},{10,9},{11,... | collective-permute-start | bytes 393224 | tf_op jit(solution)/shard_map/ppermute | solution.py:628
  1.9 0.7 copy-start.20
  1.9 0.7 copy-start.18
  1.9 0.7 copy-start.19
  1.9 0.7 copy-start.23
  2.6 1.2 copy-start.6
  3.8 1.0 copy-start.13
  4.8 0.9 copy-start.14
  5.8 0.9 copy-start.16
  8.3 5.0 %collective-permute-start.2 = (bf16[200,512]{1,0:T(8,128)(2,1)S(1)}, bf16[200,512]{1,0:T(8,128)(2,1)S(1)}, u32[]{:S(2)}, u32[]{:S(2)}) collective-permute-start(bf16[200,512]{1,0:T(8,128)(2,1)S(1)} %get-tuple-element.60), channel_id=1, source_target_pairs={{0,1},{1,0},{2,3},{3,2},{4,5},{5,4},{6,7},{7,6},{8,9},{9,8},{10,11... | collective-permute-start | bytes 614408 | tf_op jit(solution)/shard_map/ppermute | solution.py:676
  13.5 5.5 %collective-permute-start.3 = (bf16[72,512]{1,0:T(8,128)(2,1)S(1)}, bf16[72,512]{1,0:T(8,128)(2,1)S(1)}, u32[]{:S(2)}, u32[]{:S(2)}) collective-permute-start(bf16[72,512]{1,0:T(8,128)(2,1)S(1)} %shard_map.185.mine_ref), channel_id=1, source_target_pairs={{2,0},{18,16},{0,18},{16,2},{3,1},{19,17},{1,19},{17,3},{6,4},{22,... | collective-permute-start | bytes 221192 | tf_op jit(solution)/shard_map/ppermute | solution.py:684
  16.9 2.1 %collective-permute-start.4 = (bf16[72,512]{1,0:T(8,128)(2,1)S(1)}, bf16[72,512]{1,0:T(8,128)(2,1)S(1)}, u32[]{:S(2)}, u32[]{:S(2)}) collective-permute-start(bf16[72,512]{1,0:T(8,128)(2,1)S(1)} %shard_map.185.mine_ref), channel_id=1, source_target_pairs={{2,18},{18,2},{3,19},{19,3},{6,22},{22,6},{7,23},{23,7},{10,26},{2... | collective-permute-start | bytes 221192 | tf_op jit(solution)/shard_map/ppermute | solution.py:685
  19.1 18.2 %copy-start.17 = (bf16[128,512]{1,0:T(8,128)(2,1)S(1)}, bf16[128,512]{1,0:T(8,128)(2,1)}, u32[]{:S(2)}) copy-start(bf16[128,512]{1,0:T(8,128)(2,1)} %cot_ref.1) | copy-start | bytes 393220
  36.6 4.3 %collective-permute-start.5 = (bf16[4,528,128]{2,1,0:T(8,128)(2,1)S(1)}, bf16[4,528,128]{2,1,0:T(8,128)(2,1)S(1)}, u32[]{:S(2)}, u32[]{:S(2)}) collective-permute-start(bf16[4,528,128]{2,1,0:T(8,128)(2,1)S(1)} %bitcast.13), channel_id=1, source_target_pairs={{0,1},{1,0},{2,3},{3,2},{4,5},{5,4},{6,7},{7,6},{8,9},{9,8},{10,11... | collective-permute-start | bytes 1622024 | tf_op jit(solution)/shard_map/ppermute | solution.py:718
  36.6 4.3 %collective-permute-start.6 = (bf16[136,512]{1,0:T(8,128)(2,1)S(1)}, bf16[136,512]{1,0:T(8,128)(2,1)S(1)}, u32[]{:S(2)}, u32[]{:S(2)}) collective-permute-start(bf16[136,512]{1,0:T(8,128)(2,1)S(1)} %get-tuple-element.65.farpkt_ref), channel_id=1, source_target_pairs={{1,2},{2,1},{3,4},{4,3},{5,6},{6,5},{7,8},{8,7},{9,10},{10,9},{11,... | collective-permute-start | bytes 417800 | tf_op jit(solution)/shard_map/ppermute | solution.py:677
  37.3 0.7 copy-start.22
  37.3 0.7 copy-start.21
  38.0 1.8 %copy-start = (bf16[512,512]{1,0:T(8,128)(2,1)S(1)}, bf16[512,512]{1,0:T(8,128)(2,1)}, u32[]{:S(2)}) copy-start(bf16[512,512]{1,0:T(8,128)(2,1)} %middle_weight_ref.5) | copy-start | bytes 1572868
  38.0 3.0 %copy-start.8 = (bf16[512,512]{1,0:T(8,128)(2,1)S(1)}, bf16[512,512]{1,0:T(8,128)(2,1)}, u32[]{:S(2)}) copy-start(bf16[512,512]{1,0:T(8,128)(2,1)} %decode_weight_ref.1) | copy-start | bytes 1572868
  39.8 1.1 copy-start.1
  39.9 1.2 copy-start.7
  44.3 35.9 %copy-start.2 = (bf16[512,512]{1,0:T(8,128)(2,1)}, bf16[512,512]{1,0:T(8,128)(2,1)S(1)}, u32[]{:S(2)}) copy-start(bf16[512,512]{1,0:T(8,128)(2,1)S(1)} %get-tuple-element.73.summit_in_ref) | copy-start | bytes 1572868
  44.3 0.7 collective-permute-start.7
  45.3 9.2 %collective-permute-start.8 = (bf16[192,512]{1,0:T(8,128)(2,1)S(1)}, bf16[192,512]{1,0:T(8,128)(2,1)S(1)}, u32[]{:S(2)}, u32[]{:S(2)}) collective-permute-start(bf16[192,512]{1,0:T(8,128)(2,1)S(1)} %get-tuple-element.79), channel_id=1, source_target_pairs={{0,1},{1,0},{2,3},{3,2},{4,5},{5,4},{6,7},{7,6},{8,9},{9,8},{10,11... | collective-permute-start | bytes 589832 | tf_op jit(solution)/shard_map/ppermute | solution.py:810
  54.5 8.0 %collective-permute-start.9 = (bf16[64,512]{1,0:T(8,128)(2,1)S(1)}, bf16[64,512]{1,0:T(8,128)(2,1)S(1)}, u32[]{:S(2)}, u32[]{:S(2)}) collective-permute-start(bf16[64,512]{1,0:T(8,128)(2,1)S(1)} %shard_map.191.mine_ref), channel_id=1, source_target_pairs={{2,0},{18,16},{0,18},{16,2},{3,1},{19,17},{1,19},{17,3},{6,4},{22,... | collective-permute-start | bytes 196616 | tf_op jit(solution)/shard_map/ppermute | solution.py:812
  60.5 1.9 %collective-permute-start.10 = (bf16[64,512]{1,0:T(8,128)(2,1)S(1)}, bf16[64,512]{1,0:T(8,128)(2,1)S(1)}, u32[]{:S(2)}, u32[]{:S(2)}) collective-permute-start(bf16[64,512]{1,0:T(8,128)(2,1)S(1)} %shard_map.191.mine_ref), channel_id=1, source_target_pairs={{2,18},{18,2},{3,19},{19,3},{6,22},{22,6},{7,23},{23,7},{10,26},{2... | collective-permute-start | bytes 196616 | tf_op jit(solution)/shard_map/ppermute | solution.py:813
  79.7 0.9 copy-start.15
  79.7 2.7 %collective-permute-start.11 = (bf16[4,128,512]{2,1,0:T(8,128)(2,1)S(1)}, bf16[4,128,512]{2,1,0:T(8,128)(2,1)S(1)}, u32[]{:S(2)}, u32[]{:S(2)}) collective-permute-start(bf16[4,128,512]{2,1,0:T(8,128)(2,1)S(1)} %bitcast.15), channel_id=1, source_target_pairs={{0,1},{1,0},{2,3},{3,2},{4,5},{5,4},{6,7},{7,6},{8,9},{9,8},{10,11... | collective-permute-start | bytes 1572872 | tf_op jit(solution)/shard_map/ppermute | solution.py:830
  85.0 2.1 %copy-start.4 = (bf16[2,1,512,512]{3,2,1,0:T(8,128)(2,1)}, bf16[2,1,512,512]{3,2,1,0:T(8,128)(2,1)S(1)}, u32[]{:S(2)}) copy-start(bf16[2,1,512,512]{3,2,1,0:T(8,128)(2,1)S(1)} %get-tuple-element.92.grad_ref) | copy-start | bytes 3145732
  85.0 2.1 %copy-start.9 = (bf16[512,512]{1,0:T(8,128)(2,1)}, bf16[512,512]{1,0:T(8,128)(2,1)S(1)}, u32[]{:S(2)}) copy-start(bf16[512,512]{1,0:T(8,128)(2,1)S(1)} %get-tuple-element.94.top_ref) | copy-start | bytes 1572868
  85.0 2.1 %copy-start.11 = (bf16[512,512]{1,0:T(8,128)(2,1)}, bf16[512,512]{1,0:T(8,128)(2,1)S(1)}, u32[]{:S(2)}) copy-start(bf16[512,512]{1,0:T(8,128)(2,1)S(1)} %get-tuple-element.93.top_back_ref) | copy-start | bytes 1572868
  85.0 2.0 %collective-permute-start.12 = (bf16[512,512]{1,0:T(8,128)(2,1)S(1)}, bf16[512,512]{1,0:T(8,128)(2,1)S(1)}, u32[]{:S(2)}, u32[]{:S(2)}) collective-permute-start(bf16[512,512]{1,0:T(8,128)(2,1)S(1)} %get-tuple-element.91), channel_id=1, source_target_pairs={{0,1},{1,0},{2,3},{3,2},{4,5},{5,4},{6,7},{7,6},{8,9},{9,8},{10,11... | collective-permute-start | bytes 1572872 | tf_op jit(solution)/shard_map/ppermute | solution.py:863
  99.7 5.9 %collective-permute-start.13 = (bf16[64,512]{1,0:T(8,128)(2,1)S(1)}, bf16[64,512]{1,0:T(8,128)(2,1)S(1)}, u32[]{:S(2)}, u32[]{:S(2)}) collective-permute-start(bf16[64,512]{1,0:T(8,128)(2,1)S(1)} %shard_map.196.mine_ref), channel_id=1, source_target_pairs={{0,16},{16,0},{1,17},{17,1},{2,18},{18,2},{3,19},{19,3},{4,20},{20... | collective-permute-start | bytes 196616 | tf_op jit(solution)/shard_map/ppermute | solution.py:874
  116.8 6.3 %collective-permute-start.14 = (bf16[512,512]{1,0:T(8,128)(2,1)}, bf16[512,512]{1,0:T(8,128)(2,1)}, u32[]{:S(2)}, u32[]{:S(2)}) collective-permute-start(bf16[512,512]{1,0:T(8,128)(2,1)} %bitcast.10), channel_id=1, source_target_pairs={{0,1},{1,0},{2,3},{3,2},{4,5},{5,4},{6,7},{7,6},{8,9},{9,8},{10,11... | collective-permute-start | bytes 1572872 | tf_op jit(solution)/shard_map/ppermute | solution.py:877
  116.8 1.2 copy-start.5
  118.0 1.0 copy-start.12
  119.9 1.7 %copy-start.3 = (bf16[512,512]{1,0:T(8,128)(2,1)S(1)}, bf16[512,512]{1,0:T(8,128)(2,1)}, u32[]{:S(2)}) copy-start(bf16[512,512]{1,0:T(8,128)(2,1)} %copy-done.2) | copy-start | bytes 1572868
  119.9 1.7 %copy-start.10 = (bf16[512,512]{1,0:T(8,128)(2,1)S(1)}, bf16[512,512]{1,0:T(8,128)(2,1)}, u32[]{:S(2)}) copy-start(bf16[512,512]{1,0:T(8,128)(2,1)} %copy-done.9) | copy-start | bytes 1572868
